TPU v7x, 32 devices: a whole 2x2x4 slice. The times are simulated.
32 devices in a mesh: dp: 4 (over y, x), fsdp: 8 (over z, core).
Axes of the slice: x: 2, y: 2, z: 4, core: 2. Of those that a mesh axis runs over, the one named last changes fastest.
Arguments:
- tokens: bfloat16 [32, 1536, 768], P(('dp', 'fsdp')), may hold values from -6 to 6
- cotangent: bfloat16 [32, 1536, 768], P(('dp', 'fsdp')), may hold values from -6 to 6
- lengths: int32 [32, 6], P(('dp', 'fsdp')), may hold values from 0 to 1374, as said below
- step: int32 [1], replicated, may hold values from 2 to 20
- weight_qkv: float32 [768, 2304], P(('dp', 'fsdp')), may hold values from -0.21875 to 0.21875
- weight_proj: float32 [768, 768], P(('dp', 'fsdp')), may hold values from -1.5 to 1.5
- weight_fc1: float32 [768, 3072], P(('dp', 'fsdp')), may hold values from -0.21875 to 0.21875
- weight_fc2: float32 [3072, 768], P(('dp', 'fsdp')), may hold values from -0.109375 to 0.109375
- vectors: float32 [768, 14], P(('dp', 'fsdp'))
- first_qkv: float32 [768, 2304], P(('dp', 'fsdp')), may hold values from -0.00061035156 to 0.00061035156
- second_qkv: float32 [768, 2304], P(('dp', 'fsdp')), may hold values from 5.642831e-10 to 8.464247e-09
- first_proj: float32 [768, 768], P(('dp', 'fsdp')), may hold values from -0.00061035156 to 0.00061035156
- second_proj: float32 [768, 768], P(('dp', 'fsdp')), may hold values from 5.642831e-10 to 8.464247e-09
- first_fc1: float32 [768, 3072], P(('dp', 'fsdp')), may hold values from -0.00061035156 to 0.00061035156
- second_fc1: float32 [768, 3072], P(('dp', 'fsdp')), may hold values from 5.642831e-10 to 8.464247e-09
- first_fc2: float32 [3072, 768], P(('dp', 'fsdp')), may hold values from -0.00061035156 to 0.00061035156
- second_fc2: float32 [3072, 768], P(('dp', 'fsdp')), may hold values from 5.642831e-10 to 8.464247e-09
- first_vectors: float32 [768, 14], P(('dp', 'fsdp')), may hold values from -0.001953125 to 0.001953125
- second_vectors: float32 [768, 14], P(('dp', 'fsdp')), may hold values from 5.6428315e-09 to 8.464247e-08
Outputs:
- out_tokens: bfloat16 [32, 1536, 768], P(('dp', 'fsdp'))
- grad_tokens: bfloat16 [32, 1536, 768], P(('dp', 'fsdp'))
- grad_norm: float32 [1], replicated
- new_qkv: float32 [768, 2304], P(('dp', 'fsdp'))
- new_proj: float32 [768, 768], P(('dp', 'fsdp'))
- new_fc1: float32 [768, 3072], P(('dp', 'fsdp'))
- new_fc2: float32 [3072, 768], P(('dp', 'fsdp'))
- new_vectors: float32 [768, 14], P(('dp', 'fsdp'))
- new_first_qkv: float32 [768, 2304], P(('dp', 'fsdp'))
- new_second_qkv: float32 [768, 2304], P(('dp', 'fsdp'))
- new_first_proj: float32 [768, 768], P(('dp', 'fsdp'))
- new_second_proj: float32 [768, 768], P(('dp', 'fsdp'))
- new_first_fc1: float32 [768, 3072], P(('dp', 'fsdp'))
- new_second_fc1: float32 [768, 3072], P(('dp', 'fsdp'))
- new_first_fc2: float32 [3072, 768], P(('dp', 'fsdp'))
- new_second_fc2: float32 [3072, 768], P(('dp', 'fsdp'))
- new_first_vectors: float32 [768, 14], P(('dp', 'fsdp'))
- new_second_vectors: float32 [768, 14], P(('dp', 'fsdp'))
Inputs may be any that keep to these rules, and one draw needn't show every extreme that they name: `lengths`: each row holds either one sequence of 1374 tokens in its first slot or 5 sequences of 261 tokens; other slots are 0; the positions after a row's sequences form one more segment. Both kinds of rows occur.
All inputs are finite; a program needn't handle non-finite values.
Results may differ from a plain program's by a relative error of at most 0.01.
The roundings to bfloat16 on the way count: a program that leaves them out, or rounds other values in their place, can miss the bound.
Values may be sent and summed in bfloat16 or wider, within the bound.
No kernel may reach another device: no remote copies, remote signals or barrier semaphores. Data moves between devices by JAX's collectives and lax.ppermute only.
A program may use at most 192 MiB of HBM per device.

v0:
```python
import math

import jax
import jax.numpy as jnp
from jax import lax
from jax.sharding import PartitionSpec as P

D = 768
HEADS = 12
HEAD_DIM = 64
FF = 3072


NORM_EPS = 1e-06
BETA_ONE = 0.9
BETA_TWO = 0.999
ADAM_EPS = 1e-08
CLIP_LIMIT = 3.0


def layer_norm(values, gain, shift):
    center = values - jnp.mean(values, axis=-1, keepdims=True)
    spread = jnp.mean(center * center, axis=-1, keepdims=True)
    return center * lax.rsqrt(spread + NORM_EPS) * gain + shift


def exact_gelu(values):
    return jax.nn.gelu(values, approximate=False)


def segment_ids(line, count):
    ends = jnp.cumsum(line, dtype=jnp.int32)
    places = jnp.arange(count, dtype=jnp.int32)
    return jnp.sum((places[:, None] >= ends[None, :]).astype(jnp.int32), axis=1)


def unpack(vec):
    wide = FF // D
    fc1_bias = vec[:, 8 : 8 + wide].T.reshape(FF)
    return (
        vec[:, 0],
        vec[:, 1],
        vec[:, 2],
        vec[:, 3],
        vec[:, 4],
        vec[:, 5],
        vec[:, 6],
        vec[:, 7],
        fc1_bias,
        vec[:, 8 + wide],
        vec[:, 9 + wide],
    )


def masked_scores(query, keys, row_ids):
    scores = jnp.einsum("dq,dk->qk", query, keys, preferred_element_type=jnp.float32) * query.shape[
        0
    ] ** (-0.5)
    same = row_ids[:, None] == row_ids[None, :]
    return jnp.where(same, scores, -1000000000.0)


def head_forward(item):
    qkv_head, row_ids = item
    scores = masked_scores(qkv_head[0], qkv_head[1], row_ids)
    top = jnp.max(scores, axis=1, keepdims=True)
    total = top + jnp.log(jnp.sum(jnp.exp(scores - top), axis=1, keepdims=True))
    probs = jnp.exp(scores - total).astype(jnp.bfloat16)
    mixed = jnp.einsum("dk,qk->dq", qkv_head[2], probs, preferred_element_type=jnp.float32)
    return (mixed.astype(jnp.bfloat16), total[:, 0])


def head_backward(item):
    qkv_head, grad_head, total, row_ids = item
    query, keys, values = (qkv_head[0], qkv_head[1], qkv_head[2])
    scale = query.shape[0] ** (-0.5)
    probs = jnp.exp(masked_scores(query, keys, row_ids) - total[:, None])
    grad_values = jnp.einsum(
        "dq,qk->dk", grad_head, probs.astype(jnp.bfloat16), preferred_element_type=jnp.float32
    )
    grad_probs = jnp.einsum("dq,dk->qk", grad_head, values, preferred_element_type=jnp.float32)
    inner = jnp.sum(probs * grad_probs, axis=1, keepdims=True)
    grad_scores = (probs * (grad_probs - inner)).astype(jnp.bfloat16)
    grad_query = (
        jnp.einsum("qk,dk->dq", grad_scores, keys, preferred_element_type=jnp.float32) * scale
    )
    grad_keys = (
        jnp.einsum("qk,dq->dk", grad_scores, query, preferred_element_type=jnp.float32) * scale
    )
    return jnp.stack([grad_query, grad_keys, grad_values]).astype(jnp.bfloat16)


def adam_update(weight, grad, first, second, rate, decay, fix_one, fix_two):
    first = BETA_ONE * first + (1.0 - BETA_ONE) * grad
    second = BETA_TWO * second + (1.0 - BETA_TWO) * grad * grad
    stride = first / fix_one / (jnp.sqrt(second / fix_two) + ADAM_EPS)
    return (weight - rate * (stride + decay * weight), first, second)


def local(
    tokens,
    cotangent,
    lengths,
    step,
    weight_qkv,
    weight_proj,
    weight_fc1,
    weight_fc2,
    vectors,
    first_qkv,
    second_qkv,
    first_proj,
    second_proj,
    first_fc1,
    second_fc1,
    first_fc2,
    second_fc2,
    first_vectors,
    second_vectors,
):
    rows_dev, row, _ = tokens.shape
    count = rows_dev * row
    low_shards = (
        weight_qkv.astype(jnp.bfloat16),
        weight_proj.astype(jnp.bfloat16),
        weight_fc1.astype(jnp.bfloat16),
        weight_fc2.astype(jnp.bfloat16),
        vectors.astype(jnp.bfloat16),
    )
    full = (
        lax.all_gather(low_shards[0], ("dp", "fsdp"), axis=0, tiled=True),
        lax.all_gather(low_shards[1], ("dp", "fsdp"), axis=0, tiled=True),
        lax.all_gather(low_shards[2], ("dp", "fsdp"), axis=0, tiled=True),
        lax.all_gather(low_shards[3], ("dp", "fsdp"), axis=0, tiled=True),
        lax.all_gather(low_shards[4], ("dp", "fsdp"), axis=0, tiled=True),
    )
    mat_qkv, mat_proj, mat_fc1, mat_fc2 = (full[0], full[1], full[2], full[3])
    (
        gain_one,
        shift_one,
        bias_q,
        bias_v,
        bias_o,
        scale_one,
        gain_two,
        shift_two,
        bias_up,
        bias_down,
        scale_two,
    ) = unpack(full[4].astype(jnp.float32))
    ids = jax.vmap(lambda line: segment_ids(line, row))(lengths)
    ids_heads = jnp.repeat(ids, HEADS, axis=0)
    inputs = tokens.reshape(count, D).astype(jnp.float32)
    normed_f, norm_pull_one = jax.vjp(layer_norm, inputs, gain_one, shift_one)
    normed = normed_f.astype(jnp.bfloat16)
    bias = jnp.concatenate([bias_q, jnp.zeros_like(bias_q), bias_v])
    qkv = (jnp.dot(normed, mat_qkv, preferred_element_type=jnp.float32) + bias).astype(jnp.bfloat16)
    qkv_heads = qkv.reshape(rows_dev, row, 3, HEADS, HEAD_DIM).transpose(0, 3, 2, 4, 1)
    qkv_heads = qkv_heads.reshape(rows_dev * HEADS, 3, HEAD_DIM, row)
    mixed_heads, totals = lax.map(head_forward, (qkv_heads, ids_heads))
    mixed = (
        mixed_heads.reshape(rows_dev, HEADS, HEAD_DIM, row).transpose(0, 3, 1, 2).reshape(count, D)
    )
    branch = jnp.dot(mixed, mat_proj, preferred_element_type=jnp.float32) + bias_o
    middle = inputs + scale_one * branch
    normed_two_f, norm_pull_two = jax.vjp(layer_norm, middle, gain_two, shift_two)
    normed_two = normed_two_f.astype(jnp.bfloat16)
    inner = jnp.dot(normed_two, mat_fc1, preferred_element_type=jnp.float32) + bias_up
    active_f, gelu_pull = jax.vjp(exact_gelu, inner)
    active = active_f.astype(jnp.bfloat16)
    out_branch = jnp.dot(active, mat_fc2, preferred_element_type=jnp.float32) + bias_down
    result = middle + scale_two * out_branch
    out_tokens = result.astype(jnp.bfloat16).reshape(rows_dev, row, D)
    again = (
        lax.all_gather(low_shards[0], ("dp", "fsdp"), axis=0, tiled=True),
        lax.all_gather(low_shards[1], ("dp", "fsdp"), axis=0, tiled=True),
        lax.all_gather(low_shards[2], ("dp", "fsdp"), axis=0, tiled=True),
        lax.all_gather(low_shards[3], ("dp", "fsdp"), axis=0, tiled=True),
        lax.all_gather(low_shards[4], ("dp", "fsdp"), axis=0, tiled=True),
    )
    back_qkv, back_proj, back_fc1, back_fc2 = (again[0], again[1], again[2], again[3])
    grad_out = cotangent.reshape(count, D).astype(jnp.float32)
    grad_scale_two = jnp.sum(grad_out * out_branch, axis=0)
    grad_down = (scale_two * grad_out).astype(jnp.bfloat16)
    grad_bias_down = jnp.sum(grad_down.astype(jnp.float32), axis=0)
    grad_fc2 = jnp.einsum("nf,nd->fd", active, grad_down, preferred_element_type=jnp.float32)
    grad_active = jnp.einsum("nd,fd->nf", grad_down, back_fc2, preferred_element_type=jnp.float32)
    grad_inner = gelu_pull(grad_active)[0].astype(jnp.bfloat16)
    grad_bias_up = jnp.sum(grad_inner.astype(jnp.float32), axis=0)
    grad_fc1 = jnp.einsum("nd,nf->df", normed_two, grad_inner, preferred_element_type=jnp.float32)
    grad_normed_two = jnp.einsum(
        "nf,df->nd", grad_inner, back_fc1, preferred_element_type=jnp.float32
    )
    grad_ln_two, grad_gain_two, grad_shift_two = norm_pull_two(grad_normed_two)
    grad_middle = grad_out + grad_ln_two
    grad_scale_one = jnp.sum(grad_middle * branch, axis=0)
    grad_branch = (scale_one * grad_middle).astype(jnp.bfloat16)
    grad_bias_o = jnp.sum(grad_branch.astype(jnp.float32), axis=0)
    grad_proj = jnp.einsum("nd,ne->de", mixed, grad_branch, preferred_element_type=jnp.float32)
    grad_mixed = jnp.einsum(
        "ne,de->nd", grad_branch, back_proj, preferred_element_type=jnp.float32
    ).astype(jnp.bfloat16)
    grad_heads = grad_mixed.reshape(rows_dev, row, HEADS, HEAD_DIM).transpose(0, 2, 3, 1)
    grad_heads = grad_heads.reshape(rows_dev * HEADS, HEAD_DIM, row)
    grad_qkv_heads = lax.map(head_backward, (qkv_heads, grad_heads, totals, ids_heads))
    grad_qkv = (
        grad_qkv_heads.reshape(rows_dev, HEADS, 3, HEAD_DIM, row)
        .transpose(0, 4, 2, 1, 3)
        .reshape(count, 3 * D)
    )
    grad_qkv_sums = jnp.sum(grad_qkv.astype(jnp.float32), axis=0)
    grad_weight_qkv = jnp.einsum("nd,ne->de", normed, grad_qkv, preferred_element_type=jnp.float32)
    grad_normed = jnp.einsum("ne,de->nd", grad_qkv, back_qkv, preferred_element_type=jnp.float32)
    grad_ln_one, grad_gain_one, grad_shift_one = norm_pull_one(grad_normed)
    grad_inputs = grad_middle + grad_ln_one
    grad_tokens = grad_inputs.astype(jnp.bfloat16).reshape(rows_dev, row, D)
    grad_vectors = jnp.concatenate(
        [
            jnp.stack(
                [
                    grad_gain_one,
                    grad_shift_one,
                    grad_qkv_sums[:D],
                    grad_qkv_sums[2 * D :],
                    grad_bias_o,
                    grad_scale_one,
                    grad_gain_two,
                    grad_shift_two,
                ],
                axis=1,
            ),
            grad_bias_up.reshape(FF // D, D).T,
            jnp.stack([grad_bias_down, grad_scale_two], axis=1),
        ],
        axis=1,
    )
    owned = (
        lax.psum_scatter(grad_weight_qkv, ("dp", "fsdp"), scatter_dimension=0, tiled=True),
        lax.psum_scatter(grad_proj, ("dp", "fsdp"), scatter_dimension=0, tiled=True),
        lax.psum_scatter(grad_fc1, ("dp", "fsdp"), scatter_dimension=0, tiled=True),
        lax.psum_scatter(grad_fc2, ("dp", "fsdp"), scatter_dimension=0, tiled=True),
        lax.psum_scatter(grad_vectors, ("dp", "fsdp"), scatter_dimension=0, tiled=True),
    )
    local_squares = (
        jnp.sum(owned[0] * owned[0]) + jnp.sum(owned[1] * owned[1]) + jnp.sum(owned[2] * owned[2])
    )
    local_squares = local_squares + jnp.sum(owned[3] * owned[3]) + jnp.sum(owned[4] * owned[4])
    total_squares = lax.psum(local_squares, ("dp", "fsdp"))
    norm = jnp.sqrt(total_squares)
    factor = jnp.minimum(1.0, CLIP_LIMIT / (norm + 1e-06))
    steps_taken = step[0].astype(jnp.float32)
    fix_one = 1.0 - jnp.power(BETA_ONE, steps_taken)
    fix_two = 1.0 - jnp.power(BETA_TWO, steps_taken)
    rate_in = 2.0 / math.sqrt(D)
    new_qkv, new_first_qkv, new_second_qkv = adam_update(
        weight_qkv, factor * owned[0], first_qkv, second_qkv, rate_in, 0.04, fix_one, fix_two
    )
    new_proj, new_first_proj, new_second_proj = adam_update(
        weight_proj,
        factor * owned[1],
        first_proj,
        second_proj,
        2.0 / math.sqrt(D // 48),
        0.04,
        fix_one,
        fix_two,
    )
    new_fc1, new_first_fc1, new_second_fc1 = adam_update(
        weight_fc1, factor * owned[2], first_fc1, second_fc1, rate_in, 0.04, fix_one, fix_two
    )
    new_fc2, new_first_fc2, new_second_fc2 = adam_update(
        weight_fc2,
        factor * owned[3],
        first_fc2,
        second_fc2,
        2.0 / math.sqrt(FF),
        0.04,
        fix_one,
        fix_two,
    )
    new_vectors, new_first_vectors, new_second_vectors = adam_update(
        vectors, factor * owned[4], first_vectors, second_vectors, 1.0, 0.0, fix_one, fix_two
    )
    return (
        out_tokens,
        grad_tokens,
        norm.reshape(1),
        new_qkv,
        new_proj,
        new_fc1,
        new_fc2,
        new_vectors,
        new_first_qkv,
        new_second_qkv,
        new_first_proj,
        new_second_proj,
        new_first_fc1,
        new_second_fc1,
        new_first_fc2,
        new_second_fc2,
        new_first_vectors,
        new_second_vectors,
    )


def solution(mesh):
    return jax.shard_map(
        local,
        mesh=mesh,
        in_specs=(
            P(("dp", "fsdp"), None, None),
            P(("dp", "fsdp"), None, None),
            P(("dp", "fsdp"), None),
            P(),
            P(("dp", "fsdp"), None),
            P(("dp", "fsdp"), None),
            P(("dp", "fsdp"), None),
            P(("dp", "fsdp"), None),
            P(("dp", "fsdp"), None),
            P(("dp", "fsdp"), None),
            P(("dp", "fsdp"), None),
            P(("dp", "fsdp"), None),
            P(("dp", "fsdp"), None),
            P(("dp", "fsdp"), None),
            P(("dp", "fsdp"), None),
            P(("dp", "fsdp"), None),
            P(("dp", "fsdp"), None),
            P(("dp", "fsdp"), None),
            P(("dp", "fsdp"), None),
        ),
        out_specs=(
            P(("dp", "fsdp"), None, None),
            P(("dp", "fsdp"), None, None),
            P(),
            P(("dp", "fsdp"), None),
            P(("dp", "fsdp"), None),
            P(("dp", "fsdp"), None),
            P(("dp", "fsdp"), None),
            P(("dp", "fsdp"), None),
            P(("dp", "fsdp"), None),
            P(("dp", "fsdp"), None),
            P(("dp", "fsdp"), None),
            P(("dp", "fsdp"), None),
            P(("dp", "fsdp"), None),
            P(("dp", "fsdp"), None),
            P(("dp", "fsdp"), None),
            P(("dp", "fsdp"), None),
            P(("dp", "fsdp"), None),
            P(("dp", "fsdp"), None),
        ),
        check_vma=False,
    )
```

profile of v0, /device:TPU:0, one launch (start us, length us, event | category | flops | bytes accessed | tf_op | source)
XLA Modules:
  0.0 1296.7 jit_solution(5468467189678133736)
XLA Ops:
  14.6 43.9 %all-gather = bf16[32,24,14]{1,2,0:T(8,128)(2,1)S(1)} all-gather(bf16[1,24,14]{1,2,0:T(8,128)(2,1)S(1)} %convert_bitcast_fusion.1), channel_id=1, replica_groups=mesh['dp'=4,'fsdp'=8] {'dp','fsdp'}, dimensions={0}, use_global_device_ids=true | all-gather | bytes 22176 | tf_op jit(solution)/shard_map/all_gather | solution.py:135
  102.0 169.1 %while.22 = (s32[]{:T(128)}, bf16[12,64,1536]{2,1,0:T(8,128)(2,1)}, f32[12,1536]{1,0:T(8,128)}, bf16[12,3,64,1536]{3,2,1,0:T(8,128)(2,1)}, s32[12,1536]{1,0:T(8,128)S(1)}, /*index=5*/s32[]{:T(128)}, s32[]{:T(128)}, s32[]{}, s32[]{}) while((s32[]{:T(128)}, bf16[12,64,1536]{2,1,0:T(8,128)(2,1)}, f32[12,1536]{1,0:T(8,128)}, ...), condition=%wide.region_7.8_spmd, body=%wide.region_4.7_spmd.sunk | while | flops 622950912 | bytes 66946208 | solution.py:160
  282.3 53.9 %multiply_convert_fusion.1 = (bf16[1536,3072]{1,0:T(8,128)(2,1)}, f32[1536,3072]{1,0:T(8,128)}, f32[1536,3072]{1,0:T(8,128)}) fusion(f32[3072]{0:T(1024)S(1)} %add.235, bf16[768,3072]{1,0:T(8,128)(2,1)} %all-gather.10.cloned.1.call-done, bf16[1536,768]{0,1:T(8,128)(2,1)} %add_convert_fusion.6.clone.4), kind=kOutput, calls=%fused_computation.52 | convolution fusion | flops 7559184384 | bytes 54276096 | tf_op jit(solution)/shard_map/dot_general | solution.py:168
  336.2 24.0 %convert_reduce_fusion = (f32[3072]{0:T(1024)}, bf16[1536,3072]{1,0:T(8,128)(2,1)}) fusion(f32[1536,3072]{1,0:T(8,128)} %get-tuple-element.274, bf16[3072,768]{1,0:T(8,128)(2,1)} %all-gather.12.cloned.1.call-done, bf16[1,1536,768]{1,2,0:T(8,128)(2,1)S(1)} %copy-done.9, f32[768]{0:T(1024)S(1)} %copy-done.48, f32[1536,3072]{1,0:T(8,128)} %get-tuple-element.286, ...), kind=kOutput, calls=%fused_computation.50 | convolution fusion | flops 7331509248 | bytes 54291456 | tf_op jit(solution)/shard_map/nd,fd->nf/dot_general | solution.py:187
  360.3 13.5 %fusion.97 = (f32[768]{0:T(1024)}, f32[1536,768]{1,0:T(8,128)}) fusion(bf16[1536,3072]{1,0:T(8,128)(2,1)} %get-tuple-element.292, bf16[768,3072]{1,0:T(8,128)(2,1)} %all-gather.10.cloned.1.call-done), kind=kOutput, calls=%fused_computation.177 | convolution fusion | flops 7248935936 | bytes 18877440 | tf_op jit(solution)/shard_map/nf,df->nd/dot_general | solution.py:191
  400.0 419.5 %while.23 = (s32[]{:T(128)}, bf16[12,3,64,1536]{3,2,0,1:T(8,128)(2,1)}, bf16[12,3,64,1536]{3,2,1,0:T(8,128)(2,1)}, s32[12,1536]{1,0:T(8,128)}, f32[12,1536]{1,0:...) while((s32[]{:T(128)}, bf16[12,3,64,1536]{3,2,0,1:T(8,128)(2,1)}, ...), condition=%wide.region_14.15_spmd, body=%wide.region_12.14_spmd.sunk | while | flops 1535801856 | bytes 130612440 | solution.py:205
  417.4 11.3 multiply_convert_fusion.5
  452.6 11.2 multiply_convert_fusion.5
  487.7 11.1 multiply_convert_fusion.5
  522.6 11.1 multiply_convert_fusion.5
  592.4 11.1 multiply_convert_fusion.5
  627.2 11.1 multiply_convert_fusion.5
  697.0 11.1 multiply_convert_fusion.5
  731.9 11.1 multiply_convert_fusion.5
  766.8 11.1 multiply_convert_fusion.5
  801.6 11.1 multiply_convert_fusion.5
  819.6 11.2 fusion.60
  831.6 14.0 %fusion.83 = f32[768,3072]{1,0:T(8,128)} fusion(bf16[1536,3072]{1,0:T(8,128)(2,1)} %get-tuple-element.292, f32[1536,768]{0,1:T(8,128)} %copy-done.3, f32[768]{0:T(1024)S(1)} %copy-done.41, f32[768]{0:T(1024)S(1)} %copy-done.32, f32[1536]{0:T(1024)S(1)} %copy-done.24, f32[1536]{0:T(1024)S(1)} %copy-done.19), kind=kOutput, calls=%fused_computation.170 | convolution fusion | flops 7253655552 | bytes 23611392 | tf_op jit(solution)/shard_map/nd,nf->df/dot_general | solution.py:190
  846.3 13.5 %fusion.80 = f32[3072,768]{1,0:T(8,128)} fusion(bf16[1536,3072]{1,0:T(8,128)(2,1)} %get-tuple-element.273, bf16[1,1536,768]{1,2,0:T(8,128)(2,1)} %copy.95, f32[768]{0:T(1024)S(1)} %copy-done.49), kind=kOutput, calls=%fused_computation.169 | convolution fusion | flops 7251296256 | bytes 21236736 | tf_op jit(solution)/shard_map/nf,nd->fd/dot_general | solution.py:186
  883.4 21.5 %fusion.56 = (f32[768]{0:T(1024)S(1)}, f32[768]{0:T(1024)S(1)}, f32[768]{0:T(1024)S(1)}, bf16[1,1536,768]{1,2,0:T(8,128)(2,1)}, bf16[1,1536,768]{1,2,0:T(8,128)(2,1)}) fusion(bf16[1,1536,768]{1,2,0:T(8,128)(2,1)} %copy.95, f32[768]{0:T(1024)S(1)} %copy-done.50, f32[768]{0:T(1024)S(1)} %copy-done.49, f32[1536,768]{0,1:T(8,128)} %get-tuple-element.285, ...), kind=kOutput, calls=%fused_computation.94 | convolution fusion | flops 7278425088 | bytes 42519552 | tf_op jit(solution)/shard_map/dot_general | solution.py:171
  913.9 40.1 %all-reduce = f32[768,14]{0,1:T(8,128)S(1)} all-reduce(f32[768,14]{0,1:T(8,128)S(1)} %concatenate.15), channel_id=6, replica_groups=mesh['dp'=4,'fsdp'=8] {'dp','fsdp'}, use_global_device_ids=true, to_apply=%region_35.36.clone | all-reduce | flops 10752 | bytes 86016
  959.1 132.2 %reduce-scatter.10.cloned.1.call-done = f32[24,3072]{1,0:T(8,128)} async-done(((f32[768,3072]{1,0:T(8,128)}), f32[24,3072]{1,0:T(8,128)}) %reduce-scatter.10.cloned.1.call-update) | async-done | bytes 294928 | tf_op jit(solution)/shard_map/reduce_scatter | solution.py:240
  1093.7 139.2 %reduce-scatter.12.cloned.1.call-done = f32[96,768]{1,0:T(8,128)} async-done(((f32[3072,768]{1,0:T(8,128)}), f32[96,768]{1,0:T(8,128)}) %reduce-scatter.12.cloned.1.call-update) | async-done | bytes 294928 | tf_op jit(solution)/shard_map/reduce_scatter | solution.py:241
  1238.3 39.7 %psum.7 = f32[]{:T(128)} all-reduce(f32[]{:T(128)S(6)} %add.249), channel_id=1, replica_groups=mesh['dp'=4,'fsdp'=8] {'dp','fsdp'}, use_global_device_ids=true, to_apply=%region_37.38 | all-reduce | flops 1 | bytes 8 | tf_op jit(solution)/shard_map/psum | solution.py:248
  (466 shorter events, 616.5 us)
Async XLA Ops:
  7.2 67.6 %all-gather.6.cloned.1.call-start = ((), (), s32[]{:S(2)}) async-start(), calls=%async_computation.4 | async-start | bytes 3649536 | tf_op jit(solution)/shard_map/all_gather | solution.py:131
  8.9 262.3 %all-gather.8.cloned.1.call-start = ((), (), s32[]{:S(2)}) async-start(), calls=%async_computation.5 | async-start | bytes 1216512 | tf_op jit(solution)/shard_map/all_gather | solution.py:132
  10.4 271.9 %all-gather.10.cloned.1.call-start = ((), (), s32[]{:S(2)}) async-start(), calls=%async_computation.6 | async-start | bytes 4866048 | tf_op jit(solution)/shard_map/all_gather | solution.py:133
  12.2 324.1 %all-gather.12.cloned.1.call-start = ((), (), s32[]{:S(2)}) async-start(), calls=%async_computation.7 | async-start | bytes 4866048 | tf_op jit(solution)/shard_map/all_gather | solution.py:134
  13.9 940.8 %reduce-scatter.8.cloned.1.call-start = ((), (), s32[]{:S(2)}) async-start(), calls=%async_computation.9 | async-start | bytes 2433024 | tf_op jit(solution)/shard_map/reduce_scatter | solution.py:239
  59.6 211.5 %copy-start.42 = (f32[768]{0:T(1024)}, f32[768]{0:T(1024)S(1)}, u32[]{:S(2)}) copy-start(f32[768]{0:T(1024)S(1)} %get-tuple-element.231) | copy-start | bytes 9220
  59.6 211.5 %copy-start.51 = (f32[768]{0:T(1024)}, f32[768]{0:T(1024)S(1)}, u32[]{:S(2)}) copy-start(f32[768]{0:T(1024)S(1)} %get-tuple-element.226) | copy-start | bytes 9220
  59.7 219.9 %copy-start.30 = (f32[768]{0:T(1024)}, f32[768]{0:T(1024)S(1)}, u32[]{:S(2)}) copy-start(f32[768]{0:T(1024)S(1)} %get-tuple-element.225) | copy-start | bytes 9220
  59.7 219.9 %copy-start.40 = (f32[768]{0:T(1024)}, f32[768]{0:T(1024)S(1)}, u32[]{:S(2)}) copy-start(f32[768]{0:T(1024)S(1)} %get-tuple-element.224) | copy-start | bytes 9220
  66.8 204.3 %copy-start.4 = (bf16[1,1536,768]{1,2,0:T(8,128)(2,1)}, bf16[1,1536,768]{1,2,0:T(8,128)(2,1)S(1)}, u32[]{:S(2)}) copy-start(bf16[1,1536,768]{1,2,0:T(8,128)(2,1)S(1)} %copy.89) | copy-start | bytes 7077892
  394.9 561.3 %reduce-scatter.6.cloned.1.call-start = ((), (), s32[]{:S(2)}) async-start(), calls=%async_computation.8 | async-start | bytes 7299072 | tf_op jit(solution)/shard_map/reduce_scatter | solution.py:238
  400.0 419.6 %copy-start.5 = (bf16[1,1536,768]{1,2,0:T(8,128)(2,1)S(1)}, bf16[1,1536,768]{1,2,0:T(8,128)(2,1)}, u32[]{:S(2)}) copy-start(bf16[1,1536,768]{1,2,0:T(8,128)(2,1)} %copy-done.4) | copy-start | bytes 7077892
  400.0 419.6 %copy-start.21 = (f32[1536]{0:T(1024)S(1)}, f32[1536]{0:T(1024)}, u32[]{:S(2)}) copy-start(f32[1536]{0:T(1024)} %copy-done.20) | copy-start | bytes 18436
  400.0 419.6 %copy-start.34 = (f32[768]{0:T(1024)S(1)}, f32[768]{0:T(1024)}, u32[]{:S(2)}) copy-start(f32[768]{0:T(1024)} %copy-done.33) | copy-start | bytes 9220
  400.0 419.6 %copy-start.39 = (f32[1536]{0:T(1024)S(1)}, f32[1536]{0:T(1024)}, u32[]{:S(2)}) copy-start(f32[1536]{0:T(1024)} %copy-done.38) | copy-start | bytes 18436
  400.0 419.6 %copy-start.54 = (f32[768]{0:T(1024)S(1)}, f32[768]{0:T(1024)}, u32[]{:S(2)}) copy-start(f32[768]{0:T(1024)} %copy-done.53) | copy-start | bytes 9220
  830.9 260.4 %reduce-scatter.10.cloned.1.call-start = ((), (), s32[]{:S(2)}) async-start(), calls=%async_computation.10 | async-start | bytes 9732096 | tf_op jit(solution)/shard_map/reduce_scatter | solution.py:240
  845.6 387.2 %reduce-scatter.12.cloned.1.call-start = ((), (), s32[]{:S(2)}) async-start(), calls=%async_computation.11 | async-start | bytes 9732096 | tf_op jit(solution)/shard_map/reduce_scatter | solution.py:241
  909.2 326.6 %copy-start.10 = (bf16[1,1536,768]{1,2,0:T(8,128)(2,1)S(1)}, bf16[1,1536,768]{1,2,0:T(8,128)(2,1)}, u32[]{:S(2)}) copy-start(bf16[1,1536,768]{1,2,0:T(8,128)(2,1)} %get-tuple-element.281) | copy-start | bytes 7077892
  913.5 365.3 %copy-start.37 = (f32[24,14]{0,1:T(8,128)S(1)}, f32[24,14]{0,1:T(8,128)}, u32[]{:S(2)}) copy-start(f32[24,14]{0,1:T(8,128)} %param.31) | copy-start | bytes 4036
  913.5 365.3 %copy-start.47 = (f32[24,14]{0,1:T(8,128)S(1)}, f32[24,14]{0,1:T(8,128)}, u32[]{:S(2)}) copy-start(f32[24,14]{0,1:T(8,128)} %param.41) | copy-start | bytes 4036
  913.5 370.6 %copy-start.12 = (f32[24,3072]{1,0:T(8,128)S(1)}, f32[24,3072]{1,0:T(8,128)}, u32[]{:S(2)}) copy-start(f32[24,3072]{1,0:T(8,128)} %param.29) | copy-start | bytes 884740
  959.1 327.1 %copy-start.13 = (f32[96,768]{1,0:T(8,128)S(1)}, f32[96,768]{1,0:T(8,128)}, u32[]{:S(2)}) copy-start(f32[96,768]{1,0:T(8,128)} %param.30) | copy-start | bytes 884740
  1091.3 192.8 %copy-start.14 = (f32[24,3072]{1,0:T(8,128)S(1)}, f32[24,3072]{1,0:T(8,128)}, u32[]{:S(2)}) copy-start(f32[24,3072]{1,0:T(8,128)} %reduce-scatter.10.cloned.1.call-done) | copy-start | bytes 884740
  (78 other events, 485.4 us)
Sparse Core Ops, SparseCore 0:
  11.6 63.1 all-gather.5
  78.4 53.0 all-gather.7
  135.1 62.6 all-gather.9
  201.2 62.3 all-gather.11
  395.0 98.5 reduce-scatter.7
  831.0 119.4 reduce-scatter.5
  956.4 134.8 reduce-scatter.9
  1098.2 134.5 reduce-scatter.11
where the time goes:
time: 1310 us; the launch traced here: 1300 us
  matrix products  540 us (41%)
  waiting for transfers between devices  278 us (21%)
  other arithmetic  206 us (16%)
  local copies, waits for them, and re-layouts  127 us (10%)
  blocking collectives  124 us (9%)
  between operations  21.1 us (2%)
    reduce_scatter x1, waiting for transfers between devices, local(): lax.psum_scatter(grad_fc2, ('dp', 'fsdp'), scatter_dimension=0, tiled=True)  139 us
    convert_element_type x12, other arithmetic, head_backward(): grad_scores = (probs * (grad_probs - inner)).astype(jnp.bfloat16)  133 us
    reduce_scatter x1, waiting for transfers between devices, local(): lax.psum_scatter(grad_fc1, ('dp', 'fsdp'), scatter_dimension=0, tiled=True)  132 us
    dot_general x24, matrix products, masked_scores(): jnp.einsum('dq,dk->qk', query, keys, preferred_element_type=jnp.float32)  101 us
    dot_general x12, matrix products, head_backward(): jnp.einsum('dq,dk->qk', grad_head, values, preferred_element_type=jnp.flo...  73 us
    dot_general x12, matrix products, head_forward(): jnp.einsum('dk,qk->dq', qkv_head[2], probs, preferred_element_type=jnp.fl...  72.9 us
    dot_general x1, matrix products, local(): jnp.dot(normed_two, mat_fc1, preferred_element_type=jnp.float32) + bias_up  53.9 us
    dot_general x12, matrix products, head_backward(): jnp.einsum('qk,dq->dk', grad_scores, query, preferred_element_type=jnp.fl...  49.4 us
  transfers between devices with their start and end apart: 8, of which 3 were waited for; matrix products, arithmetic and copies ran while one was open for 58% of the time, Pallas kernels for 0%

commit v1 on v0

--- a/solution.py
+++ b/solution.py
@@ -3,7 +3,12 @@
 import jax
 import jax.numpy as jnp
 from jax import lax
+from jax.experimental import pallas as pl
+from jax.experimental.pallas import tpu as pltpu
 from jax.sharding import PartitionSpec as P
+
+bf=jnp.bfloat16
+f32=jnp.float32
 
 D = 768
 HEADS = 12
@@ -52,42 +57,117 @@
     )
 
 
-def masked_scores(query, keys, row_ids):
-    scores = jnp.einsum("dq,dk->qk", query, keys, preferred_element_type=jnp.float32) * query.shape[
-        0
-    ] ** (-0.5)
-    same = row_ids[:, None] == row_ids[None, :]
-    return jnp.where(same, scores, -1000000000.0)
-
-
-def head_forward(item):
-    qkv_head, row_ids = item
-    scores = masked_scores(qkv_head[0], qkv_head[1], row_ids)
-    top = jnp.max(scores, axis=1, keepdims=True)
-    total = top + jnp.log(jnp.sum(jnp.exp(scores - top), axis=1, keepdims=True))
-    probs = jnp.exp(scores - total).astype(jnp.bfloat16)
-    mixed = jnp.einsum("dk,qk->dq", qkv_head[2], probs, preferred_element_type=jnp.float32)
-    return (mixed.astype(jnp.bfloat16), total[:, 0])
-
-
-def head_backward(item):
-    qkv_head, grad_head, total, row_ids = item
-    query, keys, values = (qkv_head[0], qkv_head[1], qkv_head[2])
-    scale = query.shape[0] ** (-0.5)
-    probs = jnp.exp(masked_scores(query, keys, row_ids) - total[:, None])
-    grad_values = jnp.einsum(
-        "dq,qk->dk", grad_head, probs.astype(jnp.bfloat16), preferred_element_type=jnp.float32
-    )
-    grad_probs = jnp.einsum("dq,dk->qk", grad_head, values, preferred_element_type=jnp.float32)
-    inner = jnp.sum(probs * grad_probs, axis=1, keepdims=True)
-    grad_scores = (probs * (grad_probs - inner)).astype(jnp.bfloat16)
-    grad_query = (
-        jnp.einsum("qk,dk->dq", grad_scores, keys, preferred_element_type=jnp.float32) * scale
-    )
-    grad_keys = (
-        jnp.einsum("qk,dq->dk", grad_scores, query, preferred_element_type=jnp.float32) * scale
-    )
-    return jnp.stack([grad_query, grad_keys, grad_values]).astype(jnp.bfloat16)
+ROW=1536; BQ=256; NQ=ROW//BQ; SEGS=6
+LOG2E=1.4426950408889634
+BIG=float(2**30)
+def nt(a,b): return lax.dot_general(a,b,(((1,),(1,)),((),())),preferred_element_type=f32)
+def nn(a,b): return jnp.dot(a,b,preferred_element_type=f32)
+def seg_onehot(len_ref, rows):
+    pos=lax.broadcasted_iota(jnp.int32,(rows,128),0)
+    lane=lax.broadcasted_iota(jnp.int32,(rows,128),1)
+    idx=jnp.zeros((rows,128),jnp.int32)
+    end=jnp.int32(0)
+    for s in range(SEGS):
+        end=end+len_ref[0,s]
+        idx=idx+(pos>=end).astype(jnp.int32)
+    return (idx==lane).astype(f32)
+def prep(len_ref,q_ref,k_ref,qa,qb,ka,kb,first):
+    lane=lax.broadcasted_iota(jnp.int32,(ROW,128),1); low=lane<64
+    @pl.when(first)
+    def _():
+        oh=seg_onehot(len_ref,ROW)
+        qa[:,128:256]=oh.astype(bf); qb[:,128:256]=oh.astype(bf)
+        km=((oh-1.0)*BIG).astype(bf)
+        ka[:,128:256]=km; kb[:,128:256]=km
+    k=k_ref[...].astype(f32); kr=pltpu.roll(k,64,axis=1)
+    ka[:,0:128]=jnp.where(low,k,kr).astype(bf); kb[:,0:128]=jnp.where(low,kr,k).astype(bf)
+    q=q_ref[...].astype(f32)*(LOG2E*0.125); hi=q.astype(bf).astype(f32); lo=q-hi
+    qa[:,0:128]=jnp.where(low,hi,pltpu.roll(lo,64,axis=1)).astype(bf)
+    qb[:,0:128]=jnp.where(low,pltpu.roll(hi,64,axis=1),lo).astype(bf)
+def fwd_kernel(len_ref,q_ref,k_ref,v_ref,o_ref,lse_ref,qa,qb,ka,kb,va,vb,sa,sb,ot):
+    hp=pl.program_id(0)
+    prep(len_ref,q_ref,k_ref,qa,qb,ka,kb,hp==0)
+    vt=v_ref[...].T
+    @pl.when(hp==0)
+    def _():
+        one=(lax.broadcasted_iota(jnp.int32,(16,ROW),0)==0).astype(bf)
+        va[64:80,:]=one; vb[64:80,:]=one
+    va[0:64,:]=vt[0:64,:]; vb[0:64,:]=vt[64:128,:]
+    sa[...]=nt(ka[...],qa[0:BQ,:])
+    def soft(s_ref,v_sc,j,r):
+        s=s_ref[...]
+        m=jnp.max(s,axis=0,keepdims=True)
+        e=jnp.exp2(s-m).astype(bf)
+        o=nn(v_sc[...],e)
+        l=o[64:65,:]
+        cols=pl.ds(pl.multiple_of(j*BQ,BQ),BQ)
+        ot[64*r:64*r+64,cols]=o[0:64,:]*(1.0/l)
+        lse_ref[0,r:r+1,cols]=m+jnp.log2(l)
+    def body(j,c):
+        rows=pl.ds(pl.multiple_of(j*BQ,BQ),BQ)
+        nrow=pl.ds(pl.multiple_of(jnp.minimum(j+1,NQ-1)*BQ,BQ),BQ)
+        sb[...]=nt(kb[...],qb[rows,:])
+        soft(sa,va,j,0)
+        sa[...]=nt(ka[...],qa[nrow,:])
+        soft(sb,vb,j,1)
+        return c
+    lax.fori_loop(0,NQ,body,0)
+    o_ref[...]=ot[...].T.astype(bf)
+def attn_fwd(lengths,qkv):
+    H=6
+    return pl.pallas_call(fwd_kernel,grid=(H,),
+        in_specs=[pl.BlockSpec(memory_space=pltpu.SMEM),
+            pl.BlockSpec((ROW,128),lambda h:(0,h)),pl.BlockSpec((ROW,128),lambda h:(0,6+h)),pl.BlockSpec((ROW,128),lambda h:(0,12+h))],
+        out_specs=[pl.BlockSpec((ROW,128),lambda h:(0,h)),pl.BlockSpec((1,8,ROW),lambda h:(h,0,0))],
+        out_shape=[jax.ShapeDtypeStruct((ROW,768),bf),jax.ShapeDtypeStruct((6,8,ROW),f32)],
+        scratch_shapes=[pltpu.VMEM((ROW,256),bf)]*4+[pltpu.VMEM((80,ROW),bf)]*2+[pltpu.VMEM((ROW,BQ),f32)]*2+[pltpu.VMEM((128,ROW),f32)],
+        compiler_params=pltpu.CompilerParams(vmem_limit_bytes=60<<20),name="attn_fwd")(lengths,qkv,qkv,qkv)
+
+def bwd_kernel(len_ref,q_ref,k_ref,v_ref,o_ref,do_ref,lse_ref,dq_ref,dk_ref,dv_ref,
+               qa,qb,ka,kb,kt,da,db,qma,qmb,drow,xa,ya,xb,yb,dqt,dka,dva):
+    hp=pl.program_id(0)
+    prep(len_ref,q_ref,k_ref,qa,qb,ka,kb,hp==0)
+    lane=lax.broadcasted_iota(jnp.int32,(ROW,128),1); low=lane<64
+    kt[...]=k_ref[...].T
+    do=do_ref[...]; z=jnp.zeros_like(do)
+    da[...]=jnp.where(low,do,z); db[...]=jnp.where(low,z,do)
+    q=q_ref[...]
+    qma[...]=jnp.where(low,q,z); qmb[...]=jnp.where(low,z,q)
+    pr=(do.astype(f32)*o_ref[...].astype(f32)).T
+    drow[0:1,:]=jnp.sum(pr[0:64],axis=0,keepdims=True)
+    drow[1:2,:]=jnp.sum(pr[64:128],axis=0,keepdims=True)
+    dka[...]=jnp.zeros_like(dka); dva[...]=jnp.zeros_like(dva)
+    def mm(k_sc,q_sc,d_sc,x,y,rows):
+        x[...]=nt(k_sc[...],q_sc[rows,:])
+        y[...]=nt(v_ref[...],d_sc[rows,:])
+    def rest(x,y,d_sc,qm,r,rows):
+        p=jnp.exp2(x[...]-lse_ref[0,r:r+1,rows])
+        ds=(p*(y[...]-drow[r:r+1,rows])).astype(bf)
+        dva[...]+=nn(p.astype(bf),d_sc[rows,:])
+        dka[...]+=nn(ds,qm[rows,:])
+        dqt[64*r:64*r+64,rows]=nn(kt[64*r:64*r+64,:],ds)
+    mm(ka,qa,da,xa,ya,pl.ds(0,BQ))
+    def body(j,c):
+        rows=pl.ds(pl.multiple_of(j*BQ,BQ),BQ)
+        nrow=pl.ds(pl.multiple_of(jnp.minimum(j+1,NQ-1)*BQ,BQ),BQ)
+        mm(kb,qb,db,xb,yb,rows)
+        rest(xa,ya,da,qma,0,rows)
+        mm(ka,qa,da,xa,ya,nrow)
+        rest(xb,yb,db,qmb,1,rows)
+        return c
+    lax.fori_loop(0,NQ,body,0)
+    dq_ref[...]=(dqt[...].T*0.125).astype(bf)
+    dk_ref[...]=(dka[...]*0.125).astype(bf)
+    dv_ref[...]=dva[...].astype(bf)
+def attn_bwd(lengths,qkv,o,do,lse):
+    blk=lambda off: pl.BlockSpec((ROW,128),lambda h:(0,off+h))
+    return pl.pallas_call(bwd_kernel,grid=(6,),
+        in_specs=[pl.BlockSpec(memory_space=pltpu.SMEM),blk(0),blk(6),blk(12),blk(0),blk(0),pl.BlockSpec((1,8,ROW),lambda h:(h,0,0))],
+        out_specs=[blk(0),blk(0),blk(0)],
+        out_shape=[jax.ShapeDtypeStruct((ROW,768),bf)]*3,
+        scratch_shapes=[pltpu.VMEM((ROW,256),bf)]*4+[pltpu.VMEM((128,ROW),bf)]+[pltpu.VMEM((ROW,128),bf)]*4+[pltpu.VMEM((8,ROW),f32)]
+          +[pltpu.VMEM((ROW,BQ),f32)]*4+[pltpu.VMEM((128,ROW),f32)]+[pltpu.VMEM((ROW,128),f32)]*2,
+        compiler_params=pltpu.CompilerParams(vmem_limit_bytes=62<<20),name="attn_bwd")(lengths,qkv,qkv,qkv,o,do,lse)
 
 
 def adam_update(weight, grad, first, second, rate, decay, fix_one, fix_two):
@@ -148,19 +228,12 @@
         bias_down,
         scale_two,
     ) = unpack(full[4].astype(jnp.float32))
-    ids = jax.vmap(lambda line: segment_ids(line, row))(lengths)
-    ids_heads = jnp.repeat(ids, HEADS, axis=0)
     inputs = tokens.reshape(count, D).astype(jnp.float32)
     normed_f, norm_pull_one = jax.vjp(layer_norm, inputs, gain_one, shift_one)
     normed = normed_f.astype(jnp.bfloat16)
     bias = jnp.concatenate([bias_q, jnp.zeros_like(bias_q), bias_v])
     qkv = (jnp.dot(normed, mat_qkv, preferred_element_type=jnp.float32) + bias).astype(jnp.bfloat16)
-    qkv_heads = qkv.reshape(rows_dev, row, 3, HEADS, HEAD_DIM).transpose(0, 3, 2, 4, 1)
-    qkv_heads = qkv_heads.reshape(rows_dev * HEADS, 3, HEAD_DIM, row)
-    mixed_heads, totals = lax.map(head_forward, (qkv_heads, ids_heads))
-    mixed = (
-        mixed_heads.reshape(rows_dev, HEADS, HEAD_DIM, row).transpose(0, 3, 1, 2).reshape(count, D)
-    )
+    mixed, lse = attn_fwd(lengths, qkv)
     branch = jnp.dot(mixed, mat_proj, preferred_element_type=jnp.float32) + bias_o
     middle = inputs + scale_one * branch
     normed_two_f, norm_pull_two = jax.vjp(layer_norm, middle, gain_two, shift_two)
@@ -200,14 +273,7 @@
     grad_mixed = jnp.einsum(
         "ne,de->nd", grad_branch, back_proj, preferred_element_type=jnp.float32
     ).astype(jnp.bfloat16)
-    grad_heads = grad_mixed.reshape(rows_dev, row, HEADS, HEAD_DIM).transpose(0, 2, 3, 1)
-    grad_heads = grad_heads.reshape(rows_dev * HEADS, HEAD_DIM, row)
-    grad_qkv_heads = lax.map(head_backward, (qkv_heads, grad_heads, totals, ids_heads))
-    grad_qkv = (
-        grad_qkv_heads.reshape(rows_dev, HEADS, 3, HEAD_DIM, row)
-        .transpose(0, 4, 2, 1, 3)
-        .reshape(count, 3 * D)
-    )
+    grad_qkv = jnp.concatenate(attn_bwd(lengths, qkv, mixed, grad_mixed, lse), axis=1)
     grad_qkv_sums = jnp.sum(grad_qkv.astype(jnp.float32), axis=0)
     grad_weight_qkv = jnp.einsum("nd,ne->de", normed, grad_qkv, preferred_element_type=jnp.float32)
     grad_normed = jnp.einsum("ne,de->nd", grad_qkv, back_qkv, preferred_element_type=jnp.float32)

time: 1310 us -> 904 us (0.69)
  matrix products: 540 us -> 184 us
  other arithmetic: 206 us -> 44.8 us
  Pallas kernels: 0 us -> 143 us
  local copies, waits for them, and re-layouts: 127 us -> 40.7 us
  waiting for transfers between devices: 278 us -> 336 us
    dot_general x84 -> x0, matrix products: 352 us -> none  [the longest x24 101 us: masked_scores(): jnp.einsum('dq,dk->qk', query, keys, preferred_element_type=jnp.float32)]
    pallas_call x0 -> x2, Pallas kernels: none -> 143 us  [the longest x1 87.9 us: attn_bwd(): pl.pallas_call(bwd_kernel, grid=(6,), in_specs=[pl.BlockSpec(memory_space...]
    convert_element_type x12 -> x0, other arithmetic: 133 us -> none  [head_backward(): grad_scores = (probs * (grad_probs - inner)).astype(jnp.bfloat16)]
    all_gather x1, waiting for transfers between devices: 0.01 us -> 46.7 us  [local(): lax.all_gather(low_shards[2], ('dp', 'fsdp'), axis=0, tiled=True)]
    while x73 -> x0, local copies, waits for them, and re-layouts: 45.3 us -> none
    dynamic_slice x36 -> x0, local copies, waits for them, and re-layouts: 20.1 us -> none  [the longest x24 10.2 us: local(): mixed_heads, totals = lax.map(head_forward, (qkv_heads, ids_heads))]
    dynamic_update_slice x12 -> x0, local copies, waits for them, and re-layouts: 17.3 us -> none  [local(): mixed_heads, totals = lax.map(head_forward, (qkv_heads, ids_heads))]
    reduce_sum x13 -> x0, other arithmetic: 16 us -> none  [the longest x12 15.9 us: head_forward(): total = top + jnp.log(jnp.sum(jnp.exp(scores - top), axis=1, keepdims=True))]
  transfers between devices with their start and end apart: 8 -> 8, of which waited for: 3 -> 5; matrix products, arithmetic and copies ran while one was open for 58% -> 21% of each run, Pallas kernels for 0% -> 16%
where the time goes in v1:
time: 904 us; the launch traced here: 894 us
  waiting for transfers between devices  336 us (37%)
  matrix products  184 us (20%)
  Pallas kernels  143 us (16%)
  blocking collectives  124 us (14%)
  other arithmetic  44.8 us (5%)
  local copies, waits for them, and re-layouts  40.7 us (5%)
  between operations  21 us (2%)
    reduce_scatter x1, waiting for transfers between devices, local(): lax.psum_scatter(grad_fc2, ('dp', 'fsdp'), scatter_dimension=0, tiled=True)  139 us
    reduce_scatter x1, waiting for transfers between devices, local(): lax.psum_scatter(grad_fc1, ('dp', 'fsdp'), scatter_dimension=0, tiled=True)  132 us
    pallas_call x1, Pallas kernels, attn_bwd(): pl.pallas_call(bwd_kernel, grid=(6,), in_specs=[pl.BlockSpec(memory_space...  87.9 us
    pallas_call x1, Pallas kernels, attn_fwd(): pl.pallas_call(fwd_kernel, grid=(H,), in_specs=[pl.BlockSpec(memory_space...  54.8 us
    dot_general x1, matrix products, local(): jnp.dot(normed_two, mat_fc1, preferred_element_type=jnp.float32) + bias_up  54 us
    all_gather x1, waiting for transfers between devices, local(): lax.all_gather(low_shards[2], ('dp', 'fsdp'), axis=0, tiled=True)  46.7 us
    all_gather x1, blocking collectives, local(): lax.all_gather(low_shards[4], ('dp', 'fsdp'), axis=0, tiled=True)  43.9 us
    unnamed x1, blocking collectives  40.3 us
  transfers between devices with their start and end apart: 8, of which 5 were waited for; matrix products, arithmetic and copies ran while one was open for 21% of the time, Pallas kernels for 16%

profile of v1, /device:TPU:0, one launch (start us, length us, event | category | flops | bytes accessed | tf_op | source)
XLA Modules:
  0.0 893.6 jit_solution(9946067044179780847)
XLA Ops:
  14.6 43.9 %all-gather = bf16[32,24,14]{1,2,0:T(8,128)(2,1)S(1)} all-gather(bf16[1,24,14]{1,2,0:T(8,128)(2,1)S(1)} %convert_bitcast_fusion.1), channel_id=1, replica_groups=mesh['dp'=4,'fsdp'=8] {'dp','fsdp'}, dimensions={0}, use_global_device_ids=true | all-gather | bytes 22176 | tf_op jit(solution)/shard_map/all_gather | solution.py:215
  68.5 6.2 all-gather.6.cloned.1.call-done
  74.7 10.2 %add_convert_fusion.1.q_ref.k_ref.v_ref = bf16[1536,2304]{1,0:T(8,128)(2,1)} fusion(bf16[768,2304]{1,0:T(8,128)(2,1)} %all-gather.6.cloned.1.call-done, f32[2304]{0:T(1024)S(1)} %pad_maximum_fusion, bf16[1,1536,768]{1,2,0:T(8,128)(2,1)S(1)} %copy.66, f32[768]{0:T(1024)S(1)} %get-tuple-element.114, f32[768]{0:T(1024)S(1)} %get-tuple-element.115, ...), kind=kOutput, calls=%fused_computation.19 | convolution fusion | flops 5449973760 | bytes 13003776 | tf_op jit(solution)/shard_map/dot_general | solution.py:235
  84.9 54.8 %attn_fwd.1 = (bf16[1536,768]{1,0:T(8,128)(2,1)}, f32[6,8,1536]{2,1,0:T(8,128)}) custom-call(s32[1,6]{1,0:T(1,128)} %len_ref.3, bf16[1536,2304]{1,0:T(8,128)(2,1)} %add_convert_fusion.1.q_ref.k_ref.v_ref, bf16[1536,2304]{1,0:T(8,128)(2,1)} %add_convert_fusion.1.q_ref.k_ref.v_ref, bf16[1536,2304]{1,0:T(8,128)(2,1)} %add_convert_fusion.1.q_ref.k_ref.v_ref), custom_call_target="tpu_custom_call" | custom-call | tf_op jit(solution)/shard_map/attn_fwd/pallas_call | solution.py:118
  139.7 6.8 fusion.46
  150.8 46.7 %all-gather.10.cloned.1.call-done = bf16[768,3072]{1,0:T(8,128)(2,1)} async-done(((bf16[24,3072]{1,0:T(8,128)(2,1)}), bf16[768,3072]{1,0:T(8,128)(2,1)}) %all-gather.10.cloned.1.call-update) | async-done | bytes 4718608 | tf_op jit(solution)/shard_map/all_gather | solution.py:213
  197.6 54.0 %multiply_convert_fusion = (bf16[1536,3072]{1,0:T(8,128)(2,1)}, f32[1536,3072]{1,0:T(8,128)}, f32[1536,3072]{1,0:T(8,128)}) fusion(f32[3072]{0:T(1024)S(1)} %add.206, bf16[768,3072]{1,0:T(8,128)(2,1)} %all-gather.10.cloned.1.call-done, bf16[1536,768]{0,1:T(8,128)(2,1)} %add_convert_fusion.6.clone.4), kind=kOutput, calls=%fused_computation.4 | convolution fusion | flops 7559184384 | bytes 54276096 | tf_op jit(solution)/shard_map/dot_general | solution.py:241
  251.6 11.9 %all-gather.12.cloned.1.call-done = bf16[3072,768]{1,0:T(8,128)(2,1)} async-done(((bf16[96,768]{1,0:T(8,128)(2,1)}), bf16[3072,768]{1,0:T(8,128)(2,1)}) %all-gather.12.cloned.1.call-update) | async-done | bytes 4718608 | tf_op jit(solution)/shard_map/all_gather | solution.py:214
  263.5 23.0 %convert_reduce_fusion = (f32[3072]{0:T(1024)S(1)}, bf16[1536,3072]{1,0:T(8,128)(2,1)}) fusion(f32[1536,3072]{1,0:T(8,128)} %get-tuple-element.137, bf16[3072,768]{1,0:T(8,128)(2,1)} %all-gather.12.cloned.1.call-done, bf16[1,1536,768]{1,2,0:T(8,128)(2,1)S(1)} %copy-done.7, f32[768]{0:T(1024)S(1)} %copy-done.40, f32[1536,3072]{1,0:T(8,128)} %get-tuple-element.145, ...), kind=kOutput, calls=%fused_computation.2 | convolution fusion | flops 7331509248 | bytes 54291456 | tf_op jit(solution)/shard_map/nd,fd->nf/dot_general | solution.py:260
  286.6 13.3 %fusion.50 = (f32[768]{0:T(1024)S(1)}, f32[1536,768]{1,0:T(8,128)}) fusion(bf16[1536,3072]{1,0:T(8,128)(2,1)} %get-tuple-element.151, bf16[768,3072]{1,0:T(8,128)(2,1)} %all-gather.10.cloned.1.call-done), kind=kOutput, calls=%fused_computation.115 | convolution fusion | flops 7248935936 | bytes 18877440 | tf_op jit(solution)/shard_map/nf,df->nd/dot_general | solution.py:264
  299.9 6.2 copy.71
  306.1 5.2 multiply_reduce_fusion
  321.0 5.2 convolution_convert_fusion.do_ref
  326.2 87.9 %attn_bwd.1 = (bf16[1536,768]{1,0:T(8,128)(2,1)}, bf16[1536,768]{1,0:T(8,128)(2,1)}, bf16[1536,768]{1,0:T(8,128)(2,1)}) custom-call(s32[1,6]{1,0:T(1,128)} %len_ref.3, bf16[1536,2304]{1,0:T(8,128)(2,1)} %add_convert_fusion.1.q_ref.k_ref.v_ref, bf16[1536,2304]{1,0:T(8,128)(2,1)} %add_convert_fusion.1.q_ref.k_ref.v_ref, ...), custom_call_target="tpu_custom_call" | custom-call | tf_op jit(solution)/shard_map/attn_bwd/pallas_call | solution.py:164
  420.3 8.3 fusion.34
  429.3 13.8 %fusion.37 = f32[768,3072]{1,0:T(8,128)} fusion(bf16[1536,3072]{1,0:T(8,128)(2,1)} %get-tuple-element.151, f32[1536,768]{0,1:T(8,128)} %copy-done, f32[768]{0:T(1024)S(1)} %copy-done.36, f32[768]{0:T(1024)S(1)} %copy-done.29, f32[1536]{0:T(1024)S(1)} %copy-done.22, f32[1536]{0:T(1024)S(1)} %copy-done.18), kind=kOutput, calls=%fused_computation.109 | convolution fusion | flops 7253655552 | bytes 23611392 | tf_op jit(solution)/shard_map/nd,nf->df/dot_general | solution.py:263
  443.2 13.8 %fusion.31 = f32[3072,768]{1,0:T(8,128)} fusion(bf16[1536,3072]{1,0:T(8,128)(2,1)} %get-tuple-element.136, bf16[1,1536,768]{1,2,0:T(8,128)(2,1)} %copy.70, f32[768]{0:T(1024)S(1)} %copy-done.40), kind=kOutput, calls=%fused_computation.107 | convolution fusion | flops 7251296256 | bytes 21236736 | tf_op jit(solution)/shard_map/nf,nd->fd/dot_general | solution.py:259
  457.7 10.6 %fusion.49 = (f32[768]{0:T(1024)S(1)}, f32[1536,768]{1,0:T(8,128)}) fusion(bf16[1536,2304]{1,0:T(8,128)(2,1)} %copy-done.6, bf16[768,2304]{1,0:T(8,128)(2,1)} %all-gather.6.cloned.1.call-done), kind=kOutput, calls=%fused_computation.114 | convolution fusion | flops 5436996608 | bytes 15338496 | tf_op jit(solution)/shard_map/ne,de->nd/dot_general | solution.py:279
  468.3 6.1 copy.72
  480.5 21.5 %fusion.20 = (f32[768]{0:T(1024)S(1)}, f32[768]{0:T(1024)S(1)}, f32[768]{0:T(1024)S(1)}, bf16[1,1536,768]{1,2,0:T(8,128)(2,1)}, bf16[1,1536,768]{1,2,0:T(8,128)(2,1)}) fusion(bf16[1,1536,768]{1,2,0:T(8,128)(2,1)} %copy.70, f32[768]{0:T(1024)S(1)} %copy-done.41, f32[768]{0:T(1024)S(1)} %copy-done.40, f32[1536,768]{0,1:T(8,128)} %get-tuple-element.144, ...), kind=kOutput, calls=%fused_computation.41 | convolution fusion | flops 7278425088 | bytes 42519552 | tf_op jit(solution)/shard_map/dot_general | solution.py:244
  510.8 40.3 %all-reduce = f32[768,14]{0,1:T(8,128)S(1)} all-reduce(f32[768,14]{0,1:T(8,128)S(1)} %concatenate.11), channel_id=6, replica_groups=mesh['dp'=4,'fsdp'=8] {'dp','fsdp'}, use_global_device_ids=true, to_apply=%region_26.0.clone | all-reduce | flops 10752 | bytes 86016
  556.3 132.0 %reduce-scatter.10.cloned.1.call-done = f32[24,3072]{1,0:T(8,128)} async-done(((f32[768,3072]{1,0:T(8,128)}), f32[24,3072]{1,0:T(8,128)}) %reduce-scatter.10.cloned.1.call-update) | async-done | bytes 294928 | tf_op jit(solution)/shard_map/reduce_scatter | solution.py:306
  690.6 139.1 %reduce-scatter.12.cloned.1.call-done = f32[96,768]{1,0:T(8,128)} async-done(((f32[3072,768]{1,0:T(8,128)}), f32[96,768]{1,0:T(8,128)}) %reduce-scatter.12.cloned.1.call-update) | async-done | bytes 294928 | tf_op jit(solution)/shard_map/reduce_scatter | solution.py:307
  835.2 39.8 %psum.7 = f32[]{:T(128)} all-reduce(f32[]{:T(128)S(6)} %add.218), channel_id=1, replica_groups=mesh['dp'=4,'fsdp'=8] {'dp','fsdp'}, use_global_device_ids=true, to_apply=%region_28.0 | all-reduce | flops 1 | bytes 8 | tf_op jit(solution)/shard_map/psum | solution.py:314
  (179 shorter events, 71.9 us)
Async XLA Ops:
  7.2 67.5 %all-gather.6.cloned.1.call-start = ((), (), s32[]{:S(2)}) async-start(), calls=%async_computation.4 | async-start | bytes 3649536 | tf_op jit(solution)/shard_map/all_gather | solution.py:211
  8.9 130.8 %all-gather.8.cloned.1.call-start = ((), (), s32[]{:S(2)}) async-start(), calls=%async_computation.5 | async-start | bytes 1216512 | tf_op jit(solution)/shard_map/all_gather | solution.py:212
  10.4 187.1 %all-gather.10.cloned.1.call-start = ((), (), s32[]{:S(2)}) async-start(), calls=%async_computation.6 | async-start | bytes 4866048 | tf_op jit(solution)/shard_map/all_gather | solution.py:213
  12.2 251.4 %all-gather.12.cloned.1.call-start = ((), (), s32[]{:S(2)}) async-start(), calls=%async_computation.7 | async-start | bytes 4866048 | tf_op jit(solution)/shard_map/all_gather | solution.py:214
  13.9 538.0 %reduce-scatter.8.cloned.1.call-start = ((), (), s32[]{:S(2)}) async-start(), calls=%async_computation.9 | async-start | bytes 2433024 | tf_op jit(solution)/shard_map/reduce_scatter | solution.py:305
  59.6 80.1 %copy-start.37 = (f32[768]{0:T(1024)}, f32[768]{0:T(1024)S(1)}, u32[]{:S(2)}) copy-start(f32[768]{0:T(1024)S(1)} %get-tuple-element.116) | copy-start | bytes 9220
  59.6 80.1 %copy-start.42 = (f32[768]{0:T(1024)}, f32[768]{0:T(1024)S(1)}, u32[]{:S(2)}) copy-start(f32[768]{0:T(1024)S(1)} %get-tuple-element.111) | copy-start | bytes 9220
  59.6 87.5 %copy-start.28 = (f32[768]{0:T(1024)}, f32[768]{0:T(1024)S(1)}, u32[]{:S(2)}) copy-start(f32[768]{0:T(1024)S(1)} %get-tuple-element.110) | copy-start | bytes 9220
  59.6 87.5 %copy-start.35 = (f32[768]{0:T(1024)}, f32[768]{0:T(1024)S(1)}, u32[]{:S(2)}) copy-start(f32[768]{0:T(1024)S(1)} %get-tuple-element.109) | copy-start | bytes 9220
  66.8 72.9 %copy-start.1 = (bf16[1,1536,768]{1,2,0:T(8,128)(2,1)}, bf16[1,1536,768]{1,2,0:T(8,128)(2,1)S(1)}, u32[]{:S(2)}) copy-start(bf16[1,1536,768]{1,2,0:T(8,128)(2,1)S(1)} %copy.66) | copy-start | bytes 7077892
  67.2 17.7 %copy-start.19 = (f32[1536]{0:T(1024)}, f32[1536]{0:T(1024)S(1)}, u32[]{:S(2)}) copy-start(f32[1536]{0:T(1024)S(1)} %broadcast_multiply_fusion.1) | copy-start | bytes 18436
  68.5 16.4 %copy-start.33 = (f32[1536]{0:T(1024)}, f32[1536]{0:T(1024)S(1)}, u32[]{:S(2)}) copy-start(f32[1536]{0:T(1024)S(1)} %fusion.29) | copy-start | bytes 18436
  150.8 112.7 %copy-start.7 = (bf16[1,1536,768]{1,2,0:T(8,128)(2,1)S(1)}, bf16[1,1536,768]{1,2,0:T(8,128)(2,1)}, u32[]{:S(2)}) copy-start(bf16[1,1536,768]{1,2,0:T(8,128)(2,1)} %copy.70) | copy-start | bytes 7077892
  150.8 112.7 %copy-start.40 = (f32[768]{0:T(1024)S(1)}, f32[768]{0:T(1024)}, u32[]{:S(2)}) copy-start(f32[768]{0:T(1024)} %get-tuple-element.107) | copy-start | bytes 9220
  321.0 232.4 %reduce-scatter.6.cloned.1.call-start = ((), (), s32[]{:S(2)}) async-start(), calls=%async_computation.8 | async-start | bytes 7299072 | tf_op jit(solution)/shard_map/reduce_scatter | solution.py:304
  428.7 259.6 %reduce-scatter.10.cloned.1.call-start = ((), (), s32[]{:S(2)}) async-start(), calls=%async_computation.10 | async-start | bytes 9732096 | tf_op jit(solution)/shard_map/reduce_scatter | solution.py:306
  443.1 386.6 %reduce-scatter.12.cloned.1.call-start = ((), (), s32[]{:S(2)}) async-start(), calls=%async_computation.11 | async-start | bytes 9732096 | tf_op jit(solution)/shard_map/reduce_scatter | solution.py:307
  506.3 326.4 %copy-start.8 = (bf16[1,1536,768]{1,2,0:T(8,128)(2,1)S(1)}, bf16[1,1536,768]{1,2,0:T(8,128)(2,1)}, u32[]{:S(2)}) copy-start(bf16[1,1536,768]{1,2,0:T(8,128)(2,1)} %get-tuple-element.140) | copy-start | bytes 7077892
  510.6 365.1 %copy-start.32 = (f32[24,14]{0,1:T(8,128)S(1)}, f32[24,14]{0,1:T(8,128)}, u32[]{:S(2)}) copy-start(f32[24,14]{0,1:T(8,128)} %param.27) | copy-start | bytes 4036
  510.6 365.1 %copy-start.39 = (f32[24,14]{0,1:T(8,128)S(1)}, f32[24,14]{0,1:T(8,128)}, u32[]{:S(2)}) copy-start(f32[24,14]{0,1:T(8,128)} %param.37) | copy-start | bytes 4036
  510.6 370.4 %copy-start.13 = (f32[24,3072]{1,0:T(8,128)S(1)}, f32[24,3072]{1,0:T(8,128)}, u32[]{:S(2)}) copy-start(f32[24,3072]{1,0:T(8,128)} %param.25) | copy-start | bytes 884740
  556.2 326.9 %copy-start.14 = (f32[96,768]{1,0:T(8,128)S(1)}, f32[96,768]{1,0:T(8,128)}, u32[]{:S(2)}) copy-start(f32[96,768]{1,0:T(8,128)} %param.26) | copy-start | bytes 884740
  688.2 192.8 %copy-start.15 = (f32[24,3072]{1,0:T(8,128)S(1)}, f32[24,3072]{1,0:T(8,128)}, u32[]{:S(2)}) copy-start(f32[24,3072]{1,0:T(8,128)} %reduce-scatter.10.cloned.1.call-done) | copy-start | bytes 884740
  829.7 53.4 %copy-start.16 = (f32[96,768]{1,0:T(8,128)S(1)}, f32[96,768]{1,0:T(8,128)}, u32[]{:S(2)}) copy-start(f32[96,768]{1,0:T(8,128)} %reduce-scatter.12.cloned.1.call-done) | copy-start | bytes 884740
  (33 other events, 142.1 us)
Sparse Core Ops, SparseCore 0:
  11.6 63.0 all-gather.5
  78.3 52.9 all-gather.7
  134.9 62.5 all-gather.9
  201.0 62.4 all-gather.11
  321.1 97.7 reduce-scatter.7
  428.8 118.8 reduce-scatter.5
  553.5 134.6 reduce-scatter.9
  695.1 134.5 reduce-scatter.11

commit v2 on v1

v2 whole, which is shorter than its diff:
```python
import math

import jax
import jax.numpy as jnp
from jax import lax
from jax.experimental import pallas as pl
from jax.experimental.pallas import tpu as pltpu
from jax.sharding import PartitionSpec as P

D = 768
FF = 3072
NORM_EPS = 1e-06
BETA_ONE = 0.9
BETA_TWO = 0.999
ADAM_EPS = 1e-08
CLIP_LIMIT = 3.0
AXES = ("dp", "fsdp")
PACK = 32
bf = jnp.bfloat16
f32 = jnp.float32


def nt(a, b):
    return lax.dot_general(a, b, (((1,), (1,)), ((), ())), preferred_element_type=f32)


def nn(a, b):
    return jnp.dot(a, b, preferred_element_type=f32)


def tn(a, b):
    return lax.dot_general(a, b, (((0,), (0,)), ((), ())), preferred_element_type=f32)


ROW=1536; BQ=256; NQ=ROW//BQ; SEGS=6
LOG2E=1.4426950408889634
BIG=float(2**30)
def seg_onehot(len_ref, rows):
    pos=lax.broadcasted_iota(jnp.int32,(rows,128),0)
    lane=lax.broadcasted_iota(jnp.int32,(rows,128),1)
    idx=jnp.zeros((rows,128),jnp.int32)
    end=jnp.int32(0)
    for s in range(SEGS):
        end=end+len_ref[0,s]
        idx=idx+(pos>=end).astype(jnp.int32)
    return (idx==lane).astype(f32)
def prep(len_ref,q_ref,k_ref,qa,qb,ka,kb,first):
    lane=lax.broadcasted_iota(jnp.int32,(ROW,128),1); low=lane<64
    @pl.when(first)
    def _():
        oh=seg_onehot(len_ref,ROW)
        qa[:,128:256]=oh.astype(bf); qb[:,128:256]=oh.astype(bf)
        km=((oh-1.0)*BIG).astype(bf)
        ka[:,128:256]=km; kb[:,128:256]=km
    k=k_ref[...].astype(f32); kr=pltpu.roll(k,64,axis=1)
    ka[:,0:128]=jnp.where(low,k,kr).astype(bf); kb[:,0:128]=jnp.where(low,kr,k).astype(bf)
    q=q_ref[...].astype(f32)*(LOG2E*0.125); hi=q.astype(bf).astype(f32); lo=q-hi
    qa[:,0:128]=jnp.where(low,hi,pltpu.roll(lo,64,axis=1)).astype(bf)
    qb[:,0:128]=jnp.where(low,pltpu.roll(hi,64,axis=1),lo).astype(bf)
def fwd_kernel(len_ref,q_ref,k_ref,v_ref,o_ref,lse_ref,qa,qb,ka,kb,va,vb,sa,sb,ot):
    hp=pl.program_id(0)
    prep(len_ref,q_ref,k_ref,qa,qb,ka,kb,hp==0)
    vt=v_ref[...].T
    @pl.when(hp==0)
    def _():
        one=(lax.broadcasted_iota(jnp.int32,(16,ROW),0)==0).astype(bf)
        va[64:80,:]=one; vb[64:80,:]=one
    va[0:64,:]=vt[0:64,:]; vb[0:64,:]=vt[64:128,:]
    sa[...]=nt(ka[...],qa[0:BQ,:])
    def soft(s_ref,v_sc,j,r):
        s=s_ref[...]
        m=jnp.max(s,axis=0,keepdims=True)
        e=jnp.exp2(s-m).astype(bf)
        o=nn(v_sc[...],e)
        l=o[64:65,:]
        cols=pl.ds(pl.multiple_of(j*BQ,BQ),BQ)
        ot[64*r:64*r+64,cols]=o[0:64,:]*(1.0/l)
        lse_ref[0,r:r+1,cols]=m+jnp.log2(l)
    def body(j,c):
        rows=pl.ds(pl.multiple_of(j*BQ,BQ),BQ)
        nrow=pl.ds(pl.multiple_of(jnp.minimum(j+1,NQ-1)*BQ,BQ),BQ)
        sb[...]=nt(kb[...],qb[rows,:])
        soft(sa,va,j,0)
        sa[...]=nt(ka[...],qa[nrow,:])
        soft(sb,vb,j,1)
        return c
    lax.fori_loop(0,NQ,body,0)
    o_ref[...]=ot[...].T.astype(bf)
def attn_fwd(lengths,qkv):
    H=6
    return pl.pallas_call(fwd_kernel,grid=(H,),
        in_specs=[pl.BlockSpec(memory_space=pltpu.SMEM),
            pl.BlockSpec((ROW,128),lambda h:(0,h)),pl.BlockSpec((ROW,128),lambda h:(0,6+h)),pl.BlockSpec((ROW,128),lambda h:(0,12+h))],
        out_specs=[pl.BlockSpec((ROW,128),lambda h:(0,h)),pl.BlockSpec((1,8,ROW),lambda h:(h,0,0))],
        out_shape=[jax.ShapeDtypeStruct((ROW,768),bf),jax.ShapeDtypeStruct((6,8,ROW),f32)],
        scratch_shapes=[pltpu.VMEM((ROW,256),bf)]*4+[pltpu.VMEM((80,ROW),bf)]*2+[pltpu.VMEM((ROW,BQ),f32)]*2+[pltpu.VMEM((128,ROW),f32)],
        compiler_params=pltpu.CompilerParams(vmem_limit_bytes=60<<20),name="attn_fwd")(lengths,qkv,qkv,qkv)

def bwd_kernel(len_ref,q_ref,k_ref,v_ref,o_ref,do_ref,lse_ref,dq_ref,dk_ref,dv_ref,
               qa,qb,ka,kb,kt,da,db,qma,qmb,drow,xa,ya,xb,yb,dqt,dka,dva):
    hp=pl.program_id(0)
    prep(len_ref,q_ref,k_ref,qa,qb,ka,kb,hp==0)
    lane=lax.broadcasted_iota(jnp.int32,(ROW,128),1); low=lane<64
    kt[...]=k_ref[...].T
    do=do_ref[...]; z=jnp.zeros_like(do)
    da[...]=jnp.where(low,do,z); db[...]=jnp.where(low,z,do)
    q=q_ref[...]
    qma[...]=jnp.where(low,q,z); qmb[...]=jnp.where(low,z,q)
    pr=(do.astype(f32)*o_ref[...].astype(f32)).T
    drow[0:1,:]=jnp.sum(pr[0:64],axis=0,keepdims=True)
    drow[1:2,:]=jnp.sum(pr[64:128],axis=0,keepdims=True)
    dka[...]=jnp.zeros_like(dka); dva[...]=jnp.zeros_like(dva)
    def mm(k_sc,q_sc,d_sc,x,y,rows):
        x[...]=nt(k_sc[...],q_sc[rows,:])
        y[...]=nt(v_ref[...],d_sc[rows,:])
    def rest(x,y,d_sc,qm,r,rows):
        p=jnp.exp2(x[...]-lse_ref[0,r:r+1,rows])
        ds=(p*(y[...]-drow[r:r+1,rows])).astype(bf)
        dva[...]+=nn(p.astype(bf),d_sc[rows,:])
        dka[...]+=nn(ds,qm[rows,:])
        dqt[64*r:64*r+64,rows]=nn(kt[64*r:64*r+64,:],ds)
    mm(ka,qa,da,xa,ya,pl.ds(0,BQ))
    def body(j,c):
        rows=pl.ds(pl.multiple_of(j*BQ,BQ),BQ)
        nrow=pl.ds(pl.multiple_of(jnp.minimum(j+1,NQ-1)*BQ,BQ),BQ)
        mm(kb,qb,db,xb,yb,rows)
        rest(xa,ya,da,qma,0,rows)
        mm(ka,qa,da,xa,ya,nrow)
        rest(xb,yb,db,qmb,1,rows)
        return c
    lax.fori_loop(0,NQ,body,0)
    dq_ref[...]=(dqt[...].T*0.125).astype(bf)
    dk_ref[...]=(dka[...]*0.125).astype(bf)
    dv_ref[...]=dva[...].astype(bf)
def attn_bwd(lengths,qkv,o,do,lse):
    blk=lambda off: pl.BlockSpec((ROW,128),lambda h:(0,off+h))
    return pl.pallas_call(bwd_kernel,grid=(6,),
        in_specs=[pl.BlockSpec(memory_space=pltpu.SMEM),blk(0),blk(6),blk(12),blk(0),blk(0),pl.BlockSpec((1,8,ROW),lambda h:(h,0,0))],
        out_specs=[blk(0),blk(0),blk(0)],
        out_shape=[jax.ShapeDtypeStruct((ROW,768),bf)]*3,
        scratch_shapes=[pltpu.VMEM((ROW,256),bf)]*4+[pltpu.VMEM((128,ROW),bf)]+[pltpu.VMEM((ROW,128),bf)]*4+[pltpu.VMEM((8,ROW),f32)]
          +[pltpu.VMEM((ROW,BQ),f32)]*4+[pltpu.VMEM((128,ROW),f32)]+[pltpu.VMEM((ROW,128),f32)]*2,
        compiler_params=pltpu.CompilerParams(vmem_limit_bytes=62<<20),name="attn_bwd")(lengths,qkv,qkv,qkv,o,do,lse)


BM=512
INV_SQRT2=0.7071067811865476
INV_SQRT_2PI=0.3989422804014327
VMEM_CAP=62<<20


def norm_stats(v):
    center=v-jnp.mean(v,axis=1,keepdims=True)
    rstd=lax.rsqrt(jnp.mean(center*center,axis=1,keepdims=True)+NORM_EPS)
    return center*rstd,rstd


def params(**kw):
    return pltpu.CompilerParams(vmem_limit_bytes=VMEM_CAP,**kw)


def once(shape,index=None):
    return pl.BlockSpec(shape,index or (lambda i:(0,)*len(shape)),pipeline_mode=pl.Buffered(1))


def tile(width):
    return pl.BlockSpec((BM,width),lambda i:(i,0))


def qkv_kernel(x_ref,vec_ref,wq_ref,wk_ref,wv_ref,h_ref,qkv_ref):
    n,_=norm_stats(x_ref[...].astype(f32))
    h=(n*vec_ref[0:1,:]+vec_ref[1:2,:]).astype(bf)
    h_ref[...]=h
    qkv_ref[:,0:D]=(nn(h,wq_ref[...].reshape(D,D))+vec_ref[2:3,:]).astype(bf)
    qkv_ref[:,D:2*D]=nn(h,wk_ref[...].reshape(D,D)).astype(bf)
    qkv_ref[:,2*D:3*D]=(nn(h,wv_ref[...].reshape(D,D))+vec_ref[3:4,:]).astype(bf)


def qkv_forward(x,vec,w):
    rows=x.shape[0]
    n,r=w.shape[0],D//w.shape[0]
    blk=lambda b: pl.BlockSpec((n,r,D),lambda i:(0,b,0),pipeline_mode=pl.Buffered(1))
    return pl.pallas_call(qkv_kernel,grid=(rows//BM,),
        in_specs=[tile(D),once((16,D)),blk(0),blk(1),blk(2)],
        out_specs=[tile(D),tile(3*D)],
        out_shape=[jax.ShapeDtypeStruct((rows,D),bf),jax.ShapeDtypeStruct((rows,3*D),bf)],
        compiler_params=params(),name="qkv_forward",
        cost_estimate=pl.CostEstimate(flops=2*rows*D*3*D,bytes_accessed=14<<20,transcendentals=0))(x,vec,w,w,w)


CH=768


def mlp_kernel(x_ref,o_ref,dy_ref,vec_ref,w2_ref,wa_ref,wb_ref,wc_ref,wd_ref,wp_ref,
               out_ref,h_ref,dm_ref,z_ref,du_ref,dx_ref,da_ref,do_ref,sum_ref,
               a_s,x1_s,n2_s,mo_s,dh_s,ua,ub,ga,gb,w1_s):
    step=pl.program_id(0)
    @pl.when(step==0)
    def _():
        for b,ref in enumerate((wa_ref,wb_ref,wc_ref,wd_ref)):
            w1_s[b]=ref[...].reshape(D,D)
        sum_ref[...]=jnp.zeros_like(sum_ref)
    row=lambda i: vec_ref[i:i+1,:]
    def add(i,v):
        sum_ref[i:i+1,:]+=jnp.sum(v,axis=0,keepdims=True)
    wp=wp_ref[...].reshape(D,D)
    a=nn(o_ref[...],wp)+row(4)
    a_s[...]=a
    x1=x_ref[...].astype(f32)+row(5)*a
    x1_s[...]=x1
    n2,r2=norm_stats(x1)
    n2_s[...]=n2
    h=(n2*row(6)+row(7)).astype(bf)
    h_ref[...]=h
    dm=(row(13)*dy_ref[...].astype(f32)).astype(bf)
    dm_ref[...]=dm
    add(12,dm.astype(f32))
    mo_s[...]=jnp.zeros_like(mo_s)
    dh_s[...]=jnp.zeros_like(dh_s)
    def w2(c):
        return w2_ref[pl.ds(8*c,8)].reshape(D,D)
    def up(c,u,g):
        u[...]=nn(h_ref[...],w1_s[c])
        g[...]=nt(dm_ref[...],w2(c))
    def down(c,u,g):
        cols=pl.ds(pl.multiple_of(c*CH,CH),CH)
        v=u[...]+vec_ref[pl.ds(8+c,1),:]
        cdf=0.5+0.5*lax.erf(v*INV_SQRT2)
        z=(v*cdf).astype(bf)
        z_ref[:,cols]=z
        slope=cdf+v*(INV_SQRT_2PI*jnp.exp(v*v*(-0.5)))
        du=(g[...]*slope).astype(bf)
        du_ref[:,cols]=du
        sum_ref[pl.ds(8+c,1),:]+=jnp.sum(du.astype(f32),axis=0,keepdims=True)
        mo_s[...]+=nn(z,w2(c))
        dh_s[...]+=nt(du,w1_s[c])
    up(0,ua,ga)
    def body(i,carry):
        up(2*i+1,ub,gb)
        down(2*i,ua,ga)
        up(jnp.minimum(2*i+2,FF//CH-1),ua,ga)
        down(2*i+1,ub,gb)
        return carry
    lax.fori_loop(0,FF//CH//2,body,0)
    mo=mo_s[...]+row(12)
    out_ref[...]=(x1_s[...]+row(13)*mo).astype(bf)
    dy=dy_ref[...].astype(f32)
    add(13,dy*mo)
    dh=dh_s[...]; n2=n2_s[...]
    add(6,dh*n2); add(7,dh)
    t=dh*row(6)
    dx=dy+r2*(t-jnp.mean(t,axis=1,keepdims=True)-n2*jnp.mean(t*n2,axis=1,keepdims=True))
    dx_ref[...]=dx
    add(5,dx*a_s[...])
    da=(row(5)*dx).astype(bf)
    da_ref[...]=da
    add(4,da.astype(f32))
    do_ref[...]=nt(da,wp_ref[...].reshape(D,D)).astype(bf)


def mlp_block(x,o,dy,vec,packed):
    rows=x.shape[0]
    n,r=packed.shape[0],D//packed.shape[0]
    sd=jax.ShapeDtypeStruct
    return pl.pallas_call(mlp_kernel,grid=(rows//BM,),
        in_specs=[tile(D),tile(D),tile(D),once((16,D)),once((n,4*r,D))]+[once((n,r,D),lambda i,b=b:(0,b,0)) for b in range(4,9)],
        out_specs=[tile(D),tile(D),tile(D),tile(FF),tile(FF),tile(D),tile(D),tile(D),pl.BlockSpec((16,D),lambda i:(0,0))],
        out_shape=[sd((rows,D),bf),sd((rows,D),bf),sd((rows,D),bf),sd((rows,FF),bf),sd((rows,FF),bf),sd((rows,D),f32),sd((rows,D),bf),sd((rows,D),bf),sd((16,D),f32)],
        scratch_shapes=[pltpu.VMEM((BM,D),f32)]*5+[pltpu.VMEM((BM,CH),f32)]*4+[pltpu.VMEM((4,D,D),bf)],
        compiler_params=params(),name="mlp_block",
        cost_estimate=pl.CostEstimate(flops=2*rows*D*(2*D+4*FF),bytes_accessed=48<<20,transcendentals=0))(x,o,dy,vec,*[packed]*6)


def outer_kernel(a_ref,b_ref,g_ref):
    g_ref[...]=tn(a_ref[...],b_ref[...]).reshape(g_ref.shape).astype(bf)


def fc2_grad(z,dm,n,extra):
    rows=z.shape[0]
    per=FF//n
    return pl.pallas_call(outer_kernel,grid=(FF//D,),
        in_specs=[pl.BlockSpec((rows,D),lambda i:(0,i)),once((rows,D))],
        out_specs=pl.BlockSpec((n*D//FF,per,D),lambda i:(i,0,0)),
        out_shape=jax.ShapeDtypeStruct((n,per+extra,D),bf),
        compiler_params=params(),name="fc2_grad",
        cost_estimate=pl.CostEstimate(flops=2*rows*D*FF,bytes_accessed=16<<20,transcendentals=0))(z,dm)


def fc1_proj_kernel(h_ref,du_ref,o_ref,da_ref,old_ref,g_ref):
    i=pl.program_id(0)
    @pl.when(i<4)
    def _():
        g_ref[...]=tn(h_ref[...],du_ref[...]).reshape(g_ref.shape).astype(bf)
    @pl.when(i==4)
    def _():
        g_ref[...]=tn(o_ref[...],da_ref[...]).reshape(g_ref.shape).astype(bf)


def fc1_proj_grad(h,du,o,da,packed):
    rows=h.shape[0]
    n=packed.shape[0]; r=D//n
    base=packed.shape[1]//r-5
    return pl.pallas_call(fc1_proj_kernel,grid=(5,),
        in_specs=[once((rows,D)),pl.BlockSpec((rows,D),lambda i:(0,jnp.minimum(i,3))),once((rows,D)),once((rows,D)),pl.BlockSpec(memory_space=pl.ANY)],
        out_specs=pl.BlockSpec((n,r,D),lambda i:(0,base+i,0)),
        out_shape=jax.ShapeDtypeStruct(packed.shape,bf),input_output_aliases={4:0},
        compiler_params=params(),name="fc1_proj_grad",
        cost_estimate=pl.CostEstimate(flops=2*rows*D*(FF+D),bytes_accessed=24<<20,transcendentals=0))(h,du,o,da,packed)


def qkv_grad_kernel(h_ref,dq_ref,dk_ref,dv_ref,g_ref):
    i=pl.program_id(0)
    for b,ref in enumerate((dq_ref,dk_ref,dv_ref)):
        @pl.when(i==b)
        def _():
            g_ref[...]=tn(h_ref[...],ref[...]).reshape(g_ref.shape).astype(bf)


def qkv_grad(h,dq,dk,dv,n,extra):
    rows=h.shape[0]; r=D//n
    return pl.pallas_call(qkv_grad_kernel,grid=(3,),
        in_specs=[once((rows,D))]*4,
        out_specs=pl.BlockSpec((n,r,D),lambda i:(0,i,0)),
        out_shape=jax.ShapeDtypeStruct((n,3*r+extra,D),bf),
        compiler_params=params(),name="qkv_grad",
        cost_estimate=pl.CostEstimate(flops=2*rows*D*3*D,bytes_accessed=14<<20,transcendentals=0))(h,dq,dk,dv)


def input_kernel(x_ref,dq_ref,dk_ref,dv_ref,dx1_ref,vec_ref,old_ref,wq_ref,wk_ref,wv_ref,gx_ref,sum_ref):
    @pl.when(pl.program_id(0)==0)
    def _():
        sum_ref[...]=old_ref[...]
    def add(i,v):
        sum_ref[i:i+1,:]+=jnp.sum(v,axis=0,keepdims=True)
    dq=dq_ref[...]; dv=dv_ref[...]
    dh=nt(dq,wq_ref[...].reshape(D,D))+nt(dk_ref[...],wk_ref[...].reshape(D,D))+nt(dv,wv_ref[...].reshape(D,D))
    n,r=norm_stats(x_ref[...].astype(f32))
    add(0,dh*n); add(1,dh)
    add(2,dq.astype(f32)); add(3,dv.astype(f32))
    t=dh*vec_ref[0:1,:]
    dx=dx1_ref[...]+r*(t-jnp.mean(t,axis=1,keepdims=True)-n*jnp.mean(t*n,axis=1,keepdims=True))
    gx_ref[...]=dx.astype(bf)


def input_grad(x,dq,dk,dv,dx1,vec,sums,w):
    rows=x.shape[0]
    n,r=w.shape[0],D//w.shape[0]
    blk=lambda b: pl.BlockSpec((n,r,D),lambda i:(0,b,0),pipeline_mode=pl.Buffered(1))
    return pl.pallas_call(input_kernel,grid=(rows//BM,),
        in_specs=[tile(D)]*5+[once((16,D)),once((16,D)),blk(0),blk(1),blk(2)],
        out_specs=[tile(D),pl.BlockSpec((16,D),lambda i:(0,0))],
        out_shape=[jax.ShapeDtypeStruct((rows,D),bf),jax.ShapeDtypeStruct((16,D),f32)],
        compiler_params=params(),name="input_grad",
        cost_estimate=pl.CostEstimate(flops=2*rows*D*3*D,bytes_accessed=20<<20,transcendentals=0))(x,dq,dk,dv,dx1,vec,sums,w,w,w)


def adam_update(weight, grad, first, second, rate, decay, fix_one, fix_two):
    first = BETA_ONE * first + (1.0 - BETA_ONE) * grad
    second = BETA_TWO * second + (1.0 - BETA_TWO) * grad * grad
    stride = first / fix_one / (jnp.sqrt(second / fix_two) + ADAM_EPS)
    return (weight - rate * (stride + decay * weight), first, second)


def split_columns(shard):
    r, width = shard.shape
    return jnp.concatenate([shard[:, b * D : (b + 1) * D] for b in range(width // D)], axis=0)


def join_columns(block, r):
    return jnp.concatenate([block[b * r : (b + 1) * r] for b in range(block.shape[0] // r)], axis=1)


def pack_rows(full):
    k = full.shape[1] // D
    return full.reshape(PACK, D // PACK, k, D).transpose(0, 2, 1, 3).reshape(PACK, -1, D)


def unpack_rows(packed):
    k = packed.shape[1] * PACK // D
    return packed.reshape(PACK, k, D // PACK, D).transpose(0, 2, 1, 3).reshape(D, k * D)


def swap(value, axis, size, flip):
    return lax.ppermute(value, axis, [(i, i ^ flip) for i in range(size)])


def by_xor(parts, me):
    if len(parts) == 2:
        odd = me % 2 == 1
        return jnp.stack([jnp.where(odd, parts[1], parts[0]), jnp.where(odd, parts[0], parts[1])])
    low, high = (me % 2 == 1, me // 2 == 1)
    return jnp.stack(
        [
            jnp.where(high, jnp.where(low, parts[j ^ 3], parts[j ^ 2]), jnp.where(low, parts[j ^ 1], parts[j]))
            for j in range(4)
        ]
    )


def places():
    inner = lax.axis_index("fsdp")
    return (lax.axis_index("dp"), inner // 2, inner % 2)


def gather_direct(shard):
    me_dp, me_z, me_core = places()
    part = by_xor([shard] + [swap(shard, "fsdp", 8, 2 * k) for k in (1, 2, 3)], me_z)
    part = by_xor([part] + [swap(part, "dp", 4, k) for k in (1, 2, 3)], me_dp)
    part = by_xor([part, swap(part, "fsdp", 8, 1)], me_core)
    return part.transpose(1, 2, 0, 3, 4).reshape(PACK, *shard.shape)


def scatter_direct(packed, small):
    me_dp, me_z, me_core = places()
    packed = packed.reshape(4, 4, 2, -1, D)
    small = small.reshape(4, 4, 2, -1, D)

    def of_core(core):
        return jnp.concatenate(
            [lax.dynamic_index_in_dim(v, core, 2, keepdims=False) for v in (packed, small)], axis=2
        )

    mine, other = (of_core(me_core), of_core(1 - me_core))
    total = (mine.astype(f32) + swap(other, "fsdp", 8, 1).astype(f32)).astype(bf)
    pick = lambda v, i: lax.dynamic_index_in_dim(v, i, 0, keepdims=False)
    parts = [swap(pick(total, me_dp ^ k), "dp", 4, k) for k in (1, 2, 3)]
    total = (pick(total, me_dp).astype(f32) + sum(p.astype(f32) for p in parts)).astype(bf)
    parts = [swap(pick(total, me_z ^ k), "fsdp", 8, 2 * k) for k in (1, 2, 3)]
    return pick(total, me_z).astype(f32) + sum(p.astype(f32) for p in parts)


def make_local(fast):
    def gather(shard):
        return lax.all_gather(shard, AXES, axis=0, tiled=True)

    def scatter(full):
        return lax.psum_scatter(full, AXES, scatter_dimension=0, tiled=True)

    def local(
        tokens,
        cotangent,
        lengths,
        step,
        weight_qkv,
        weight_proj,
        weight_fc1,
        weight_fc2,
        vectors,
        first_qkv,
        second_qkv,
        first_proj,
        second_proj,
        first_fc1,
        second_fc1,
        first_fc2,
        second_fc2,
        first_vectors,
        second_vectors,
    ):
        per = weight_qkv.shape[0]
        cols = vectors.shape[1]
        low = [w.astype(bf) for w in (weight_qkv, weight_proj, weight_fc1, weight_fc2, vectors)]
        if fast:
            rest = lax.all_gather(
                jnp.concatenate([low[3], split_columns(low[2]), low[1]], axis=0), AXES, axis=0, tiled=False
            )
            line = jnp.pad(low[4].T.reshape(1, cols * per), ((0, 7), (0, D - cols * per)))
            mats_qkv = gather_direct(jnp.concatenate([split_columns(low[0]), line], axis=0))
            vec = mats_qkv[:, 3 * per, : cols * per].reshape(PACK, cols, per).transpose(1, 0, 2).reshape(cols, D)
        else:
            full = [gather(w) for w in low]
            rest = jnp.concatenate(
                [full[3].reshape(PACK, FF // PACK, D), pack_rows(full[2]), pack_rows(full[1])], axis=1
            )
            mats_qkv = pack_rows(full[0])
            vec = full[4].T
        vec = jnp.pad(vec.astype(f32), ((0, 16 - cols), (0, 0)))
        rows_dev, row, _ = tokens.shape
        count = rows_dev * row
        inputs = tokens.reshape(count, D)
        normed, qkv = qkv_forward(inputs, vec, mats_qkv)
        each = lambda v, b: v[b * row : (b + 1) * row]
        done = [attn_fwd(lengths[b : b + 1], each(qkv, b)) for b in range(rows_dev)]
        mixed = jnp.concatenate([o for o, _ in done], axis=0)
        result, normed_two, grad_down, active, grad_inner, grad_middle, grad_branch, grad_mixed, sums = mlp_block(
            inputs, mixed, cotangent.reshape(count, D), vec, rest
        )
        grads = fc2_grad(active, grad_down, PACK, 5 * D // PACK)
        grads = fc1_proj_grad(normed_two, grad_inner, mixed, grad_branch, grads)
        if fast:
            rest_owned = lax.psum_scatter(grads, AXES, scatter_dimension=0, tiled=False).astype(f32)
        back = [
            attn_bwd(lengths[b : b + 1], each(qkv, b), done[b][0], each(grad_mixed, b), done[b][1])
            for b in range(rows_dev)
        ]
        dq, dk, dv = (jnp.concatenate([v[i] for v in back], axis=0) for i in range(3))
        grad_inputs, sums = input_grad(inputs, dq, dk, dv, grad_middle, vec, sums, mats_qkv)
        grads_qkv = qkv_grad(normed, dq, dk, dv, PACK, 0)
        grads_vec = sums[:cols]
        if fast:
            line = grads_vec.reshape(cols, PACK, per).transpose(1, 0, 2).reshape(PACK, 1, cols * per)
            line = jnp.pad(line.astype(bf), ((0, 0), (0, 7), (0, D - cols * per)))
            first_owned = scatter_direct(grads_qkv, line)
            owned = (
                join_columns(first_owned[: 3 * per], per),
                rest_owned[8 * per :],
                join_columns(rest_owned[4 * per : 8 * per], per),
                rest_owned[: 4 * per],
                first_owned[3 * per, : cols * per].reshape(cols, per).T,
            )
        else:
            wide = FF // PACK
            owned = (
                scatter(unpack_rows(grads_qkv)),
                scatter(unpack_rows(grads[:, 2 * wide :])),
                scatter(unpack_rows(grads[:, wide : 2 * wide])),
                scatter(grads[:, :wide].reshape(FF, D)),
                scatter(grads_vec.T),
            )
            owned = tuple(g.astype(f32) for g in owned)
        squares = sum(jnp.sum(g * g) for g in owned)
        if fast:
            squares = jnp.sum(
                lax.all_to_all(jnp.full((PACK, 128), squares), AXES, 0, 0, tiled=True), axis=0
            )[0]
        else:
            squares = lax.psum(squares, AXES)
        norm = jnp.sqrt(squares)
        factor = jnp.minimum(1.0, CLIP_LIMIT / (norm + 1e-06))
        taken = step[0].astype(f32)
        fix_one = 1.0 - jnp.power(BETA_ONE, taken)
        fix_two = 1.0 - jnp.power(BETA_TWO, taken)
        rate_in = 2.0 / math.sqrt(D)
        states = (
            (weight_qkv, first_qkv, second_qkv, rate_in, 0.04),
            (weight_proj, first_proj, second_proj, 2.0 / math.sqrt(D // 48), 0.04),
            (weight_fc1, first_fc1, second_fc1, rate_in, 0.04),
            (weight_fc2, first_fc2, second_fc2, 2.0 / math.sqrt(FF), 0.04),
            (vectors, first_vectors, second_vectors, 1.0, 0.0),
        )
        new = [
            adam_update(w, factor * g, m, v, rate, decay, fix_one, fix_two)
            for g, (w, m, v, rate, decay) in zip(owned, states)
        ]
        shape = (rows_dev, row, D)
        outs = [result.reshape(shape), grad_inputs.reshape(shape), norm.reshape(1)]
        outs += [w for w, _, _ in new]
        for _, m, v in new:
            outs += [m, v]
        return tuple(outs)

    return local


def solution(mesh):
    rows = P(AXES, None)
    tokens = P(AXES, None, None)
    fast = (mesh.shape["dp"], mesh.shape["fsdp"]) == (4, 8)
    return jax.shard_map(
        make_local(fast),
        mesh=mesh,
        in_specs=(tokens, tokens, rows, P()) + (rows,) * 15,
        out_specs=(tokens, tokens, P()) + (rows,) * 15,
        check_vma=False,
    )
```

time: 904 us -> 432 us (0.48)
  waiting for transfers between devices: 336 us -> 87.5 us
  matrix products: 184 us -> 0 us
  blocking collectives: 124 us -> 0 us
  Pallas kernels: 143 us -> 259 us
  local copies, waits for them, and re-layouts: 40.7 us -> 11.5 us
  starting transfers between devices: 0.33 us -> 21.9 us
  other arithmetic: 44.8 us -> 24.5 us
    reduce_scatter x4 -> x1, waiting for transfers between devices: 271 us -> 0.01 us  [local(): lax.psum_scatter(grads, AXES, scatter_dimension=0, tiled=False).astype(f32)]
    dot_general x12 -> x0, matrix products: 184 us -> none  [the longest x1 54 us: local(): jnp.dot(normed_two, mat_fc1, preferred_element_type=jnp.float32) + bias_up]
    pallas_call x0 -> x6, Pallas kernels: none -> 117 us  [the longest x1 54.3 us: mlp_block(): pl.pallas_call(mlp_kernel, grid=(rows // BM,), in_specs=[tile(D), tile(D)...]
    ppermute x0 -> x14, waiting for transfers between devices: none -> 81.1 us  [swap(): return lax.ppermute(value, axis, [(i, i ^ flip) for i in range(size)])]
    all_gather x4 -> x1, waiting for transfers between devices: 64.9 us -> 0.01 us  [local(): lax.all_gather(jnp.concatenate([low[3], split_columns(low[2]), low[1]], a...]
    all_gather x1 -> x0, blocking collectives: 43.9 us -> none  [local(): lax.all_gather(low_shards[4], ('dp', 'fsdp'), axis=0, tiled=True)]
    unnamed x1 -> x0, blocking collectives: 40.3 us -> none
    psum x1 -> x0, blocking collectives: 39.8 us -> none  [local(): total_squares = lax.psum(local_squares, ('dp', 'fsdp'))]
  transfers between devices with their start and end apart: 8 -> 17, of which waited for: 5 -> 13; matrix products, arithmetic and copies ran while one was open for 21% -> 5% of each run, Pallas kernels for 16% -> 42%
where the time goes in v2:
time: 432 us; the launch traced here: 425 us
  Pallas kernels  259 us (60%)
  waiting for transfers between devices  87.5 us (20%)
  other arithmetic  24.5 us (6%)
  starting transfers between devices  21.9 us (5%)
  between operations  20.2 us (5%)
  local copies, waits for them, and re-layouts  11.5 us (3%)
    pallas_call x1, Pallas kernels, attn_bwd(): pl.pallas_call(bwd_kernel, grid=(6,), in_specs=[pl.BlockSpec(memory_space...  87.8 us
    ppermute x14, waiting for transfers between devices, swap(): return lax.ppermute(value, axis, [(i, i ^ flip) for i in range(size)])  81.1 us
    pallas_call x1, Pallas kernels, attn_fwd(): pl.pallas_call(fwd_kernel, grid=(H,), in_specs=[pl.BlockSpec(memory_space...  54.8 us
    pallas_call x1, Pallas kernels, mlp_block(): pl.pallas_call(mlp_kernel, grid=(rows // BM,), in_specs=[tile(D), tile(D)...  54.3 us
    ppermute x14, starting transfers between devices, swap(): return lax.ppermute(value, axis, [(i, i ^ flip) for i in range(size)])  17.8 us
    pallas_call x1, Pallas kernels, fc1_proj_grad(): pl.pallas_call(fc1_proj_kernel, grid=(5,), in_specs=[once((rows, D)), pl....  15.5 us
    pallas_call x1, Pallas kernels, input_grad(): pl.pallas_call(input_kernel, grid=(rows // BM,), in_specs=[tile(D)] * 5 +...  12.5 us
    pallas_call x1, Pallas kernels, fc2_grad(): pl.pallas_call(outer_kernel, grid=(FF // D,), in_specs=[pl.BlockSpec((row...  11.7 us
  transfers between devices with their start and end apart: 17, of which 13 were waited for; matrix products, arithmetic and copies ran while one was open for 5% of the time, Pallas kernels for 42%

profile of v2, /device:TPU:0, one launch (start us, length us, event | category | flops | bytes accessed | tf_op | source)
XLA Modules:
  0.0 424.8 jit_solution(2345968126465953752)
XLA Ops:
  12.7 5.1 %collective-permute-start = (bf16[80,768]{1,0:T(8,128)(2,1)S(1)}, bf16[80,768]{1,0:T(8,128)(2,1)S(1)}, u32[]{:S(2)}, u32[]{:S(2)}) collective-permute-start(bf16[80,768]{1,0:T(8,128)(2,1)S(1)} %fusion.6), channel_id=1, source_target_pairs={{0,6},{1,7},{2,4},{3,5},{4,2},{5,3},{6,0},{7,1},{8,14},{9,15},{10,... | collective-permute-start | bytes 368648 | tf_op jit(solution)/shard_map/ppermute | solution.py:384
  18.5 3.6 collective-permute-done
  22.1 9.2 %collective-permute-done.1 = bf16[80,768]{1,0:T(8,128)(2,1)S(1)} collective-permute-done((bf16[80,768]{1,0:T(8,128)(2,1)S(1)}, bf16[80,768]{1,0:T(8,128)(2,1)S(1)}, u32[]{:S(2)}, u32[]{:S(2)}) %collective-permute-start.1) | collective-permute-done | bytes 122912 | tf_op jit(solution)/shard_map/ppermute | solution.py:384
  31.6 3.2 collective-permute-start.3
  35.5 15.2 %collective-permute-done.3 = bf16[4,80,768]{2,1,0:T(8,128)(2,1)S(1)} collective-permute-done((bf16[4,80,768]{2,1,0:T(8,128)(2,1)S(1)}, bf16[4,80,768]{2,1,0:T(8,128)(2,1)S(1)}, u32[]{:S(2)}, u32[]{:S(2)}) %collective-permute-start.3) | collective-permute-done | bytes 491552 | tf_op jit(solution)/shard_map/ppermute | solution.py:384
  50.7 6.8 %collective-permute-done.4 = bf16[4,80,768]{2,1,0:T(8,128)(2,1)S(1)} collective-permute-done((bf16[4,80,768]{2,1,0:T(8,128)(2,1)S(1)}, bf16[4,80,768]{2,1,0:T(8,128)(2,1)S(1)}, u32[]{:S(2)}, u32[]{:S(2)}) %collective-permute-start.4) | collective-permute-done | bytes 491552 | tf_op jit(solution)/shard_map/ppermute | solution.py:384
  57.5 4.9 %collective-permute-done.5 = bf16[4,80,768]{2,1,0:T(8,128)(2,1)S(1)} collective-permute-done((bf16[4,80,768]{2,1,0:T(8,128)(2,1)S(1)}, bf16[4,80,768]{2,1,0:T(8,128)(2,1)S(1)}, u32[]{:S(2)}, u32[]{:S(2)}) %collective-permute-start.5) | collective-permute-done | bytes 491552 | tf_op jit(solution)/shard_map/ppermute | solution.py:384
  65.3 4.3 %collective-permute-done.6 = bf16[4,4,80,768]{3,2,1,0:T(8,128)(2,1)} collective-permute-done((bf16[4,4,80,768]{3,2,1,0:T(8,128)(2,1)}, bf16[4,4,80,768]{3,2,1,0:T(8,128)(2,1)}, u32[]{:S(2)}, u32[]{:S(2)}) %collective-permute-start.6) | collective-permute-done | bytes 1966112 | tf_op jit(solution)/shard_map/ppermute | solution.py:384
  75.2 10.9 %qkv_forward.1 = (bf16[1536,768]{1,0:T(8,128)(2,1)}, bf16[1536,2304]{1,0:T(8,128)(2,1)}) custom-call(bf16[1536,768]{1,0:T(8,128)(2,1)} %bitcast.102, f32[16,768]{1,0:T(8,128)} %pad_convert_fusion.vec_ref, bf16[32,80,768]{2,1,0:T(8,128)(2,1)} %bitcast.95, bf16[32,80,768]{2,1,0:T(8,128)(2,1)} %bitcast.96, bf16[32,80,768]{2,1,0:T(8,128)(2,1)} %bitcast.97), custom_call_target="tpu_custom_call" | custom-call | flops 5435817984 | bytes 14680064 | tf_op jit(solution)/shard_map/qkv_forward/pallas_call | solution.py:183
  86.1 54.8 %attn_fwd.1 = (bf16[1536,768]{1,0:T(8,128)(2,1)}, f32[6,8,1536]{2,1,0:T(8,128)}) custom-call(s32[1,6]{1,0:T(1,128)} %len_ref.3, bf16[1536,2304]{1,0:T(8,128)(2,1)} %get-tuple-element.36.q_ref.k_ref.v_ref, bf16[1536,2304]{1,0:T(8,128)(2,1)} %get-tuple-element.36.q_ref.k_ref.v_ref, bf16[1536,2304]{1,0:T(8,128)(2,1)} %get-tuple-element.36.q_ref.k_ref.v_ref), custom_call_target="tpu_custom_call" | custom-call | tf_op jit(solution)/shard_map/attn_fwd/pallas_call | solution.py:91
  140.9 54.3 %mlp_block.1 = (bf16[1536,768]{1,0:T(8,128)(2,1)}, bf16[1536,768]{1,0:T(8,128)(2,1)}, bf16[1536,768]{1,0:T(8,128)(2,1)}, bf16[1536,3072]{1,0:T(8,128)(2,1)}, bf1...) custom-call(bf16[1536,768]{1,0:T(8,128)(2,1)} %bitcast.103, ...), custom_call_target="tpu_custom_call" | custom-call | flops 32614907904 | bytes 50331648 | tf_op jit(solution)/shard_map/mlp_block/pallas_call | solution.py:265
  195.3 11.7 %fc2_grad.1.old_ref = bf16[32,216,768]{2,1,0:T(8,128)(2,1)} custom-call(bf16[1536,3072]{1,0:T(8,128)(2,1)} %get-tuple-element.52.a_ref, bf16[1536,768]{1,0:T(8,128)(2,1)} %get-tuple-element.53.b_ref), custom_call_target="tpu_custom_call" | custom-call | flops 7247757312 | bytes 16777216 | tf_op jit(solution)/shard_map/fc2_grad/pallas_call | solution.py:281
  207.0 15.5 %fc1_proj_grad.1 = bf16[32,216,768]{2,1,0:T(8,128)(2,1)} custom-call(bf16[1536,768]{1,0:T(8,128)(2,1)} %get-tuple-element.49.h_ref, bf16[1536,3072]{1,0:T(8,128)(2,1)} %get-tuple-element.50.du_ref, bf16[1536,768]{1,0:T(8,128)(2,1)} %get-tuple-element.37.o_ref, bf16[1536,768]{1,0:T(8,128)(2,1)} %get-tuple-element.51.da_ref, ...), custom_call_target="tpu_custom_call", output_to_operand_aliasing={{}: (4, {})} | custom-call | flops 9059696640 | bytes 25165824 | tf_op jit(solution)/shard_map/fc1_proj_grad/pallas_call | solution.py:303
  222.5 87.8 %attn_bwd.1 = (bf16[1536,768]{1,0:T(8,128)(2,1)}, bf16[1536,768]{1,0:T(8,128)(2,1)}, bf16[1536,768]{1,0:T(8,128)(2,1)}) custom-call(s32[1,6]{1,0:T(1,128)} %len_ref.3, bf16[1536,2304]{1,0:T(8,128)(2,1)} %get-tuple-element.36.q_ref.k_ref.v_ref, bf16[1536,2304]{1,0:T(8,128)(2,1)} %get-tuple-element.36.q_ref.k_ref.v_ref, ...), custom_call_target="tpu_custom_call" | custom-call | tf_op jit(solution)/shard_map/attn_bwd/pallas_call | solution.py:137
  310.3 12.5 %input_grad.1 = (bf16[1536,768]{1,0:T(8,128)(2,1)}, f32[16,768]{1,0:T(8,128)}) custom-call(bf16[1536,768]{1,0:T(8,128)(2,1)} %bitcast.104, bf16[1536,768]{1,0:T(8,128)(2,1)} %get-tuple-element.41.dq_ref, bf16[1536,768]{1,0:T(8,128)(2,1)} %get-tuple-element.42.dk_ref, bf16[1536,768]{1,0:T(8,128)(2,1)} %get-tuple-element.43.dv_ref, ...), custom_call_target="tpu_custom_call" | custom-call | flops 5435817984 | bytes 20971520 | tf_op jit(solution)/shard_map/input_grad/pallas_call | solution.py:349
  324.1 11.7 %qkv_grad.1 = bf16[32,72,768]{2,1,0:T(8,128)(2,1)} custom-call(bf16[1536,768]{1,0:T(8,128)(2,1)} %get-tuple-element.47.h_ref, bf16[1536,768]{1,0:T(8,128)(2,1)} %get-tuple-element.41.dq_ref, bf16[1536,768]{1,0:T(8,128)(2,1)} %get-tuple-element.42.dk_ref, bf16[1536,768]{1,0:T(8,128)(2,1)} %get-tuple-element.43.dv_ref), custom_call_target="tpu_custom_call" | custom-call | flops 5435817984 | bytes 14680064 | tf_op jit(solution)/shard_map/qkv_grad/pallas_call | solution.py:321
  335.8 3.5 dynamic-slice_bitcast_fusion.1
  340.9 4.0 collective-permute-done.7
  346.2 2.6 add_convert_fusion
  353.2 13.9 %collective-permute-done.10 = bf16[4,80,768]{2,1,0:T(8,128)(2,1)S(1)} collective-permute-done((bf16[4,80,768]{2,1,0:T(8,128)(2,1)}, bf16[4,80,768]{2,1,0:T(8,128)(2,1)S(1)}, u32[]{:S(2)}, u32[]{:S(2)}) %collective-permute-start.10) | collective-permute-done | bytes 491552 | tf_op jit(solution)/shard_map/ppermute | solution.py:384
  367.1 9.7 %collective-permute-done.8 = bf16[4,80,768]{2,1,0:T(8,128)(2,1)} collective-permute-done((bf16[4,80,768]{2,1,0:T(8,128)(2,1)S(1)}, bf16[4,80,768]{2,1,0:T(8,128)(2,1)}, u32[]{:S(2)}, u32[]{:S(2)}) %collective-permute-start.8) | collective-permute-done | bytes 491552 | tf_op jit(solution)/shard_map/ppermute | solution.py:384
  385.3 7.0 %collective-permute-done.12 = bf16[80,768]{1,0:T(8,128)(2,1)S(1)} collective-permute-done((bf16[80,768]{1,0:T(8,128)(2,1)S(1)}, bf16[80,768]{1,0:T(8,128)(2,1)S(1)}, u32[]{:S(2)}, u32[]{:S(2)}) %collective-permute-start.12) | collective-permute-done | bytes 122912 | tf_op jit(solution)/shard_map/ppermute | solution.py:384
  400.5 4.0 all-to-all-start
  405.2 6.3 %all-to-all-done = f32[32,1,128]{2,1,0:T(1,128)S(1)} async-done(((f32[32,1,128]{2,1,0:T(1,128)}), f32[32,1,128]{2,1,0:T(1,128)S(1)}, u32[]{:S(2)}, u32[]{:S(2)}) %all-to-all-start) | async-done | bytes 16416 | tf_op jit(solution)/shard_map/all_to_all | solution.py:524
  (119 shorter events, 42.0 us)
Async XLA Ops:
  7.2 133.8 %all-gather.3.cloned.1.call-start = ((), (), s32[]{:S(2)}) async-start(), calls=%async_computation.3 | async-start | bytes 10948608 | tf_op jit(solution)/shard_map/all_gather | solution.py:464
  10.9 382.7 %reduce-scatter.2.cloned.1.call-start = ((), (), s32[]{:S(2)}) async-start(), calls=%async_computation.2 | async-start | bytes 10948608 | tf_op jit(solution)/shard_map/reduce_scatter | solution.py:491
  12.7 9.4 %collective-permute-start = (bf16[80,768]{1,0:T(8,128)(2,1)S(1)}, bf16[80,768]{1,0:T(8,128)(2,1)S(1)}, u32[]{:S(2)}, u32[]{:S(2)}) collective-permute-start(bf16[80,768]{1,0:T(8,128)(2,1)S(1)} %fusion.6), channel_id=1, source_target_pairs={{0,6},{1,7},{2,4},{3,5},{4,2},{5,3},{6,0},{7,1},{8,14},{9,15},{10,... | collective-permute-start | bytes 368648 | tf_op jit(solution)/shard_map/ppermute | solution.py:384
  17.9 13.4 %collective-permute-start.1 = (bf16[80,768]{1,0:T(8,128)(2,1)S(1)}, bf16[80,768]{1,0:T(8,128)(2,1)S(1)}, u32[]{:S(2)}, u32[]{:S(2)}) collective-permute-start(bf16[80,768]{1,0:T(8,128)(2,1)S(1)} %fusion.6), channel_id=1, source_target_pairs={{0,4},{1,5},{2,6},{3,7},{4,0},{5,1},{6,2},{7,3},{8,12},{9,13},{10,... | collective-permute-start | bytes 368648 | tf_op jit(solution)/shard_map/ppermute | solution.py:384
  17.9 13.4 %collective-permute-start.2 = (bf16[80,768]{1,0:T(8,128)(2,1)S(1)}, bf16[80,768]{1,0:T(8,128)(2,1)S(1)}, u32[]{:S(2)}, u32[]{:S(2)}) collective-permute-start(bf16[80,768]{1,0:T(8,128)(2,1)S(1)} %fusion.6), channel_id=1, source_target_pairs={{0,2},{1,3},{2,0},{3,1},{4,6},{5,7},{6,4},{7,5},{8,10},{9,11},{10,... | collective-permute-start | bytes 368648 | tf_op jit(solution)/shard_map/ppermute | solution.py:384
  31.4 31.0 %copy-start.2 = (bf16[1,80,768]{2,1,0:T(8,128)(2,1)}, bf16[1,80,768]{2,1,0:T(8,128)(2,1)S(1)}, u32[]{:S(2)}) copy-start(bf16[1,80,768]{2,1,0:T(8,128)(2,1)S(1)} %select_bitcast_fusion.6) | copy-start | bytes 368644
  31.5 30.9 %copy-start.3 = (bf16[1,80,768]{2,1,0:T(8,128)(2,1)}, bf16[1,80,768]{2,1,0:T(8,128)(2,1)S(1)}, u32[]{:S(2)}) copy-start(bf16[1,80,768]{2,1,0:T(8,128)(2,1)S(1)} %get-tuple-element.87) | copy-start | bytes 368644
  31.5 30.9 %copy-start.4 = (bf16[1,80,768]{2,1,0:T(8,128)(2,1)}, bf16[1,80,768]{2,1,0:T(8,128)(2,1)S(1)}, u32[]{:S(2)}) copy-start(bf16[1,80,768]{2,1,0:T(8,128)(2,1)S(1)} %get-tuple-element.88) | copy-start | bytes 368644
  31.5 30.9 %copy-start.5 = (bf16[1,80,768]{2,1,0:T(8,128)(2,1)}, bf16[1,80,768]{2,1,0:T(8,128)(2,1)S(1)}, u32[]{:S(2)}) copy-start(bf16[1,80,768]{2,1,0:T(8,128)(2,1)S(1)} %get-tuple-element.89) | copy-start | bytes 368644
  31.6 19.1 %collective-permute-start.3 = (bf16[4,80,768]{2,1,0:T(8,128)(2,1)S(1)}, bf16[4,80,768]{2,1,0:T(8,128)(2,1)S(1)}, u32[]{:S(2)}, u32[]{:S(2)}) collective-permute-start(bf16[4,80,768]{2,1,0:T(8,128)(2,1)S(1)} %pad_maximum_fusion.2), channel_id=1, source_target_pairs={{0,24},{8,16},{16,8},{24,0},{1,25},{9,17},{17,9},{25,1},{2,26},{10... | collective-permute-start | bytes 1474568 | tf_op jit(solution)/shard_map/ppermute | solution.py:384
  34.8 22.7 %collective-permute-start.4 = (bf16[4,80,768]{2,1,0:T(8,128)(2,1)S(1)}, bf16[4,80,768]{2,1,0:T(8,128)(2,1)S(1)}, u32[]{:S(2)}, u32[]{:S(2)}) collective-permute-start(bf16[4,80,768]{2,1,0:T(8,128)(2,1)S(1)} %pad_maximum_fusion.2), channel_id=1, source_target_pairs={{0,16},{8,24},{16,0},{24,8},{1,17},{9,25},{17,1},{25,9},{2,18},{10... | collective-permute-start | bytes 1474568 | tf_op jit(solution)/shard_map/ppermute | solution.py:384
  34.8 27.6 %collective-permute-start.5 = (bf16[4,80,768]{2,1,0:T(8,128)(2,1)S(1)}, bf16[4,80,768]{2,1,0:T(8,128)(2,1)S(1)}, u32[]{:S(2)}, u32[]{:S(2)}) collective-permute-start(bf16[4,80,768]{2,1,0:T(8,128)(2,1)S(1)} %pad_maximum_fusion.2), channel_id=1, source_target_pairs={{0,8},{8,0},{16,24},{24,16},{1,9},{9,1},{17,25},{25,17},{2,10},{10... | collective-permute-start | bytes 1474568 | tf_op jit(solution)/shard_map/ppermute | solution.py:384
  65.3 4.3 %collective-permute-start.6 = (bf16[4,4,80,768]{3,2,1,0:T(8,128)(2,1)}, bf16[4,4,80,768]{3,2,1,0:T(8,128)(2,1)}, u32[]{:S(2)}, u32[]{:S(2)}) collective-permute-start(bf16[4,4,80,768]{3,2,1,0:T(8,128)(2,1)} %pad_maximum_fusion), channel_id=1, source_target_pairs={{0,1},{1,0},{2,3},{3,2},{4,5},{5,4},{6,7},{7,6},{8,9},{9,8},{10,11... | collective-permute-start | bytes 5898248 | tf_op jit(solution)/shard_map/ppermute | solution.py:384
  340.7 4.2 collective-permute-start.7
  349.7 17.4 %collective-permute-start.10 = (bf16[4,80,768]{2,1,0:T(8,128)(2,1)}, bf16[4,80,768]{2,1,0:T(8,128)(2,1)S(1)}, u32[]{:S(2)}, u32[]{:S(2)}) collective-permute-start(bf16[4,80,768]{2,1,0:T(8,128)(2,1)} %get-tuple-element.74), channel_id=1, source_target_pairs={{0,24},{8,16},{16,8},{24,0},{1,25},{9,17},{17,9},{25,1},{2,26},{10... | collective-permute-start | bytes 1474568 | tf_op jit(solution)/shard_map/ppermute | solution.py:384
  351.7 25.1 %collective-permute-start.8 = (bf16[4,80,768]{2,1,0:T(8,128)(2,1)S(1)}, bf16[4,80,768]{2,1,0:T(8,128)(2,1)}, u32[]{:S(2)}, u32[]{:S(2)}) collective-permute-start(bf16[4,80,768]{2,1,0:T(8,128)(2,1)S(1)} %get-tuple-element.73), channel_id=1, source_target_pairs={{0,8},{8,0},{16,24},{24,16},{1,9},{9,1},{17,25},{25,17},{2,10},{10... | collective-permute-start | bytes 1474568 | tf_op jit(solution)/shard_map/ppermute | solution.py:384
  352.3 24.6 %collective-permute-start.9 = (bf16[4,80,768]{2,1,0:T(8,128)(2,1)S(1)}, bf16[4,80,768]{2,1,0:T(8,128)(2,1)}, u32[]{:S(2)}, u32[]{:S(2)}) collective-permute-start(bf16[4,80,768]{2,1,0:T(8,128)(2,1)S(1)} %get-tuple-element.75), channel_id=1, source_target_pairs={{0,16},{8,24},{16,0},{24,8},{1,17},{9,25},{17,1},{25,9},{2,18},{10... | collective-permute-start | bytes 1474568 | tf_op jit(solution)/shard_map/ppermute | solution.py:384
  378.4 33.5 %copy-start.6 = (f32[96,768]{1,0:T(8,128)S(1)}, f32[96,768]{1,0:T(8,128)}, u32[]{:S(2)}) copy-start(f32[96,768]{1,0:T(8,128)} %param.26) | copy-start | bytes 884740
  378.4 33.5 %copy-start.11 = (f32[96,768]{1,0:T(8,128)S(1)}, f32[96,768]{1,0:T(8,128)}, u32[]{:S(2)}) copy-start(f32[96,768]{1,0:T(8,128)} %param.35) | copy-start | bytes 884740
  378.4 33.5 %copy-start.12 = (f32[96,768]{1,0:T(8,128)S(1)}, f32[96,768]{1,0:T(8,128)}, u32[]{:S(2)}) copy-start(f32[96,768]{1,0:T(8,128)} %param.34) | copy-start | bytes 884740
  378.4 6.8 %collective-permute-start.11 = (bf16[80,768]{1,0:T(8,128)(2,1)S(1)}, bf16[80,768]{1,0:T(8,128)(2,1)S(1)}, u32[]{:S(2)}, u32[]{:S(2)}) collective-permute-start(bf16[80,768]{1,0:T(8,128)(2,1)S(1)} %get-tuple-element.84), channel_id=1, source_target_pairs={{0,2},{1,3},{2,0},{3,1},{4,6},{5,7},{6,4},{7,5},{8,10},{9,11},{10,... | collective-permute-start | bytes 368648 | tf_op jit(solution)/shard_map/ppermute | solution.py:384
  379.8 12.4 %collective-permute-start.12 = (bf16[80,768]{1,0:T(8,128)(2,1)S(1)}, bf16[80,768]{1,0:T(8,128)(2,1)S(1)}, u32[]{:S(2)}, u32[]{:S(2)}) collective-permute-start(bf16[80,768]{1,0:T(8,128)(2,1)S(1)} %get-tuple-element.86), channel_id=1, source_target_pairs={{0,4},{1,5},{2,6},{3,7},{4,0},{5,1},{6,2},{7,3},{8,12},{9,13},{10,... | collective-permute-start | bytes 368648 | tf_op jit(solution)/shard_map/ppermute | solution.py:384
  382.4 9.9 %collective-permute-start.13 = (bf16[80,768]{1,0:T(8,128)(2,1)S(1)}, bf16[80,768]{1,0:T(8,128)(2,1)S(1)}, u32[]{:S(2)}, u32[]{:S(2)}) collective-permute-start(bf16[80,768]{1,0:T(8,128)(2,1)S(1)} %get-tuple-element.85), channel_id=1, source_target_pairs={{0,6},{1,7},{2,4},{3,5},{4,2},{5,3},{6,0},{7,1},{8,14},{9,15},{10,... | collective-permute-start | bytes 368648 | tf_op jit(solution)/shard_map/ppermute | solution.py:384
  400.5 11.1 %all-to-all-start = ((f32[32,1,128]{2,1,0:T(1,128)}), f32[32,1,128]{2,1,0:T(1,128)S(1)}, u32[]{:S(2)}, u32[]{:S(2)}) async-start(f32[32,1,128]{2,1,0:T(1,128)} %broadcast_in_dim.3), calls=%async_computation.1 | async-start | bytes 32768 | tf_op jit(solution)/shard_map/all_to_all | solution.py:524
  (15 other events, 82.6 us)
Sparse Core Ops, SparseCore 0:
  11.6 98.1 all-gather.2
  222.6 153.9 reduce-scatter.1

commit v3 on v2

v3 whole, which is shorter than its diff:
```python
import functools
import math

import jax
import jax.numpy as jnp
from jax import lax
from jax.experimental import pallas as pl
from jax.experimental.pallas import tpu as pltpu
from jax.sharding import PartitionSpec as P

D = 768
FF = 3072
NORM_EPS = 1e-06
BETA_ONE = 0.9
BETA_TWO = 0.999
ADAM_EPS = 1e-08
CLIP_LIMIT = 3.0
AXES = ("dp", "fsdp")
PACK = 32
bf = jnp.bfloat16
f32 = jnp.float32


def nt(a, b):
    return lax.dot_general(a, b, (((1,), (1,)), ((), ())), preferred_element_type=f32)


def nn(a, b):
    return jnp.dot(a, b, preferred_element_type=f32)


def tn(a, b):
    return lax.dot_general(a, b, (((0,), (0,)), ((), ())), preferred_element_type=f32)


ROW=1536
BQ=256
NQ=ROW//BQ
SEGS=6
LOG2E=1.4426950408889634
BIG=float(2**30)


def seg_onehot(len_ref):
    lane=lax.broadcasted_iota(jnp.int32,(1,128),1)
    start=jnp.zeros((1,128),jnp.int32); stop=jnp.zeros((1,128),jnp.int32)
    end=jnp.int32(0)
    for s in range(SEGS):
        start=jnp.where(lane==s,end,start)
        end=end+len_ref[0,s]
        stop=jnp.where(lane==s,end,stop)
    start=jnp.where(lane==SEGS,end,start)
    stop=jnp.where(lane==SEGS,ROW,stop)
    pos=lax.broadcasted_iota(jnp.int32,(ROW,128),0)
    return jnp.where((pos>=start)&(pos<stop),1.0,0.0)


def segments(len_ref,seg,mask):
    @pl.when(pl.program_id(0)==0)
    def _():
        oh=seg_onehot(len_ref)
        seg[...]=oh.astype(bf)
        mask[...]=((oh-1.0)*BIG).astype(bf)


def half(v,r):
    low=lax.broadcasted_iota(jnp.int32,v.shape,1)<64
    return jnp.where(low,v,jnp.zeros_like(v)) if r==0 else jnp.where(low,jnp.zeros_like(v),v)


MAIN=1376
CHUNKS=((0,256),(256,512),(512,768),(768,1024),(1024,MAIN))
LAST=slice(ROW-BQ,ROW)
TAIL=slice(MAIN,ROW)
EIGHTH=0.125


def tile_rows(j):
    return pl.ds(pl.multiple_of(j*BQ,BQ),BQ)


def fwd_kernel(len_ref,qkv_ref,o_ref,lse_ref,seg,mask,va,vb,sa,sb,ma,mb,ot,last):
    segments(len_ref,seg,mask)
    q_ref,k_ref,v_ref=(qkv_ref.at[:,128*b:128*b+128] for b in range(3))
    def query(rows,r):
        return jnp.concatenate([half(q_ref[rows,:]*jnp.asarray(EIGHTH,bf),r),seg[rows,:]],axis=1)
    def keys(rows):
        return jnp.concatenate([k_ref[rows,:],mask[rows,:]],axis=1)
    vt=v_ref[...].T
    one=(lax.broadcasted_iota(jnp.int32,(16,ROW),0)==0).astype(bf)
    va[64:80,:]=one; vb[64:80,:]=one
    va[0:64,:]=vt[0:64,:]; vb[0:64,:]=vt[64:128,:]
    for r,v_sc in enumerate((va,vb)):
        s=nt(keys(TAIL),query(LAST,r))*LOG2E
        m=jnp.max(s,axis=0,keepdims=True)
        o=nn(v_sc[:,TAIL],jnp.exp2(s-m).astype(bf))
        last[72*r:72*r+64,:]=o[0:64,:]*(1.0/o[64:65,:])
        last[72*r+64:72*r+65,:]=m+jnp.log2(o[64:65,:])
    def first(rows,r,s_sc,m_sc):
        q=query(rows,r)
        m=None
        for lo,hi in CHUNKS:
            s=nt(keys(slice(lo,hi)),q)
            s_sc[lo:hi,:]=s
            t=jnp.max(s,axis=0,keepdims=True)
            m=t if m is None else jnp.maximum(m,t)
        m_sc[0:1,:]=m*LOG2E
    def step(s_sc,m_sc,v_sc,j,r,rows,r2,s_next,m_next):
        q=query(rows,r2)
        m=m_sc[0:1,:]
        top=None
        o=0.0
        for lo,hi in CHUNKS:
            s=nt(keys(slice(lo,hi)),q)
            s_next[lo:hi,:]=s
            t=jnp.max(s,axis=0,keepdims=True)
            top=t if top is None else jnp.maximum(top,t)
        m_next[0:1,:]=top*LOG2E
        for lo,hi in CHUNKS:
            o=o+nn(v_sc[:,lo:hi],jnp.exp2(s_sc[lo:hi,:]*LOG2E-m).astype(bf))
        l=o[64:65,:]
        cols=tile_rows(j)
        ot[64*r:64*r+64,cols]=o[0:64,:]*(1.0/l)
        lse_ref[0,r:r+1,cols]=m+jnp.log2(l)
    first(pl.ds(0,BQ),0,sa,ma)
    def body(j,c):
        step(sa,ma,va,j,0,tile_rows(j),1,sb,mb)
        step(sb,mb,vb,j,1,tile_rows(jnp.minimum(j+1,NQ-1)),0,sa,ma)
        return c
    lax.fori_loop(0,NQ,body,0)
    for r in range(2):
        old=lse_ref[0,r:r+1,LAST]
        lse=last[72*r+64:72*r+65,:]
        top=jnp.maximum(old,lse)
        a=jnp.exp2(old-top); b=jnp.exp2(lse-top); t=1.0/(a+b)
        ot[64*r:64*r+64,LAST]=ot[64*r:64*r+64,LAST]*(a*t)+last[72*r:72*r+64,:]*(b*t)
        lse_ref[0,r:r+1,LAST]=top-jnp.log2(t)
    o_ref[...]=ot[...].T.astype(bf)


def attn_fwd(lengths,qkv):
    blk=lambda width: pl.BlockSpec((ROW,width),lambda h:(0,h))
    return pl.pallas_call(fwd_kernel,grid=(6,),
        in_specs=[pl.BlockSpec(memory_space=pltpu.SMEM),blk(384)],
        out_specs=[blk(128),pl.BlockSpec((1,8,ROW),lambda h:(h,0,0))],
        out_shape=[jax.ShapeDtypeStruct((ROW,768),bf),jax.ShapeDtypeStruct((6,8,ROW),f32)],
        scratch_shapes=[pltpu.VMEM((ROW,128),bf)]*2+[pltpu.VMEM((80,ROW),bf)]*2+[pltpu.VMEM((MAIN,BQ),f32)]*2+[pltpu.VMEM((8,BQ),f32)]*2
          +[pltpu.VMEM((128,ROW),f32),pltpu.VMEM((144,BQ),f32)],
        compiler_params=pltpu.CompilerParams(vmem_limit_bytes=60<<20),name="attn_fwd",
        cost_estimate=pl.CostEstimate(flops=4*ROW*ROW*D,bytes_accessed=10<<20,transcendentals=12*ROW*ROW))(lengths,qkv)


def bwd_kernel(len_ref,qkv_ref,o_ref,do_ref,lse_ref,d_ref,
               seg,mask,kt,xa,ya,xb,yb,dqt,dqe,dka,dva):
    segments(len_ref,seg,mask)
    q_ref,k_ref,v_ref=(qkv_ref.at[:,128*b:128*b+128] for b in range(3))
    kt[...]=k_ref[...].T
    def query(rows,r):
        return half(q_ref[rows,:]*jnp.asarray(EIGHTH,bf),r)
    def keys(rows):
        return jnp.concatenate([k_ref[rows,:],mask[rows,:]],axis=1)
    def rowsums(rows):
        t=(do_ref[rows,:].astype(f32)*o_ref[rows,:].astype(f32)).T
        return [jnp.sum(t[64*r:64*r+64],axis=0,keepdims=True) for r in range(2)]
    def products(rows,r,span,x,y):
        q=jnp.concatenate([query(rows,r),seg[rows,:]],axis=1); d=half(do_ref[rows,:],r)
        for lo,hi in span:
            x[lo:hi,:]=nt(keys(slice(lo,hi)),q)
            y[lo:hi,:]=nt(v_ref[lo:hi,:],d)
    def grads(x,y,lse,total):
        p=jnp.exp2(x*LOG2E-lse)
        return p.astype(bf),(p*(y-total)).astype(bf)
    sums=rowsums(LAST)
    dv=0.0; dk=0.0
    for r in range(2):
        q=query(LAST,r); d=half(do_ref[LAST,:],r)
        p,ds=grads(nt(keys(TAIL),jnp.concatenate([q,seg[LAST,:]],axis=1)),nt(v_ref[TAIL,:],d),lse_ref[0,r:r+1,LAST],sums[r])
        dv=dv+nn(p,d); dk=dk+nn(ds,q)
        dqe[64*r:64*r+64,:]=nn(kt[64*r:64*r+64,TAIL],ds)
    dva[TAIL,:]=dv; dka[TAIL,:]=dk
    dva[0:MAIN,:]=jnp.zeros((MAIN,128),f32); dka[0:MAIN,:]=jnp.zeros((MAIN,128),f32)
    def rest(x,y,r,rows,total):
        q=query(rows,r); d=half(do_ref[rows,:],r); lse=lse_ref[0,r:r+1,rows]
        dq=0.0
        for lo,hi in CHUNKS:
            p,ds=grads(x[lo:hi,:],y[lo:hi,:],lse,total)
            dva[lo:hi,:]+=nn(p,d)
            dka[lo:hi,:]+=nn(ds,q)
            dq=dq+nn(kt[64*r:64*r+64,lo:hi],ds)
        dqt[64*r:64*r+64,rows]=dq
    def body(j,c):
        rows=tile_rows(j)
        sums=rowsums(rows)
        products(rows,0,CHUNKS,xa,ya)
        products(rows,1,CHUNKS,xb,yb)
        rest(xa,ya,0,rows,sums[0])
        rest(xb,yb,1,rows,sums[1])
        return c
    lax.fori_loop(0,NQ,body,0)
    dqt[:,LAST]+=dqe[...]
    d_ref[:,0:128]=(dqt[...].T*EIGHTH).astype(bf)
    d_ref[:,128:256]=dka[...].astype(bf)
    d_ref[:,256:384]=dva[...].astype(bf)


def attn_bwd(lengths,qkv,o,do,lse):
    blk=lambda width: pl.BlockSpec((ROW,width),lambda h:(0,h))
    return pl.pallas_call(bwd_kernel,grid=(6,),
        in_specs=[pl.BlockSpec(memory_space=pltpu.SMEM),blk(384),blk(128),blk(128),pl.BlockSpec((1,8,ROW),lambda h:(h,0,0))],
        out_specs=blk(384),
        out_shape=jax.ShapeDtypeStruct((ROW,3*D),bf),
        scratch_shapes=[pltpu.VMEM((ROW,128),bf)]*2+[pltpu.VMEM((128,ROW),bf)]+[pltpu.VMEM((MAIN,BQ),f32)]*4
          +[pltpu.VMEM((128,ROW),f32),pltpu.VMEM((128,BQ),f32)]+[pltpu.VMEM((ROW,128),f32)]*2,
        compiler_params=pltpu.CompilerParams(vmem_limit_bytes=62<<20),name="attn_bwd",
        cost_estimate=pl.CostEstimate(flops=10*ROW*ROW*D,bytes_accessed=20<<20,transcendentals=12*ROW*ROW))(lengths,qkv,o,do,lse)


BM=512
INV_SQRT2=0.7071067811865476
INV_SQRT_2PI=0.3989422804014327
VMEM_CAP=62<<20


def norm_stats(v):
    center=v-jnp.mean(v,axis=1,keepdims=True)
    rstd=lax.rsqrt(jnp.mean(center*center,axis=1,keepdims=True)+NORM_EPS)
    return center*rstd,rstd


def params(**kw):
    return pltpu.CompilerParams(vmem_limit_bytes=VMEM_CAP,**kw)


def once(shape,index=None):
    return pl.BlockSpec(shape,index or (lambda i:(0,)*len(shape)),pipeline_mode=pl.Buffered(1))


def tile(width):
    return pl.BlockSpec((BM,width),lambda i:(i,0))


WIDE=3*D+128


def norm_kernel(x_ref,n_ref,r_ref):
    n,r=norm_stats(x_ref[...].astype(f32))
    n_ref[...]=n
    r_ref[...]=jnp.broadcast_to(r,r_ref.shape)


def norm_input(x):
    rows=x.shape[0]
    return pl.pallas_call(norm_kernel,grid=(rows//BM,),
        in_specs=[tile(D)],out_specs=[tile(D),tile(128)],
        out_shape=[jax.ShapeDtypeStruct((rows,D),f32),jax.ShapeDtypeStruct((rows,128),f32)],
        compiler_params=params(),name="norm_input",
        cost_estimate=pl.CostEstimate(flops=12*rows*D,bytes_accessed=8<<20,transcendentals=0))(x)


def qkv_kernel(n_ref,w_ref,v_ref,h_ref,qkv_ref,vec_ref):
    @pl.when(pl.program_id(0)==0)
    def _():
        vec_ref[...]=v_ref[...].reshape(D,128).astype(f32).T[0:16]
    h=(n_ref[...]*vec_ref[0:1,:]+vec_ref[1:2,:]).astype(bf)
    h_ref[...]=h
    zero=jnp.zeros((1,128),f32)
    bias=jnp.concatenate([b for p in range(6) for b in (vec_ref[2:3,128*p:128*p+128],zero,vec_ref[3:4,128*p:128*p+128])],axis=1)
    qkv_ref[...]=(nn(h,w_ref[...].reshape(D,3*D))+bias).astype(bf)


def packed_specs(w):
    n,r=w.shape[:2]
    return [once((n,r,3*D),lambda i:(0,0,0)),once((n,r,128),lambda i:(0,0,3*D//128))]


def qkv_forward(n,w):
    rows=n.shape[0]
    sd=jax.ShapeDtypeStruct
    return pl.pallas_call(qkv_kernel,grid=(rows//BM,),
        in_specs=[tile(D)]+packed_specs(w),
        out_specs=[tile(D),tile(3*D),pl.BlockSpec((16,D),lambda i:(0,0))],
        out_shape=[sd((rows,D),bf),sd((rows,3*D),bf),sd((16,D),f32)],
        compiler_params=params(),name="qkv_forward",
        cost_estimate=pl.CostEstimate(flops=2*rows*D*3*D,bytes_accessed=18<<20,transcendentals=0))(n,w,w)


CH=768


def mlp_kernel(x_ref,o_ref,dy_ref,vec_ref,w2_ref,wa_ref,wb_ref,wc_ref,wd_ref,wp_ref,
               out_ref,h_ref,dm_ref,z_ref,du_ref,dx_ref,da_ref,do_ref,sum_ref,
               a_s,x1_s,n2_s,mo_s,dh_s,ua,ub,ga,gb,w1_s):
    step=pl.program_id(0)
    @pl.when(step==0)
    def _():
        for b,ref in enumerate((wa_ref,wb_ref,wc_ref,wd_ref)):
            w1_s[b]=ref[...].reshape(D,D)
        sum_ref[...]=jnp.zeros_like(sum_ref)
    row=lambda i: vec_ref[i:i+1,:]
    def add(i,v):
        sum_ref[i:i+1,:]+=jnp.sum(v,axis=0,keepdims=True)
    wp=wp_ref[...].reshape(D,D)
    a=nn(o_ref[...],wp)+row(4)
    a_s[...]=a
    x1=x_ref[...].astype(f32)+row(5)*a
    x1_s[...]=x1
    n2,r2=norm_stats(x1)
    n2_s[...]=n2
    h=(n2*row(6)+row(7)).astype(bf)
    h_ref[...]=h
    dm=(row(13)*dy_ref[...].astype(f32)).astype(bf)
    dm_ref[...]=dm
    add(12,dm.astype(f32))
    mo_s[...]=jnp.zeros_like(mo_s)
    dh_s[...]=jnp.zeros_like(dh_s)
    def w2(c):
        return w2_ref[pl.ds(8*c,8)].reshape(D,D)
    def up(c,u,g):
        u[...]=nn(h_ref[...],w1_s[c])
        g[...]=nt(dm_ref[...],w2(c))
    def down(c,u,g):
        cols=pl.ds(pl.multiple_of(c*CH,CH),CH)
        v=u[...]+vec_ref[pl.ds(8+c,1),:]
        cdf=0.5+0.5*lax.erf(v*INV_SQRT2)
        z=(v*cdf).astype(bf)
        z_ref[:,cols]=z
        slope=cdf+v*(INV_SQRT_2PI*jnp.exp(v*v*(-0.5)))
        du=(g[...]*slope).astype(bf)
        du_ref[:,cols]=du
        sum_ref[pl.ds(8+c,1),:]+=jnp.sum(du.astype(f32),axis=0,keepdims=True)
        mo_s[...]+=nn(z,w2(c))
        dh_s[...]+=nt(du,w1_s[c])
    def body(i,carry):
        up(2*i,ua,ga)
        up(2*i+1,ub,gb)
        down(2*i,ua,ga)
        down(2*i+1,ub,gb)
        return carry
    lax.fori_loop(0,FF//CH//2,body,0)
    mo=mo_s[...]+row(12)
    out_ref[...]=(x1_s[...]+row(13)*mo).astype(bf)
    dy=dy_ref[...].astype(f32)
    add(13,dy*mo)
    dh=dh_s[...]; n2=n2_s[...]
    add(6,dh*n2); add(7,dh)
    t=dh*row(6)
    dx=dy+r2*(t-jnp.mean(t,axis=1,keepdims=True)-n2*jnp.mean(t*n2,axis=1,keepdims=True))
    dx_ref[...]=dx
    add(5,dx*a_s[...])
    da=(row(5)*dx).astype(bf)
    da_ref[...]=da
    add(4,da.astype(f32))
    do_ref[...]=nt(da,wp_ref[...].reshape(D,D)).astype(bf)


def mlp_block(x,o,dy,vec,packed):
    rows=x.shape[0]
    n,r=packed.shape[0],D//packed.shape[0]
    sd=jax.ShapeDtypeStruct
    return pl.pallas_call(mlp_kernel,grid=(rows//BM,),
        in_specs=[tile(D),tile(D),tile(D),once((16,D)),once((n,4*r,D))]+[once((n,r,D),lambda i,b=b:(0,b,0)) for b in range(4,9)],
        out_specs=[tile(D),tile(D),tile(D),tile(FF),tile(FF),tile(D),tile(D),tile(D),pl.BlockSpec((16,D),lambda i:(0,0))],
        out_shape=[sd((rows,D),bf),sd((rows,D),bf),sd((rows,D),bf),sd((rows,FF),bf),sd((rows,FF),bf),sd((rows,D),f32),sd((rows,D),bf),sd((rows,D),bf),sd((16,D),f32)],
        scratch_shapes=[pltpu.VMEM((BM,D),f32)]*5+[pltpu.VMEM((BM,CH),f32)]*4+[pltpu.VMEM((4,D,D),bf)],
        compiler_params=params(),name="mlp_block",
        cost_estimate=pl.CostEstimate(flops=2*rows*D*(2*D+4*FF),bytes_accessed=48<<20,transcendentals=0))(x,o,dy,vec,*[packed]*6)


def outer_kernel(a_ref,b_ref,g_ref):
    g_ref[...]=tn(a_ref[...],b_ref[...]).reshape(g_ref.shape).astype(bf)


def fc2_grad(z,dm,n,extra):
    rows=z.shape[0]
    per=FF//n
    return pl.pallas_call(outer_kernel,grid=(FF//D,),
        in_specs=[pl.BlockSpec((rows,D),lambda i:(0,i)),once((rows,D))],
        out_specs=pl.BlockSpec((n*D//FF,per,D),lambda i:(i,0,0)),
        out_shape=jax.ShapeDtypeStruct((n,per+extra,D),bf),
        compiler_params=params(),name="fc2_grad",
        cost_estimate=pl.CostEstimate(flops=2*rows*D*FF,bytes_accessed=16<<20,transcendentals=0))(z,dm)


def fc1_proj_kernel(h_ref,du_ref,o_ref,da_ref,old_ref,g_ref):
    i=pl.program_id(0)
    @pl.when(i<4)
    def _():
        g_ref[...]=tn(h_ref[...],du_ref[...]).reshape(g_ref.shape).astype(bf)
    @pl.when(i==4)
    def _():
        g_ref[...]=tn(o_ref[...],da_ref[...]).reshape(g_ref.shape).astype(bf)


def fc1_proj_grad(h,du,o,da,packed):
    rows=h.shape[0]
    n=packed.shape[0]; r=D//n
    base=packed.shape[1]//r-5
    return pl.pallas_call(fc1_proj_kernel,grid=(5,),
        in_specs=[once((rows,D)),pl.BlockSpec((rows,D),lambda i:(0,jnp.minimum(i,3))),once((rows,D)),once((rows,D)),pl.BlockSpec(memory_space=pl.ANY)],
        out_specs=pl.BlockSpec((n,r,D),lambda i:(0,base+i,0)),
        out_shape=jax.ShapeDtypeStruct(packed.shape,bf),input_output_aliases={4:0},
        compiler_params=params(),name="fc1_proj_grad",
        cost_estimate=pl.CostEstimate(flops=2*rows*D*(FF+D),bytes_accessed=24<<20,transcendentals=0))(h,du,o,da,packed)


def qkv_grad_kernel(core_ref,h_ref,d_ref,sum_ref,mine_ref,other_ref):
    i=pl.program_id(0)
    even=core_ref[0]==0
    def put(v,cols):
        v=v.reshape(mine_ref.shape[0],2,mine_ref.shape[1],v.shape[1])
        mine_ref[:,:,cols]=jnp.where(even,v[:,0],v[:,1]).astype(bf)
        other_ref[:,:,cols]=jnp.where(even,v[:,1],v[:,0]).astype(bf)
    @pl.when(i==0)
    def _():
        sums=jnp.concatenate([sum_ref[...],jnp.zeros((112,D),f32)],axis=0)
        put(sums.T,slice(3*D,WIDE))
    put(tn(h_ref[...],d_ref[...]),pl.ds(pl.multiple_of(i*D,D),D))


def qkv_grad(core,h,d,sums):
    rows=h.shape[0]
    half_shape=(PACK//2,D//PACK,WIDE)
    out=pl.BlockSpec(half_shape,lambda i:(0,0,0))
    return pl.pallas_call(qkv_grad_kernel,grid=(3,),
        in_specs=[pl.BlockSpec(memory_space=pltpu.SMEM),once((rows,D)),pl.BlockSpec((rows,D),lambda i:(0,i)),once((16,D))],
        out_specs=[out,out],
        out_shape=[jax.ShapeDtypeStruct(half_shape,bf)]*2,
        compiler_params=params(),name="qkv_grad",
        cost_estimate=pl.CostEstimate(flops=2*rows*D*3*D,bytes_accessed=14<<20,transcendentals=0))(core,h,d,sums)


def input_kernel(n_ref,r_ref,d_ref,dx1_ref,vec_ref,old_ref,w_ref,gx_ref,sum_ref):
    @pl.when(pl.program_id(0)==0)
    def _():
        sum_ref[...]=old_ref[...]
    def add(i,v):
        sum_ref[i:i+1,:]+=v
    d=d_ref[...]
    dh=nt(d,w_ref[...].reshape(D,3*D))
    total=jnp.sum(d.astype(f32),axis=0,keepdims=True)
    n=n_ref[...]; r=r_ref[:,0:1]
    add(0,jnp.sum(dh*n,axis=0,keepdims=True))
    add(1,jnp.sum(dh,axis=0,keepdims=True))
    for i,b in ((2,0),(3,2)):
        add(i,jnp.concatenate([total[:,384*p+128*b:384*p+128*b+128] for p in range(6)],axis=1))
    t=dh*vec_ref[0:1,:]
    dx=dx1_ref[...]+r*(t-jnp.mean(t,axis=1,keepdims=True)-n*jnp.mean(t*n,axis=1,keepdims=True))
    gx_ref[...]=dx.astype(bf)


def input_grad(n,r,d,dx1,vec,sums,w):
    rows=n.shape[0]
    return pl.pallas_call(input_kernel,grid=(rows//BM,),
        in_specs=[tile(D),tile(128),tile(3*D),tile(D),once((16,D)),once((16,D))]+packed_specs(w)[:1],
        out_specs=[tile(D),pl.BlockSpec((16,D),lambda i:(0,0))],
        out_shape=[jax.ShapeDtypeStruct((rows,D),bf),jax.ShapeDtypeStruct((16,D),f32)],
        compiler_params=params(),name="input_grad",
        cost_estimate=pl.CostEstimate(flops=2*rows*D*3*D,bytes_accessed=24<<20,transcendentals=0))(n,r,d,dx1,vec,sums,w)


def stage_kernel(count,place_ref,*refs):
    ins,outs=refs[:count],refs[count:]
    for k,out in enumerate(outs):
        at=place_ref[0]^k
        out[...]=sum(ref[at].astype(f32) for ref in ins).astype(bf)


def stage_sum(place,parts):
    shape=parts[0].shape
    whole=lambda s: pl.BlockSpec(s,lambda i:(0,)*len(s))
    return pl.pallas_call(functools.partial(stage_kernel,len(parts)),grid=(1,),
        in_specs=[pl.BlockSpec(memory_space=pltpu.SMEM)]+[whole(shape)]*len(parts),
        out_specs=[whole(shape[1:])]*4,
        out_shape=[jax.ShapeDtypeStruct(shape[1:],bf)]*4,
        compiler_params=params(),name="stage_sum")(place,*parts)


def finish_kernel(a_ref,b_ref,c_ref,d_ref,rest_ref,g_ref,square_ref):
    g=sum(ref[...].astype(f32) for ref in (a_ref,b_ref,c_ref,d_ref))
    g_ref[...]=g
    rest=rest_ref[...].astype(f32)
    total=jnp.sum(g*g,keepdims=True)+jnp.sum(rest*rest,keepdims=True)
    square_ref[...]=jnp.broadcast_to(total,square_ref.shape)


def finish_sum(parts,rest):
    whole=lambda s: pl.BlockSpec(s,lambda i:(0,)*len(s))
    shape=parts[0].shape
    return pl.pallas_call(finish_kernel,grid=(1,),
        in_specs=[whole(shape)]*4+[whole(rest.shape)],
        out_specs=[whole(shape),whole((PACK,128))],
        out_shape=[jax.ShapeDtypeStruct(shape,f32),jax.ShapeDtypeStruct((PACK,128),f32)],
        compiler_params=params(),name="finish_sum")(*parts,rest)


def adam_update(weight, grad, first, second, rate, decay, fix_one, fix_two):
    first = BETA_ONE * first + (1.0 - BETA_ONE) * grad
    second = BETA_TWO * second + (1.0 - BETA_TWO) * grad * grad
    stride = first / fix_one / (jnp.sqrt(second / fix_two) + ADAM_EPS)
    return (weight - rate * (stride + decay * weight), first, second)


def split_columns(shard):
    r, width = shard.shape
    return jnp.concatenate([shard[:, b * D : (b + 1) * D] for b in range(width // D)], axis=0)


def join_columns(block, r):
    return jnp.concatenate([block[b * r : (b + 1) * r] for b in range(block.shape[0] // r)], axis=1)


def pack_rows(full):
    k = full.shape[1] // D
    return full.reshape(PACK, D // PACK, k, D).transpose(0, 2, 1, 3).reshape(PACK, -1, D)


def unpack_rows(packed):
    k = packed.shape[1] * PACK // D
    return packed.reshape(PACK, k, D // PACK, D).transpose(0, 2, 1, 3).reshape(D, k * D)


def swap(value, axis, size, flip):
    return lax.ppermute(value, axis, [(i, i ^ flip) for i in range(size)])


def by_xor(parts, me):
    if len(parts) == 2:
        odd = me % 2 == 1
        return jnp.stack([jnp.where(odd, parts[1], parts[0]), jnp.where(odd, parts[0], parts[1])])
    low, high = (me % 2 == 1, me // 2 == 1)
    return jnp.stack(
        [
            jnp.where(high, jnp.where(low, parts[j ^ 3], parts[j ^ 2]), jnp.where(low, parts[j ^ 1], parts[j]))
            for j in range(4)
        ]
    )


def places():
    inner = lax.axis_index("fsdp")
    return (lax.axis_index("dp"), inner // 2, inner % 2)


def gather_direct(shard):
    me_dp, me_z, me_core = places()
    part = by_xor([shard] + [swap(shard, "fsdp", 8, 2 * k) for k in (1, 2, 3)], me_z)
    part = by_xor([part] + [swap(part, "dp", 4, k) for k in (1, 2, 3)], me_dp)
    part = by_xor([part, swap(part, "fsdp", 8, 1)], me_core)
    return part.transpose(1, 2, 0, 3, 4).reshape(PACK, *shard.shape)


def scatter_direct(mine, other):
    me_dp, me_z, _ = places()
    got = swap(other, "fsdp", 8, 1)
    shape = (4, 4) + mine.shape[1:]
    keep, *send = stage_sum(me_dp.reshape(1), [mine.reshape(shape), got.reshape(shape)])
    parts = [swap(v, "dp", 4, k + 1) for k, v in enumerate(send)]
    keep, *send = stage_sum(me_z.reshape(1), [keep] + parts)
    return [keep] + [swap(v, "fsdp", 8, 2 * k + 2) for k, v in enumerate(send)]


def to_pairs(w):
    return w.reshape(-1, 3, 6, 128).transpose(0, 2, 1, 3).reshape(-1, 3 * D)


def from_pairs(w):
    return w.reshape(-1, 6, 3, 128).transpose(0, 2, 1, 3).reshape(-1, 3 * D)


def make_local(fast):
    def gather(shard):
        return lax.all_gather(shard, AXES, axis=0, tiled=True)

    def scatter(full):
        return lax.psum_scatter(full, AXES, scatter_dimension=0, tiled=True)

    def local(
        tokens,
        cotangent,
        lengths,
        step,
        weight_qkv,
        weight_proj,
        weight_fc1,
        weight_fc2,
        vectors,
        first_qkv,
        second_qkv,
        first_proj,
        second_proj,
        first_fc1,
        second_fc1,
        first_fc2,
        second_fc2,
        first_vectors,
        second_vectors,
    ):
        per = weight_qkv.shape[0]
        cols = vectors.shape[1]
        low = [w.astype(bf) for w in (weight_qkv, weight_proj, weight_fc1, weight_fc2, vectors)]
        first = jnp.concatenate([to_pairs(low[0]), jnp.pad(low[4], ((0, 0), (0, 128 - cols)))], axis=1)
        if fast:
            mats_qkv = gather_direct(first)
            rest = lax.all_gather(
                jnp.concatenate([low[3], split_columns(low[2]), low[1]], axis=0), AXES, axis=0, tiled=False
            )
        else:
            mats_qkv = gather(first).reshape(PACK, D // PACK, WIDE)
            full = [gather(w) for w in low[1:4]]
            rest = jnp.concatenate(
                [full[2].reshape(PACK, FF // PACK, D), pack_rows(full[1]), pack_rows(full[0])], axis=1
            )
        rows_dev, row, _ = tokens.shape
        count = rows_dev * row
        inputs = tokens.reshape(count, D)
        centered, spread = norm_input(inputs)
        normed, qkv, vec = qkv_forward(centered, mats_qkv)
        each = lambda v, b: v[b * row : (b + 1) * row]
        done = [attn_fwd(lengths[b : b + 1], each(qkv, b)) for b in range(rows_dev)]
        mixed = jnp.concatenate([o for o, _ in done], axis=0)
        result, normed_two, grad_down, active, grad_inner, grad_middle, grad_branch, grad_mixed, sums = mlp_block(
            inputs, mixed, cotangent.reshape(count, D), vec, rest
        )
        grads = fc2_grad(active, grad_down, PACK, 5 * D // PACK)
        grads = fc1_proj_grad(normed_two, grad_inner, mixed, grad_branch, grads)
        if fast:
            rest_owned = lax.psum_scatter(grads, AXES, scatter_dimension=0, tiled=False)
        back = [
            attn_bwd(lengths[b : b + 1], each(qkv, b), done[b][0], each(grad_mixed, b), done[b][1])
            for b in range(rows_dev)
        ]
        grad_qkv = jnp.concatenate(back, axis=0)
        grad_inputs, sums = input_grad(centered, spread, grad_qkv, grad_middle, vec, sums, mats_qkv)
        core = places()[2].reshape(1) if fast else jnp.zeros((1,), jnp.int32)
        mine, other = qkv_grad(core, normed, grad_qkv, sums)
        if fast:
            first_owned, squares = finish_sum(scatter_direct(mine, other), rest_owned)
            rest_owned = rest_owned.astype(f32)
            owned = (
                from_pairs(first_owned[:, : 3 * D]),
                rest_owned[8 * per :],
                join_columns(rest_owned[4 * per : 8 * per], per),
                rest_owned[: 4 * per],
                first_owned[:, 3 * D : 3 * D + cols],
            )
            squares = jnp.sum(lax.all_to_all(squares, AXES, 0, 0, tiled=True), axis=0)[0]
        else:
            wide = FF // PACK
            grads_first = jnp.stack([mine, other], axis=1).reshape(D, WIDE)
            owned = (
                scatter(from_pairs(grads_first[:, : 3 * D])),
                scatter(unpack_rows(grads[:, 2 * wide :])),
                scatter(unpack_rows(grads[:, wide : 2 * wide])),
                scatter(grads[:, :wide].reshape(FF, D)),
                scatter(grads_first[:, 3 * D : 3 * D + cols]),
            )
            owned = tuple(g.astype(f32) for g in owned)
            squares = lax.psum(sum(jnp.sum(g * g) for g in owned), AXES)
        norm = jnp.sqrt(squares)
        factor = jnp.minimum(1.0, CLIP_LIMIT / (norm + 1e-06))
        taken = step[0].astype(f32)
        fix_one = 1.0 - jnp.power(BETA_ONE, taken)
        fix_two = 1.0 - jnp.power(BETA_TWO, taken)
        rate_in = 2.0 / math.sqrt(D)
        states = (
            (weight_qkv, first_qkv, second_qkv, rate_in, 0.04),
            (weight_proj, first_proj, second_proj, 2.0 / math.sqrt(D // 48), 0.04),
            (weight_fc1, first_fc1, second_fc1, rate_in, 0.04),
            (weight_fc2, first_fc2, second_fc2, 2.0 / math.sqrt(FF), 0.04),
            (vectors, first_vectors, second_vectors, 1.0, 0.0),
        )
        new = [
            adam_update(w, factor * g, m, v, rate, decay, fix_one, fix_two)
            for g, (w, m, v, rate, decay) in zip(owned, states)
        ]
        shape = (rows_dev, row, D)
        outs = [result.reshape(shape), grad_inputs.reshape(shape), norm.reshape(1)]
        outs += [w for w, _, _ in new]
        for _, m, v in new:
            outs += [m, v]
        return tuple(outs)

    return local


def solution(mesh):
    rows = P(AXES, None)
    tokens = P(AXES, None, None)
    fast = (mesh.shape["dp"], mesh.shape["fsdp"]) == (4, 8)
    return jax.shard_map(
        make_local(fast),
        mesh=mesh,
        in_specs=(tokens, tokens, rows, P()) + (rows,) * 15,
        out_specs=(tokens, tokens, P()) + (rows,) * 15,
        check_vma=False,
    )
```

time: 432 us -> 390 us (0.903); the launches traced: 425 us -> 389 us
  Pallas kernels: 259 us -> 245 us
  other arithmetic: 24.5 us -> 15.8 us
  waiting for transfers between devices: 87.5 us -> 82.4 us
    pallas_call x1, Pallas kernels: 87.8 us -> 73.2 us  [attn_bwd(): pl.pallas_call(bwd_kernel, grid=(6,), in_specs=[pl.BlockSpec(memory_space...]
    ppermute x14, waiting for transfers between devices: 81.1 us -> 68 us  [swap(): return lax.ppermute(value, axis, [(i, i ^ flip) for i in range(size)])]
    reduce_scatter x1, waiting for transfers between devices: 0.01 us -> 8.34 us  [local(): rest_owned = lax.psum_scatter(grads, AXES, scatter_dimension=0, tiled=False)]
    squeeze x4 -> x0, local copies, waits for them, and re-layouts: 4.43 us -> none  [the longest x2 3.51 us: of_core(): lax.dynamic_index_in_dim(v, core, 2, keepdims=False)]
    pallas_call x4 -> x8, Pallas kernels: 89.9 us -> 92.1 us  [the longest x1 44.8 us: attn_fwd(): pl.pallas_call(fwd_kernel, grid=(6,), in_specs=[pl.BlockSpec(memory_space...]
  transfers between devices with their start and end apart: 17 -> 17, of which waited for: 13 -> 13; matrix products, arithmetic and copies ran while one was open for 5% -> 3% of each run, Pallas kernels for 42% -> 42%
where the time goes in v3:
time: 390 us; the launch traced here: 389 us
  Pallas kernels  245 us (63%)
  waiting for transfers between devices  82.4 us (21%)
  starting transfers between devices  21.1 us (5%)
  between operations  16.4 us (4%)
  other arithmetic  15.8 us (4%)
  local copies, waits for them, and re-layouts  8.68 us (2%)
    pallas_call x1, Pallas kernels, attn_bwd(): pl.pallas_call(bwd_kernel, grid=(6,), in_specs=[pl.BlockSpec(memory_space...  73.2 us
    ppermute x14, waiting for transfers between devices, swap(): return lax.ppermute(value, axis, [(i, i ^ flip) for i in range(size)])  68 us
    pallas_call x1, Pallas kernels, mlp_block(): pl.pallas_call(mlp_kernel, grid=(rows // BM,), in_specs=[tile(D), tile(D)...  52.8 us
    pallas_call x1, Pallas kernels, attn_fwd(): pl.pallas_call(fwd_kernel, grid=(6,), in_specs=[pl.BlockSpec(memory_space...  44.8 us
    ppermute x14, starting transfers between devices, swap(): return lax.ppermute(value, axis, [(i, i ^ flip) for i in range(size)])  18.1 us
    pallas_call x1, Pallas kernels, fc1_proj_grad(): pl.pallas_call(fc1_proj_kernel, grid=(5,), in_specs=[once((rows, D)), pl....  15.3 us
    pallas_call x1, Pallas kernels, input_grad(): pl.pallas_call(input_kernel, grid=(rows // BM,), in_specs=[tile(D), tile(...  13 us
    pallas_call x1, Pallas kernels, fc2_grad(): pl.pallas_call(outer_kernel, grid=(FF // D,), in_specs=[pl.BlockSpec((row...  11.7 us
  transfers between devices with their start and end apart: 17, of which 13 were waited for; matrix products, arithmetic and copies ran while one was open for 3% of the time, Pallas kernels for 42%

profile of v3, /device:TPU:0, one launch (start us, length us, event | category | flops | bytes accessed | tf_op | source)
XLA Modules:
  0.0 389.5 jit_solution(17337988357861578166)
XLA Ops:
  12.4 5.1 %collective-permute-start = (bf16[24,2432]{1,0:T(8,128)(2,1)S(1)}, bf16[24,2432]{1,0:T(8,128)(2,1)S(1)}, u32[]{:S(2)}, u32[]{:S(2)}) collective-permute-start(bf16[24,2432]{1,0:T(8,128)(2,1)S(1)} %fusion.4), channel_id=1, source_target_pairs={{0,6},{1,7},{2,4},{3,5},{4,2},{5,3},{6,0},{7,1},{8,14},{9,15},{10,... | collective-permute-start | bytes 350216 | tf_op jit(solution)/shard_map/ppermute | solution.py:523
  18.1 3.5 collective-permute-done
  21.6 7.6 %collective-permute-done.1 = bf16[24,2432]{1,0:T(8,128)(2,1)S(1)} collective-permute-done((bf16[24,2432]{1,0:T(8,128)(2,1)S(1)}, bf16[24,2432]{1,0:T(8,128)(2,1)S(1)}, u32[]{:S(2)}, u32[]{:S(2)}) %collective-permute-start.1) | collective-permute-done | bytes 116768 | tf_op jit(solution)/shard_map/ppermute | solution.py:523
  29.4 2.8 collective-permute-start.3
  32.9 11.0 %collective-permute-done.3 = bf16[4,24,2432]{2,1,0:T(8,128)(2,1)S(1)} collective-permute-done((bf16[4,24,2432]{2,1,0:T(8,128)(2,1)S(1)}, bf16[4,24,2432]{2,1,0:T(8,128)(2,1)S(1)}, u32[]{:S(2)}, u32[]{:S(2)}) %collective-permute-start.3) | collective-permute-done | bytes 466976 | tf_op jit(solution)/shard_map/ppermute | solution.py:523
  44.0 6.5 %collective-permute-done.4 = bf16[4,24,2432]{2,1,0:T(8,128)(2,1)S(1)} collective-permute-done((bf16[4,24,2432]{2,1,0:T(8,128)(2,1)S(1)}, bf16[4,24,2432]{2,1,0:T(8,128)(2,1)S(1)}, u32[]{:S(2)}, u32[]{:S(2)}) %collective-permute-start.4) | collective-permute-done | bytes 466976 | tf_op jit(solution)/shard_map/ppermute | solution.py:523
  55.5 5.1 %norm_input.1 = (f32[1536,768]{1,0:T(8,128)}, f32[1536,128]{1,0:T(8,128)}) custom-call(bf16[1536,768]{1,0:T(8,128)(2,1)} %bitcast.47), custom_call_target="tpu_custom_call" | custom-call | flops 14155776 | bytes 8388608 | tf_op jit(solution)/shard_map/norm_input/pallas_call | solution.py:253
  65.1 10.6 %qkv_forward.1 = (bf16[1536,768]{1,0:T(8,128)(2,1)}, bf16[1536,2304]{1,0:T(8,128)(2,1)}, f32[16,768]{1,0:T(8,128)}) custom-call(f32[1536,768]{1,0:T(8,128)} %get-tuple-element.48.n_ref, bf16[32,24,2432]{2,1,0:T(8,128)(2,1)} %bitcast.44, bf16[32,24,2432]{2,1,0:T(8,128)(2,1)} %bitcast.45), custom_call_target="tpu_custom_call" | custom-call | flops 5435817984 | bytes 18874368 | tf_op jit(solution)/shard_map/qkv_forward/pallas_call | solution.py:279
  75.8 44.8 %attn_fwd.1 = (bf16[1536,768]{1,0:T(8,128)(2,1)}, f32[6,8,1536]{2,1,0:T(8,128)}) custom-call(s32[1,6]{1,0:T(1,128)} %len_ref.3, bf16[1536,2304]{1,0:T(8,128)(2,1)} %get-tuple-element.49.qkv_ref), custom_call_target="tpu_custom_call" | custom-call | flops 7247757312 | bytes 10485760 | tf_op jit(solution)/shard_map/attn_fwd/pallas_call | solution.py:143
  120.5 52.8 %mlp_block.1 = (bf16[1536,768]{1,0:T(8,128)(2,1)}, bf16[1536,768]{1,0:T(8,128)(2,1)}, bf16[1536,768]{1,0:T(8,128)(2,1)}, bf16[1536,3072]{1,0:T(8,128)(2,1)}, bf1...) custom-call(bf16[1536,768]{1,0:T(8,128)(2,1)} %bitcast.48, ...), custom_call_target="tpu_custom_call" | custom-call | flops 32614907904 | bytes 50331648 | tf_op jit(solution)/shard_map/mlp_block/pallas_call | solution.py:360
  173.3 11.7 %fc2_grad.1.old_ref = bf16[32,216,768]{2,1,0:T(8,128)(2,1)} custom-call(bf16[1536,3072]{1,0:T(8,128)(2,1)} %get-tuple-element.74.a_ref, bf16[1536,768]{1,0:T(8,128)(2,1)} %get-tuple-element.75.b_ref), custom_call_target="tpu_custom_call" | custom-call | flops 7247757312 | bytes 16777216 | tf_op jit(solution)/shard_map/fc2_grad/pallas_call | solution.py:376
  185.0 15.3 %fc1_proj_grad.1 = bf16[32,216,768]{2,1,0:T(8,128)(2,1)} custom-call(bf16[1536,768]{1,0:T(8,128)(2,1)} %get-tuple-element.71.h_ref, bf16[1536,3072]{1,0:T(8,128)(2,1)} %get-tuple-element.72.du_ref, bf16[1536,768]{1,0:T(8,128)(2,1)} %get-tuple-element.50.o_ref, bf16[1536,768]{1,0:T(8,128)(2,1)} %get-tuple-element.73.da_ref, ...), custom_call_target="tpu_custom_call", output_to_operand_aliasing={{}: (4, {})} | custom-call | flops 9059696640 | bytes 25165824 | tf_op jit(solution)/shard_map/fc1_proj_grad/pallas_call | solution.py:398
  200.3 73.2 %attn_bwd.1.d_ref = bf16[1536,2304]{1,0:T(8,128)(2,1)} custom-call(s32[1,6]{1,0:T(1,128)} %len_ref.3, bf16[1536,2304]{1,0:T(8,128)(2,1)} %get-tuple-element.49.qkv_ref, bf16[1536,768]{1,0:T(8,128)(2,1)} %get-tuple-element.50.o_ref, bf16[1536,768]{1,0:T(8,128)(2,1)} %get-tuple-element.54.do_ref, f32[6,8,1536]{2,1,0:T(8,128)} %get-tuple-element.55.lse_ref), custom_call_target="tpu_custom_call" | custom-call | flops 18119393280 | bytes 20971520 | tf_op jit(solution)/shard_map/attn_bwd/pallas_call | solution.py:208
  273.5 13.0 %input_grad.1 = (bf16[1536,768]{1,0:T(8,128)(2,1)}, f32[16,768]{1,0:T(8,128)}) custom-call(f32[1536,768]{1,0:T(8,128)} %get-tuple-element.48.n_ref, f32[1536,128]{1,0:T(8,128)} %get-tuple-element.53.r_ref, bf16[1536,2304]{1,0:T(8,128)(2,1)} %attn_bwd.1.d_ref, f32[1536,768]{1,0:T(8,128)} %get-tuple-element.56.dx1_ref, f32[16,768]{1,0:T(8,128)} %get-tuple-element.51.vec_ref, ...), custom_call_target="tpu_custom_call" | custom-call | flops 5435817984 | bytes 25165824 | tf_op jit(solution)/shard_map/input_grad/pallas_call | solution.py:453
  286.5 10.6 %qkv_grad.1 = (bf16[16,24,2432]{2,1,0:T(8,128)(2,1)}, bf16[16,24,2432]{2,1,0:T(8,128)(2,1)}) custom-call(s32[1]{0:T(128)} %bitcast.20.core_ref, bf16[1536,768]{1,0:T(8,128)(2,1)} %get-tuple-element.59.h_ref, bf16[1536,2304]{1,0:T(8,128)(2,1)} %attn_bwd.1.d_ref, f32[16,768]{1,0:T(8,128)} %get-tuple-element.60.sum_ref), custom_call_target="tpu_custom_call" | custom-call | flops 5435817984 | bytes 14680064 | tf_op jit(solution)/shard_map/qkv_grad/pallas_call | solution.py:424
  297.4 3.8 collective-permute-done.7
  302.5 3.5 stage_sum.2
  310.1 10.6 %collective-permute-done.10.refs_3_ = bf16[4,24,2432]{2,1,0:T(8,128)(2,1)S(1)} collective-permute-done((bf16[4,24,2432]{2,1,0:T(8,128)(2,1)}, bf16[4,24,2432]{2,1,0:T(8,128)(2,1)S(1)}, u32[]{:S(2)}, u32[]{:S(2)}) %collective-permute-start.10) | collective-permute-done | bytes 466976 | tf_op jit(solution)/shard_map/ppermute | solution.py:523
  320.6 9.4 %collective-permute-done.8.refs_1_ = bf16[4,24,2432]{2,1,0:T(8,128)(2,1)S(1)} collective-permute-done((bf16[4,24,2432]{2,1,0:T(8,128)(2,1)}, bf16[4,24,2432]{2,1,0:T(8,128)(2,1)S(1)}, u32[]{:S(2)}, u32[]{:S(2)}) %collective-permute-start.8) | collective-permute-done | bytes 466976 | tf_op jit(solution)/shard_map/ppermute | solution.py:523
  330.1 3.4 collective-permute-done.9.refs_2_
  343.6 9.2 %collective-permute-done.12.c_ref = bf16[24,2432]{1,0:T(8,128)(2,1)S(1)} collective-permute-done((bf16[24,2432]{1,0:T(8,128)(2,1)}, bf16[24,2432]{1,0:T(8,128)(2,1)S(1)}, u32[]{:S(2)}, u32[]{:S(2)}) %collective-permute-start.12) | collective-permute-done | bytes 116768 | tf_op jit(solution)/shard_map/ppermute | solution.py:523
  352.8 8.3 %reduce-scatter.2.cloned.1.call-done = bf16[1,216,768]{2,1,0:T(8,128)(2,1)} async-done(((bf16[32,216,768]{2,1,0:T(8,128)(2,1)}), bf16[1,216,768]{2,1,0:T(8,128)(2,1)}) %reduce-scatter.2.cloned.1.call-update) | async-done | bytes 331792 | tf_op jit(solution)/shard_map/reduce_scatter | solution.py:627
  363.5 2.9 all-to-all-start
  367.5 6.0 %all-to-all-done = f32[32,1,128]{2,1,0:T(1,128)S(1)} async-done(((f32[32,1,128]{2,1,0:T(1,128)}), f32[32,1,128]{2,1,0:T(1,128)S(1)}, u32[]{:S(2)}, u32[]{:S(2)}) %all-to-all-start) | async-done | bytes 16416 | tf_op jit(solution)/shard_map/all_to_all | solution.py:646
  (111 shorter events, 42.3 us)
Async XLA Ops:
  7.2 113.3 %all-gather.3.cloned.1.call-start = ((), (), s32[]{:S(2)}) async-start(), calls=%async_computation.3 | async-start | bytes 10948608 | tf_op jit(solution)/shard_map/all_gather | solution.py:604
  10.9 350.3 %reduce-scatter.2.cloned.1.call-start = ((), (), s32[]{:S(2)}) async-start(), calls=%async_computation.2 | async-start | bytes 10948608 | tf_op jit(solution)/shard_map/reduce_scatter | solution.py:627
  12.4 9.2 %collective-permute-start = (bf16[24,2432]{1,0:T(8,128)(2,1)S(1)}, bf16[24,2432]{1,0:T(8,128)(2,1)S(1)}, u32[]{:S(2)}, u32[]{:S(2)}) collective-permute-start(bf16[24,2432]{1,0:T(8,128)(2,1)S(1)} %fusion.4), channel_id=1, source_target_pairs={{0,6},{1,7},{2,4},{3,5},{4,2},{5,3},{6,0},{7,1},{8,14},{9,15},{10,... | collective-permute-start | bytes 350216 | tf_op jit(solution)/shard_map/ppermute | solution.py:523
  17.5 11.7 %collective-permute-start.1 = (bf16[24,2432]{1,0:T(8,128)(2,1)S(1)}, bf16[24,2432]{1,0:T(8,128)(2,1)S(1)}, u32[]{:S(2)}, u32[]{:S(2)}) collective-permute-start(bf16[24,2432]{1,0:T(8,128)(2,1)S(1)} %fusion.4), channel_id=1, source_target_pairs={{0,4},{1,5},{2,6},{3,7},{4,0},{5,1},{6,2},{7,3},{8,12},{9,13},{10,... | collective-permute-start | bytes 350216 | tf_op jit(solution)/shard_map/ppermute | solution.py:523
  17.5 11.7 %collective-permute-start.2 = (bf16[24,2432]{1,0:T(8,128)(2,1)S(1)}, bf16[24,2432]{1,0:T(8,128)(2,1)S(1)}, u32[]{:S(2)}, u32[]{:S(2)}) collective-permute-start(bf16[24,2432]{1,0:T(8,128)(2,1)S(1)} %fusion.4), channel_id=1, source_target_pairs={{0,2},{1,3},{2,0},{3,1},{4,6},{5,7},{6,4},{7,5},{8,10},{9,11},{10,... | collective-permute-start | bytes 350216 | tf_op jit(solution)/shard_map/ppermute | solution.py:523
  29.4 14.6 %collective-permute-start.3 = (bf16[4,24,2432]{2,1,0:T(8,128)(2,1)S(1)}, bf16[4,24,2432]{2,1,0:T(8,128)(2,1)S(1)}, u32[]{:S(2)}, u32[]{:S(2)}) collective-permute-start(bf16[4,24,2432]{2,1,0:T(8,128)(2,1)S(1)} %pad_maximum_fusion.1), channel_id=1, source_target_pairs={{0,24},{8,16},{16,8},{24,0},{1,25},{9,17},{17,9},{25,1},{2,26},{10... | collective-permute-start | bytes 1400840 | tf_op jit(solution)/shard_map/ppermute | solution.py:523
  32.2 18.3 %collective-permute-start.4 = (bf16[4,24,2432]{2,1,0:T(8,128)(2,1)S(1)}, bf16[4,24,2432]{2,1,0:T(8,128)(2,1)S(1)}, u32[]{:S(2)}, u32[]{:S(2)}) collective-permute-start(bf16[4,24,2432]{2,1,0:T(8,128)(2,1)S(1)} %pad_maximum_fusion.1), channel_id=1, source_target_pairs={{0,16},{8,24},{16,0},{24,8},{1,17},{9,25},{17,1},{25,9},{2,18},{10... | collective-permute-start | bytes 1400840 | tf_op jit(solution)/shard_map/ppermute | solution.py:523
  32.6 19.2 %collective-permute-start.5 = (bf16[4,24,2432]{2,1,0:T(8,128)(2,1)S(1)}, bf16[4,24,2432]{2,1,0:T(8,128)(2,1)S(1)}, u32[]{:S(2)}, u32[]{:S(2)}) collective-permute-start(bf16[4,24,2432]{2,1,0:T(8,128)(2,1)S(1)} %pad_maximum_fusion.1), channel_id=1, source_target_pairs={{0,8},{8,0},{16,24},{24,16},{1,9},{9,1},{17,25},{25,17},{2,10},{10... | collective-permute-start | bytes 1400840 | tf_op jit(solution)/shard_map/ppermute | solution.py:523
  55.5 5.1 %collective-permute-start.6 = (bf16[4,4,24,2432]{3,2,1,0:T(8,128)(2,1)}, bf16[4,4,24,2432]{3,2,1,0:T(8,128)(2,1)}, u32[]{:S(2)}, u32[]{:S(2)}) collective-permute-start(bf16[4,4,24,2432]{3,2,1,0:T(8,128)(2,1)} %pad_maximum_fusion), channel_id=1, source_target_pairs={{0,1},{1,0},{2,3},{3,2},{4,5},{5,4},{6,7},{7,6},{8,9},{9,8},{10,11... | collective-permute-start | bytes 5603336 | tf_op jit(solution)/shard_map/ppermute | solution.py:523
  297.1 4.0 %collective-permute-start.7 = (bf16[16,24,2432]{2,1,0:T(8,128)(2,1)}, bf16[16,24,2432]{2,1,0:T(8,128)(2,1)S(1)}, u32[]{:S(2)}, u32[]{:S(2)}) collective-permute-start(bf16[16,24,2432]{2,1,0:T(8,128)(2,1)} %get-tuple-element.62), channel_id=1, source_target_pairs={{0,1},{1,0},{2,3},{3,2},{4,5},{5,4},{6,7},{7,6},{8,9},{9,8},{10,11... | collective-permute-start | bytes 5603336 | tf_op jit(solution)/shard_map/ppermute | solution.py:523
  305.9 35.9 %copy-start.22 = (f32[24,14]{0,1:T(8,128)S(1)}, f32[24,14]{0,1:T(8,128)}, u32[]{:S(2)}) copy-start(f32[24,14]{0,1:T(8,128)} %param.36) | copy-start | bytes 4036
  305.9 36.0 %copy-start.23 = (f32[24,14]{0,1:T(8,128)S(1)}, f32[24,14]{0,1:T(8,128)}, u32[]{:S(2)}) copy-start(f32[24,14]{0,1:T(8,128)} %param.37) | copy-start | bytes 4036
  305.9 14.7 %collective-permute-start.10 = (bf16[4,24,2432]{2,1,0:T(8,128)(2,1)}, bf16[4,24,2432]{2,1,0:T(8,128)(2,1)S(1)}, u32[]{:S(2)}, u32[]{:S(2)}) collective-permute-start(bf16[4,24,2432]{2,1,0:T(8,128)(2,1)} %get-tuple-element.66), channel_id=1, source_target_pairs={{0,24},{8,16},{16,8},{24,0},{1,25},{9,17},{17,9},{25,1},{2,26},{10... | collective-permute-start | bytes 1400840 | tf_op jit(solution)/shard_map/ppermute | solution.py:523
  307.6 22.5 %collective-permute-start.8 = (bf16[4,24,2432]{2,1,0:T(8,128)(2,1)}, bf16[4,24,2432]{2,1,0:T(8,128)(2,1)S(1)}, u32[]{:S(2)}, u32[]{:S(2)}) collective-permute-start(bf16[4,24,2432]{2,1,0:T(8,128)(2,1)} %get-tuple-element.64), channel_id=1, source_target_pairs={{0,8},{8,0},{16,24},{24,16},{1,9},{9,1},{17,25},{25,17},{2,10},{10... | collective-permute-start | bytes 1400840 | tf_op jit(solution)/shard_map/ppermute | solution.py:523
  308.7 24.8 %collective-permute-start.9 = (bf16[4,24,2432]{2,1,0:T(8,128)(2,1)}, bf16[4,24,2432]{2,1,0:T(8,128)(2,1)S(1)}, u32[]{:S(2)}, u32[]{:S(2)}) collective-permute-start(bf16[4,24,2432]{2,1,0:T(8,128)(2,1)} %get-tuple-element.65), channel_id=1, source_target_pairs={{0,16},{8,24},{16,0},{24,8},{1,17},{9,25},{17,1},{25,9},{2,18},{10... | collective-permute-start | bytes 1400840 | tf_op jit(solution)/shard_map/ppermute | solution.py:523
  320.6 12.9 %copy-start.6 = (bf16[4,24,2432]{2,1,0:T(8,128)(2,1)}, bf16[4,24,2432]{2,1,0:T(8,128)(2,1)S(1)}, u32[]{:S(2)}) copy-start(bf16[4,24,2432]{2,1,0:T(8,128)(2,1)S(1)} %collective-permute-done.10.refs_3_) | copy-start | bytes 1400836
  336.6 7.0 %collective-permute-start.11 = (bf16[24,2432]{1,0:T(8,128)(2,1)}, bf16[24,2432]{1,0:T(8,128)(2,1)S(1)}, u32[]{:S(2)}, u32[]{:S(2)}) collective-permute-start(bf16[24,2432]{1,0:T(8,128)(2,1)} %get-tuple-element.68), channel_id=1, source_target_pairs={{0,2},{1,3},{2,0},{3,1},{4,6},{5,7},{6,4},{7,5},{8,10},{9,11},{10,... | collective-permute-start | bytes 350216 | tf_op jit(solution)/shard_map/ppermute | solution.py:523
  338.1 14.7 %collective-permute-start.12 = (bf16[24,2432]{1,0:T(8,128)(2,1)}, bf16[24,2432]{1,0:T(8,128)(2,1)S(1)}, u32[]{:S(2)}, u32[]{:S(2)}) collective-permute-start(bf16[24,2432]{1,0:T(8,128)(2,1)} %get-tuple-element.69), channel_id=1, source_target_pairs={{0,4},{1,5},{2,6},{3,7},{4,0},{5,1},{6,2},{7,3},{8,12},{9,13},{10,... | collective-permute-start | bytes 350216 | tf_op jit(solution)/shard_map/ppermute | solution.py:523
  340.5 12.3 %collective-permute-start.13 = (bf16[24,2432]{1,0:T(8,128)(2,1)}, bf16[24,2432]{1,0:T(8,128)(2,1)S(1)}, u32[]{:S(2)}, u32[]{:S(2)}) collective-permute-start(bf16[24,2432]{1,0:T(8,128)(2,1)} %get-tuple-element.70), channel_id=1, source_target_pairs={{0,6},{1,7},{2,4},{3,5},{4,2},{5,3},{6,0},{7,1},{8,14},{9,15},{10,... | collective-permute-start | bytes 350216 | tf_op jit(solution)/shard_map/ppermute | solution.py:523
  343.6 17.6 %copy-start.16 = (bf16[24,2432]{1,0:T(8,128)(2,1)}, bf16[24,2432]{1,0:T(8,128)(2,1)S(1)}, u32[]{:S(2)}) copy-start(bf16[24,2432]{1,0:T(8,128)(2,1)S(1)} %collective-permute-done.11.b_ref) | copy-start | bytes 350212
  361.2 16.5 %copy-start.2 = (f32[96,768]{1,0:T(8,128)S(1)}, f32[96,768]{1,0:T(8,128)}, u32[]{:S(2)}) copy-start(f32[96,768]{1,0:T(8,128)} %param.26) | copy-start | bytes 884740
  361.2 16.5 %copy-start.10 = (f32[96,768]{1,0:T(8,128)S(1)}, f32[96,768]{1,0:T(8,128)}, u32[]{:S(2)}) copy-start(f32[96,768]{1,0:T(8,128)} %param.35) | copy-start | bytes 884740
  361.2 16.5 %copy-start.11 = (f32[96,768]{1,0:T(8,128)S(1)}, f32[96,768]{1,0:T(8,128)}, u32[]{:S(2)}) copy-start(f32[96,768]{1,0:T(8,128)} %param.34) | copy-start | bytes 884740
  363.5 10.0 %all-to-all-start = ((f32[32,1,128]{2,1,0:T(1,128)}), f32[32,1,128]{2,1,0:T(1,128)S(1)}, u32[]{:S(2)}, u32[]{:S(2)}) async-start(f32[32,1,128]{2,1,0:T(1,128)} %bitcast.54), calls=%async_computation.1 | async-start | bytes 32768 | tf_op jit(solution)/shard_map/all_to_all | solution.py:646
  (17 other events, 50.9 us)
Sparse Core Ops, SparseCore 0:
  11.6 96.9 all-gather.2
  200.4 160.7 reduce-scatter.1

commit v4 on v3

--- a/solution.py
+++ b/solution.py
@@ -79,7 +79,7 @@
     return pl.ds(pl.multiple_of(j*BQ,BQ),BQ)
 
 
-def fwd_kernel(len_ref,qkv_ref,o_ref,lse_ref,seg,mask,va,vb,sa,sb,ma,mb,ot,last):
+def fwd_kernel(len_ref,qkv_ref,left_ref,o_ref,lse_ref,seg,mask,va,vb,sa,sb,ma,mb,ot,last):
     segments(len_ref,seg,mask)
     q_ref,k_ref,v_ref=(qkv_ref.at[:,128*b:128*b+128] for b in range(3))
     def query(rows,r):
@@ -138,19 +138,19 @@
     o_ref[...]=ot[...].T.astype(bf)
 
 
-def attn_fwd(lengths,qkv):
+def attn_fwd(lengths,qkv,left):
     blk=lambda width: pl.BlockSpec((ROW,width),lambda h:(0,h))
     return pl.pallas_call(fwd_kernel,grid=(6,),
-        in_specs=[pl.BlockSpec(memory_space=pltpu.SMEM),blk(384)],
-        out_specs=[blk(128),pl.BlockSpec((1,8,ROW),lambda h:(h,0,0))],
-        out_shape=[jax.ShapeDtypeStruct((ROW,768),bf),jax.ShapeDtypeStruct((6,8,ROW),f32)],
+        in_specs=[pl.BlockSpec(memory_space=pltpu.SMEM),blk(384),pl.BlockSpec(memory_space=pl.ANY)],
+        out_specs=[pl.BlockSpec((ROW,128),lambda h:(0,6+h)),pl.BlockSpec((1,8,ROW),lambda h:(h,0,0))],
+        out_shape=[jax.ShapeDtypeStruct((ROW,2*D),bf),jax.ShapeDtypeStruct((6,8,ROW),f32)],input_output_aliases={2:0},
         scratch_shapes=[pltpu.VMEM((ROW,128),bf)]*2+[pltpu.VMEM((80,ROW),bf)]*2+[pltpu.VMEM((MAIN,BQ),f32)]*2+[pltpu.VMEM((8,BQ),f32)]*2
           +[pltpu.VMEM((128,ROW),f32),pltpu.VMEM((144,BQ),f32)],
         compiler_params=pltpu.CompilerParams(vmem_limit_bytes=60<<20),name="attn_fwd",
-        cost_estimate=pl.CostEstimate(flops=4*ROW*ROW*D,bytes_accessed=10<<20,transcendentals=12*ROW*ROW))(lengths,qkv)
-
-
-def bwd_kernel(len_ref,qkv_ref,o_ref,do_ref,lse_ref,d_ref,
+        cost_estimate=pl.CostEstimate(flops=4*ROW*ROW*D,bytes_accessed=10<<20,transcendentals=12*ROW*ROW))(lengths,qkv,left)
+
+
+def bwd_kernel(len_ref,qkv_ref,o_ref,do_ref,lse_ref,right_ref,d_ref,
                seg,mask,kt,xa,ya,xb,yb,dqt,dqe,dka,dva):
     segments(len_ref,seg,mask)
     q_ref,k_ref,v_ref=(qkv_ref.at[:,128*b:128*b+128] for b in range(3))
@@ -203,16 +203,16 @@
     d_ref[:,256:384]=dva[...].astype(bf)
 
 
-def attn_bwd(lengths,qkv,o,do,lse):
+def attn_bwd(lengths,qkv,left,do,lse,right):
     blk=lambda width: pl.BlockSpec((ROW,width),lambda h:(0,h))
     return pl.pallas_call(bwd_kernel,grid=(6,),
-        in_specs=[pl.BlockSpec(memory_space=pltpu.SMEM),blk(384),blk(128),blk(128),pl.BlockSpec((1,8,ROW),lambda h:(h,0,0))],
+        in_specs=[pl.BlockSpec(memory_space=pltpu.SMEM),blk(384),pl.BlockSpec((ROW,128),lambda h:(0,6+h)),blk(128),pl.BlockSpec((1,8,ROW),lambda h:(h,0,0)),pl.BlockSpec(memory_space=pl.ANY)],
         out_specs=blk(384),
-        out_shape=jax.ShapeDtypeStruct((ROW,3*D),bf),
+        out_shape=jax.ShapeDtypeStruct((ROW,4*D),bf),input_output_aliases={5:0},
         scratch_shapes=[pltpu.VMEM((ROW,128),bf)]*2+[pltpu.VMEM((128,ROW),bf)]+[pltpu.VMEM((MAIN,BQ),f32)]*4
           +[pltpu.VMEM((128,ROW),f32),pltpu.VMEM((128,BQ),f32)]+[pltpu.VMEM((ROW,128),f32)]*2,
         compiler_params=pltpu.CompilerParams(vmem_limit_bytes=62<<20),name="attn_bwd",
-        cost_estimate=pl.CostEstimate(flops=10*ROW*ROW*D,bytes_accessed=20<<20,transcendentals=12*ROW*ROW))(lengths,qkv,o,do,lse)
+        cost_estimate=pl.CostEstimate(flops=10*ROW*ROW*D,bytes_accessed=20<<20,transcendentals=12*ROW*ROW))(lengths,qkv,left,do,lse,right)
 
 
 BM=512
@@ -254,34 +254,73 @@
         in_specs=[tile(D)],out_specs=[tile(D),tile(128)],
         out_shape=[jax.ShapeDtypeStruct((rows,D),f32),jax.ShapeDtypeStruct((rows,128),f32)],
         compiler_params=params(),name="norm_input",
-        cost_estimate=pl.CostEstimate(flops=12*rows*D,bytes_accessed=8<<20,transcendentals=0))(x)
-
-
-def qkv_kernel(n_ref,w_ref,v_ref,h_ref,qkv_ref,vec_ref):
-    @pl.when(pl.program_id(0)==0)
+        cost_estimate=pl.CostEstimate(flops=1000,bytes_accessed=1000,transcendentals=0))(x)
+
+
+def pack_kernel(qkv_ref,proj_ref,fc1_ref,fc2_ref,vec_ref,first_ref,rest_ref):
+    r=qkv_ref.shape[0]
+    for p in range(6):
+        for part in range(3):
+            at=384*p+128*part
+            first_ref[:,at:at+128]=qkv_ref[:,D*part+128*p:D*part+128*p+128].astype(bf)
+    vec=vec_ref[...]
+    vec=jnp.concatenate([vec,jnp.zeros((128-vec.shape[0],r),f32)],axis=0)
+    first_ref[:,3*D:WIDE]=vec.T.astype(bf)
+    rest_ref[0:4*r,:]=fc2_ref[...].astype(bf)
+    for c in range(4):
+        rest_ref[(4+c)*r:(5+c)*r,:]=fc1_ref[:,D*c:D*c+D].astype(bf)
+    rest_ref[8*r:9*r,:]=proj_ref[...].astype(bf)
+
+
+def pack_shards(qkv,proj,fc1,fc2,vectors):
+    r=qkv.shape[0]
+    ins=(qkv,proj,fc1,fc2,vectors.T)
+    shapes=[(r,WIDE),(9*r,D)]
+    whole=lambda s: pl.BlockSpec(s,lambda i:(0,)*len(s))
+    return pl.pallas_call(pack_kernel,grid=(1,),
+        in_specs=[whole(v.shape) for v in ins],out_specs=[whole(v) for v in shapes],
+        out_shape=[jax.ShapeDtypeStruct(v,bf) for v in shapes],
+        compiler_params=params(),name="pack_shards")(*ins)
+
+
+def qkv_kernel(place_ref,n_ref,*refs):
+    parts,(left_ref,qkv_ref,vec_ref,w_ref,w,sems,out_sem)=refs[:8],refs[8:]
+    step=pl.program_id(0)
+    keep=pltpu.make_async_copy(w,w_ref,out_sem)
+    @pl.when(step==0)
     def _():
-        vec_ref[...]=v_ref[...].reshape(D,128).astype(f32).T[0:16]
+        copies=[]
+        for i,part in enumerate(parts):
+            core,dp=place_ref[2]^(i//4),place_ref[0]^(i%4)
+            for k in range(4):
+                copies.append(pltpu.make_async_copy(part.at[k],w.at[dp,place_ref[1]^k,core],sems.at[4*i+k]))
+        for copy in copies:
+            copy.start()
+        for copy in copies:
+            copy.wait()
+        keep.start()
+        vec_ref[...]=w[:,:,:,:,3*D:WIDE].reshape(D,128).astype(f32).T[0:16]
     h=(n_ref[...]*vec_ref[0:1,:]+vec_ref[1:2,:]).astype(bf)
-    h_ref[...]=h
+    left_ref[...]=h
     zero=jnp.zeros((1,128),f32)
     bias=jnp.concatenate([b for p in range(6) for b in (vec_ref[2:3,128*p:128*p+128],zero,vec_ref[3:4,128*p:128*p+128])],axis=1)
-    qkv_ref[...]=(nn(h,w_ref[...].reshape(D,3*D))+bias).astype(bf)
-
-
-def packed_specs(w):
-    n,r=w.shape[:2]
-    return [once((n,r,3*D),lambda i:(0,0,0)),once((n,r,128),lambda i:(0,0,3*D//128))]
-
-
-def qkv_forward(n,w):
+    qkv_ref[...]=(nn(h,w[:,:,:,:,0:3*D].reshape(D,3*D))+bias).astype(bf)
+    @pl.when(step==pl.num_programs(0)-1)
+    def _():
+        keep.wait()
+
+
+def qkv_forward(place,n,parts):
     rows=n.shape[0]
     sd=jax.ShapeDtypeStruct
+    wide=(4,4,2,D//PACK,WIDE)
     return pl.pallas_call(qkv_kernel,grid=(rows//BM,),
-        in_specs=[tile(D)]+packed_specs(w),
-        out_specs=[tile(D),tile(3*D),pl.BlockSpec((16,D),lambda i:(0,0))],
-        out_shape=[sd((rows,D),bf),sd((rows,3*D),bf),sd((16,D),f32)],
+        in_specs=[pl.BlockSpec(memory_space=pltpu.SMEM),tile(D)]+[pl.BlockSpec(memory_space=pl.ANY)]*8,
+        out_specs=[tile(D),tile(3*D),pl.BlockSpec((16,D),lambda i:(0,0)),pl.BlockSpec(memory_space=pl.ANY)],
+        out_shape=[sd((rows,2*D),bf),sd((rows,3*D),bf),sd((16,D),f32),sd(wide,bf)],
+        scratch_shapes=[pltpu.VMEM(wide,bf),pltpu.SemaphoreType.DMA((32,)),pltpu.SemaphoreType.DMA],
         compiler_params=params(),name="qkv_forward",
-        cost_estimate=pl.CostEstimate(flops=2*rows*D*3*D,bytes_accessed=18<<20,transcendentals=0))(n,w,w)
+        cost_estimate=pl.CostEstimate(flops=2*rows*D*3*D,bytes_accessed=18<<20,transcendentals=0))(place,n,*parts)
 
 
 CH=768
@@ -358,9 +397,9 @@
     n,r=packed.shape[0],D//packed.shape[0]
     sd=jax.ShapeDtypeStruct
     return pl.pallas_call(mlp_kernel,grid=(rows//BM,),
-        in_specs=[tile(D),tile(D),tile(D),once((16,D)),once((n,4*r,D))]+[once((n,r,D),lambda i,b=b:(0,b,0)) for b in range(4,9)],
-        out_specs=[tile(D),tile(D),tile(D),tile(FF),tile(FF),tile(D),tile(D),tile(D),pl.BlockSpec((16,D),lambda i:(0,0))],
-        out_shape=[sd((rows,D),bf),sd((rows,D),bf),sd((rows,D),bf),sd((rows,FF),bf),sd((rows,FF),bf),sd((rows,D),f32),sd((rows,D),bf),sd((rows,D),bf),sd((16,D),f32)],
+        in_specs=[tile(D),pl.BlockSpec((BM,D),lambda i:(i,1)),tile(D),once((16,D)),once((n,4*r,D))]+[once((n,r,D),lambda i,b=b:(0,b,0)) for b in range(4,9)],
+        out_specs=[tile(D),tile(D),tile(D),tile(FF),tile(FF),tile(D),pl.BlockSpec((BM,D),lambda i:(i,3)),tile(D),pl.BlockSpec((16,D),lambda i:(0,0))],
+        out_shape=[sd((rows,D),bf),sd((rows,D),bf),sd((rows,D),bf),sd((rows,FF),bf),sd((rows,FF),bf),sd((rows,D),f32),sd((rows,4*D),bf),sd((rows,D),bf),sd((16,D),f32)],
         scratch_shapes=[pltpu.VMEM((BM,D),f32)]*5+[pltpu.VMEM((BM,CH),f32)]*4+[pltpu.VMEM((4,D,D),bf)],
         compiler_params=params(),name="mlp_block",
         cost_estimate=pl.CostEstimate(flops=2*rows*D*(2*D+4*FF),bytes_accessed=48<<20,transcendentals=0))(x,o,dy,vec,*[packed]*6)
@@ -381,52 +420,49 @@
         cost_estimate=pl.CostEstimate(flops=2*rows*D*FF,bytes_accessed=16<<20,transcendentals=0))(z,dm)
 
 
-def fc1_proj_kernel(h_ref,du_ref,o_ref,da_ref,old_ref,g_ref):
-    i=pl.program_id(0)
-    @pl.when(i<4)
-    def _():
-        g_ref[...]=tn(h_ref[...],du_ref[...]).reshape(g_ref.shape).astype(bf)
-    @pl.when(i==4)
-    def _():
-        g_ref[...]=tn(o_ref[...],da_ref[...]).reshape(g_ref.shape).astype(bf)
-
-
-def fc1_proj_grad(h,du,o,da,packed):
+def fc1_kernel(a_ref,b_ref,old_ref,g_ref):
+    outer_kernel(a_ref,b_ref,g_ref)
+
+
+def fc1_grad(h,du,packed):
     rows=h.shape[0]
     n=packed.shape[0]; r=D//n
-    base=packed.shape[1]//r-5
-    return pl.pallas_call(fc1_proj_kernel,grid=(5,),
-        in_specs=[once((rows,D)),pl.BlockSpec((rows,D),lambda i:(0,jnp.minimum(i,3))),once((rows,D)),once((rows,D)),pl.BlockSpec(memory_space=pl.ANY)],
-        out_specs=pl.BlockSpec((n,r,D),lambda i:(0,base+i,0)),
-        out_shape=jax.ShapeDtypeStruct(packed.shape,bf),input_output_aliases={4:0},
-        compiler_params=params(),name="fc1_proj_grad",
-        cost_estimate=pl.CostEstimate(flops=2*rows*D*(FF+D),bytes_accessed=24<<20,transcendentals=0))(h,du,o,da,packed)
-
-
-def qkv_grad_kernel(core_ref,h_ref,d_ref,sum_ref,mine_ref,other_ref):
+    return pl.pallas_call(fc1_kernel,grid=(FF//D,),
+        in_specs=[once((rows,D)),pl.BlockSpec((rows,D),lambda i:(0,i)),pl.BlockSpec(memory_space=pl.ANY)],
+        out_specs=pl.BlockSpec((n,r,D),lambda i:(0,FF//D+i,0)),
+        out_shape=jax.ShapeDtypeStruct(packed.shape,bf),input_output_aliases={2:0},
+        compiler_params=params(),name="fc1_grad",
+        cost_estimate=pl.CostEstimate(flops=2*rows*D*FF,bytes_accessed=20<<20,transcendentals=0))(h,du,packed)
+
+
+def split_kernel(core_ref,left_ref,right_ref,*refs):
+    sum_ref,(mine_ref,other_ref)=refs[:-2],refs[-2:]
     i=pl.program_id(0)
     even=core_ref[0]==0
     def put(v,cols):
         v=v.reshape(mine_ref.shape[0],2,mine_ref.shape[1],v.shape[1])
         mine_ref[:,:,cols]=jnp.where(even,v[:,0],v[:,1]).astype(bf)
         other_ref[:,:,cols]=jnp.where(even,v[:,1],v[:,0]).astype(bf)
-    @pl.when(i==0)
-    def _():
-        sums=jnp.concatenate([sum_ref[...],jnp.zeros((112,D),f32)],axis=0)
-        put(sums.T,slice(3*D,WIDE))
-    put(tn(h_ref[...],d_ref[...]),pl.ds(pl.multiple_of(i*D,D),D))
-
-
-def qkv_grad(core,h,d,sums):
-    rows=h.shape[0]
-    half_shape=(PACK//2,D//PACK,WIDE)
-    out=pl.BlockSpec(half_shape,lambda i:(0,0,0))
-    return pl.pallas_call(qkv_grad_kernel,grid=(3,),
-        in_specs=[pl.BlockSpec(memory_space=pltpu.SMEM),once((rows,D)),pl.BlockSpec((rows,D),lambda i:(0,i)),once((16,D))],
+    if sum_ref:
+        @pl.when(i==0)
+        def _():
+            sums=jnp.concatenate([sum_ref[0][...],jnp.zeros((112,D),f32)],axis=0)
+            put(sums.T,slice(2*D,2*D+128))
+    put(tn(left_ref[...],right_ref[...]),pl.ds(pl.multiple_of(i*D,D),D))
+
+
+def split_grad(core,left,right,sums=None):
+    rows=left.shape[0]
+    more=[] if sums is None else [sums]
+    index=(lambda i:(0,1-i),lambda i:(0,3-3*i)) if sums is None else (lambda i:(0,0),lambda i:(0,1+i))
+    shape=(PACK//2,D//PACK,2*D+128*len(more))
+    out=pl.BlockSpec(memory_space=pltpu.VMEM)
+    return pl.pallas_call(split_kernel,grid=(2,),
+        in_specs=[pl.BlockSpec(memory_space=pltpu.SMEM)]+[pl.BlockSpec((rows,D),f) for f in index]+[once((16,D))]*len(more),
         out_specs=[out,out],
-        out_shape=[jax.ShapeDtypeStruct(half_shape,bf)]*2,
-        compiler_params=params(),name="qkv_grad",
-        cost_estimate=pl.CostEstimate(flops=2*rows*D*3*D,bytes_accessed=14<<20,transcendentals=0))(core,h,d,sums)
+        out_shape=[jax.ShapeDtypeStruct(shape,bf)]*2,
+        compiler_params=pltpu.CompilerParams(vmem_limit_bytes=48<<20),name="split_grad",
+        cost_estimate=pl.CostEstimate(flops=1000,bytes_accessed=1000,transcendentals=0))(core,left,right,*more)
 
 
 def input_kernel(n_ref,r_ref,d_ref,dx1_ref,vec_ref,old_ref,w_ref,gx_ref,sum_ref):
@@ -451,11 +487,11 @@
 def input_grad(n,r,d,dx1,vec,sums,w):
     rows=n.shape[0]
     return pl.pallas_call(input_kernel,grid=(rows//BM,),
-        in_specs=[tile(D),tile(128),tile(3*D),tile(D),once((16,D)),once((16,D))]+packed_specs(w)[:1],
+        in_specs=[tile(D),tile(128),tile(3*D),tile(D),once((16,D)),once((16,D)),once(w.shape[:-1]+(3*D,),lambda i:(0,)*len(w.shape))],
         out_specs=[tile(D),pl.BlockSpec((16,D),lambda i:(0,0))],
         out_shape=[jax.ShapeDtypeStruct((rows,D),bf),jax.ShapeDtypeStruct((16,D),f32)],
         compiler_params=params(),name="input_grad",
-        cost_estimate=pl.CostEstimate(flops=2*rows*D*3*D,bytes_accessed=24<<20,transcendentals=0))(n,r,d,dx1,vec,sums,w)
+        cost_estimate=pl.CostEstimate(flops=1000,bytes_accessed=1000,transcendentals=0))(n,r,d,dx1,vec,sums,w)
 
 
 def stage_kernel(count,place_ref,*refs):
@@ -467,30 +503,44 @@
 
 def stage_sum(place,parts):
     shape=parts[0].shape
-    whole=lambda s: pl.BlockSpec(s,lambda i:(0,)*len(s))
-    return pl.pallas_call(functools.partial(stage_kernel,len(parts)),grid=(1,),
-        in_specs=[pl.BlockSpec(memory_space=pltpu.SMEM)]+[whole(shape)]*len(parts),
-        out_specs=[whole(shape[1:])]*4,
+    near=pl.BlockSpec(memory_space=pltpu.VMEM)
+    return pl.pallas_call(functools.partial(stage_kernel,len(parts)),
+        in_specs=[pl.BlockSpec(memory_space=pltpu.SMEM)]+[near]*len(parts),
+        out_specs=[near]*4,
         out_shape=[jax.ShapeDtypeStruct(shape[1:],bf)]*4,
-        compiler_params=params(),name="stage_sum")(place,*parts)
-
-
-def finish_kernel(a_ref,b_ref,c_ref,d_ref,rest_ref,g_ref,square_ref):
-    g=sum(ref[...].astype(f32) for ref in (a_ref,b_ref,c_ref,d_ref))
-    g_ref[...]=g
+        compiler_params=pltpu.CompilerParams(vmem_limit_bytes=16<<20),name="stage_sum",
+        cost_estimate=pl.CostEstimate(flops=1000,bytes_accessed=1000,transcendentals=0))(place,*parts)
+
+
+def finish_kernel(*refs):
+    first,second,(rest_ref,qkv_ref,proj_ref,fc1_ref,fc2_ref,vec_ref,square_ref)=refs[:4],refs[4:8],refs[8:]
+    a=sum(ref[...].astype(f32) for ref in first)
+    b=sum(ref[...].astype(f32) for ref in second)
     rest=rest_ref[...].astype(f32)
-    total=jnp.sum(g*g,keepdims=True)+jnp.sum(rest*rest,keepdims=True)
+    total=jnp.sum(a*a,keepdims=True)+jnp.sum(b*b,keepdims=True)+jnp.sum(rest*rest,keepdims=True)
     square_ref[...]=jnp.broadcast_to(total,square_ref.shape)
-
-
-def finish_sum(parts,rest):
-    whole=lambda s: pl.BlockSpec(s,lambda i:(0,)*len(s))
-    shape=parts[0].shape
-    return pl.pallas_call(finish_kernel,grid=(1,),
-        in_specs=[whole(shape)]*4+[whole(rest.shape)],
-        out_specs=[whole(shape),whole((PACK,128))],
-        out_shape=[jax.ShapeDtypeStruct(shape,f32),jax.ShapeDtypeStruct((PACK,128),f32)],
-        compiler_params=params(),name="finish_sum")(*parts,rest)
+    r=a.shape[0]
+    proj_ref[...]=a[:,0:D]
+    for p in range(6):
+        for part in range(3):
+            at=384*p+128*part
+            qkv_ref[:,D*part+128*p:D*part+128*p+128]=a[:,D+at:D+at+128] if p<2 else b[:,at-D:at-D+128]
+    vec_ref[...]=b[:,2*D:2*D+128].T
+    fc2_ref[...]=rest[0:4*r]
+    for c in range(4):
+        fc1_ref[:,D*c:D*c+D]=rest[(4+c)*r:(5+c)*r]
+
+
+def finish_sum(first,second,rest):
+    near=pl.BlockSpec(memory_space=pltpu.VMEM)
+    r=rest.shape[0]//8
+    shapes=[(r,3*D),(r,D),(r,FF),(4*r,D),(128,r),(PACK,128)]
+    return pl.pallas_call(finish_kernel,
+        in_specs=[near]*9,
+        out_specs=[near]*6,
+        out_shape=[jax.ShapeDtypeStruct(v,f32) for v in shapes],
+        compiler_params=pltpu.CompilerParams(vmem_limit_bytes=24<<20),name="finish_sum",
+        cost_estimate=pl.CostEstimate(flops=1000,bytes_accessed=1000,transcendentals=0))(*first,*second,rest)
 
 
 def adam_update(weight, grad, first, second, rate, decay, fix_one, fix_two):
@@ -500,15 +550,6 @@
     return (weight - rate * (stride + decay * weight), first, second)
 
 
-def split_columns(shard):
-    r, width = shard.shape
-    return jnp.concatenate([shard[:, b * D : (b + 1) * D] for b in range(width // D)], axis=0)
-
-
-def join_columns(block, r):
-    return jnp.concatenate([block[b * r : (b + 1) * r] for b in range(block.shape[0] // r)], axis=1)
-
-
 def pack_rows(full):
     k = full.shape[1] // D
     return full.reshape(PACK, D // PACK, k, D).transpose(0, 2, 1, 3).reshape(PACK, -1, D)
@@ -523,39 +564,24 @@
     return lax.ppermute(value, axis, [(i, i ^ flip) for i in range(size)])
 
 
-def by_xor(parts, me):
-    if len(parts) == 2:
-        odd = me % 2 == 1
-        return jnp.stack([jnp.where(odd, parts[1], parts[0]), jnp.where(odd, parts[0], parts[1])])
-    low, high = (me % 2 == 1, me // 2 == 1)
-    return jnp.stack(
-        [
-            jnp.where(high, jnp.where(low, parts[j ^ 3], parts[j ^ 2]), jnp.where(low, parts[j ^ 1], parts[j]))
-            for j in range(4)
-        ]
-    )
-
-
 def places():
     inner = lax.axis_index("fsdp")
     return (lax.axis_index("dp"), inner // 2, inner % 2)
 
 
-def gather_direct(shard):
-    me_dp, me_z, me_core = places()
-    part = by_xor([shard] + [swap(shard, "fsdp", 8, 2 * k) for k in (1, 2, 3)], me_z)
-    part = by_xor([part] + [swap(part, "dp", 4, k) for k in (1, 2, 3)], me_dp)
-    part = by_xor([part, swap(part, "fsdp", 8, 1)], me_core)
-    return part.transpose(1, 2, 0, 3, 4).reshape(PACK, *shard.shape)
-
-
-def scatter_direct(mine, other):
-    me_dp, me_z, _ = places()
+def first_stage(me, mine, other):
     got = swap(other, "fsdp", 8, 1)
     shape = (4, 4) + mine.shape[1:]
-    keep, *send = stage_sum(me_dp.reshape(1), [mine.reshape(shape), got.reshape(shape)])
-    parts = [swap(v, "dp", 4, k + 1) for k, v in enumerate(send)]
-    keep, *send = stage_sum(me_z.reshape(1), [keep] + parts)
+    return stage_sum(me, [mine.reshape(shape), got.reshape(shape)])
+
+
+def second_stage(me, parts):
+    keep, *send = parts
+    return stage_sum(me, [keep] + [swap(v, "dp", 4, k + 1) for k, v in enumerate(send)])
+
+
+def third_stage(parts):
+    keep, *send = parts
     return [keep] + [swap(v, "fsdp", 8, 2 * k + 2) for k, v in enumerate(send)]
 
 
@@ -597,65 +623,82 @@
     ):
         per = weight_qkv.shape[0]
         cols = vectors.shape[1]
-        low = [w.astype(bf) for w in (weight_qkv, weight_proj, weight_fc1, weight_fc2, vectors)]
-        first = jnp.concatenate([to_pairs(low[0]), jnp.pad(low[4], ((0, 0), (0, 128 - cols)))], axis=1)
+        rows_dev, row, _ = tokens.shape
+        count = rows_dev * row
+        inputs = tokens.reshape(count, D)
+        centered, spread = norm_input(inputs)
         if fast:
-            mats_qkv = gather_direct(first)
-            rest = lax.all_gather(
-                jnp.concatenate([low[3], split_columns(low[2]), low[1]], axis=0), AXES, axis=0, tiled=False
-            )
+            first, packed = pack_shards(weight_qkv, weight_proj, weight_fc1, weight_fc2, vectors)
+            rest = lax.all_gather(packed, AXES, axis=0, tiled=False)
+            along = jnp.stack([first] + [swap(first, "fsdp", 8, 2 * k) for k in (1, 2, 3)])
+            parts = [along] + [swap(along, "dp", 4, k) for k in (1, 2, 3)]
+            far = parts.pop()
+            parts = [parts, [swap(v, "fsdp", 8, 1) for v in parts]]
+            far, parts, centered, spread = lax.optimization_barrier((far, parts, centered, spread))
+            parts = parts[0] + [far] + parts[1] + [swap(far, "fsdp", 8, 1)]
+            place = jnp.stack(places()).astype(jnp.int32)
         else:
-            mats_qkv = gather(first).reshape(PACK, D // PACK, WIDE)
+            low = [w.astype(bf) for w in (weight_qkv, weight_proj, weight_fc1, weight_fc2, vectors)]
+            first = jnp.concatenate([to_pairs(low[0]), jnp.pad(low[4], ((0, 0), (0, 128 - cols)))], axis=1)
+            whole = gather(first).reshape(4, 4, 2, D // PACK, WIDE)
+            parts = [whole[k, :, c] for c in range(2) for k in range(4)]
+            place = jnp.zeros((3,), jnp.int32)
             full = [gather(w) for w in low[1:4]]
             rest = jnp.concatenate(
                 [full[2].reshape(PACK, FF // PACK, D), pack_rows(full[1]), pack_rows(full[0])], axis=1
             )
-        rows_dev, row, _ = tokens.shape
-        count = rows_dev * row
-        inputs = tokens.reshape(count, D)
-        centered, spread = norm_input(inputs)
-        normed, qkv, vec = qkv_forward(centered, mats_qkv)
+        left, qkv, vec, mats_qkv = qkv_forward(place, centered, parts)
         each = lambda v, b: v[b * row : (b + 1) * row]
-        done = [attn_fwd(lengths[b : b + 1], each(qkv, b)) for b in range(rows_dev)]
-        mixed = jnp.concatenate([o for o, _ in done], axis=0)
-        result, normed_two, grad_down, active, grad_inner, grad_middle, grad_branch, grad_mixed, sums = mlp_block(
-            inputs, mixed, cotangent.reshape(count, D), vec, rest
+        done = [attn_fwd(lengths[b : b + 1], each(qkv, b), each(left, b)) for b in range(rows_dev)]
+        left = jnp.concatenate([v for v, _ in done], axis=0)
+        result, normed_two, grad_down, active, grad_inner, grad_middle, right, grad_mixed, sums = mlp_block(
+            inputs, left, cotangent.reshape(count, D), vec, rest
         )
-        grads = fc2_grad(active, grad_down, PACK, 5 * D // PACK)
-        grads = fc1_proj_grad(normed_two, grad_inner, mixed, grad_branch, grads)
+        grads = fc2_grad(active, grad_down, PACK, FF // PACK)
+        grads = fc1_grad(normed_two, grad_inner, grads)
         if fast:
             rest_owned = lax.psum_scatter(grads, AXES, scatter_dimension=0, tiled=False)
-        back = [
-            attn_bwd(lengths[b : b + 1], each(qkv, b), done[b][0], each(grad_mixed, b), done[b][1])
-            for b in range(rows_dev)
-        ]
-        grad_qkv = jnp.concatenate(back, axis=0)
-        grad_inputs, sums = input_grad(centered, spread, grad_qkv, grad_middle, vec, sums, mats_qkv)
-        core = places()[2].reshape(1) if fast else jnp.zeros((1,), jnp.int32)
-        mine, other = qkv_grad(core, normed, grad_qkv, sums)
+        right = jnp.concatenate(
+            [
+                attn_bwd(
+                    lengths[b : b + 1], each(qkv, b), each(left, b), each(grad_mixed, b), done[b][1], each(right, b)
+                )
+                for b in range(rows_dev)
+            ],
+            axis=0,
+        )
+        core = place[2:]
+        mine_a, other_a = split_grad(core, left, right)
         if fast:
-            first_owned, squares = finish_sum(scatter_direct(mine, other), rest_owned)
-            rest_owned = rest_owned.astype(f32)
-            owned = (
-                from_pairs(first_owned[:, : 3 * D]),
-                rest_owned[8 * per :],
-                join_columns(rest_owned[4 * per : 8 * per], per),
-                rest_owned[: 4 * per],
-                first_owned[:, 3 * D : 3 * D + cols],
-            )
+            me_dp, me_z = place[0:1], place[1:2]
+            stage_a = first_stage(me_dp, mine_a, other_a)
+            *stage_a, vec = lax.optimization_barrier((*stage_a, vec))
+        grad_inputs, sums = input_grad(centered, spread, right, grad_middle, vec, sums, mats_qkv)
+        if fast:
+            stage_a = second_stage(me_z, stage_a)
+            *stage_a, sums = lax.optimization_barrier((*stage_a, sums))
+            owned_a = third_stage(stage_a)
+            mine_b, other_b = split_grad(core, left, right, sums)
+            *owned_a, other_b = lax.optimization_barrier((*owned_a, other_b))
+            owned_b = third_stage(second_stage(me_z, first_stage(me_dp, mine_b, other_b)))
+            *owned, squares = finish_sum(owned_a, owned_b, rest_owned)
+            owned[4] = owned[4][:cols]
             squares = jnp.sum(lax.all_to_all(squares, AXES, 0, 0, tiled=True), axis=0)[0]
         else:
+            mine_b, other_b = split_grad(core, left, right, sums)
             wide = FF // PACK
-            grads_first = jnp.stack([mine, other], axis=1).reshape(D, WIDE)
-            owned = (
-                scatter(from_pairs(grads_first[:, : 3 * D])),
-                scatter(unpack_rows(grads[:, 2 * wide :])),
-                scatter(unpack_rows(grads[:, wide : 2 * wide])),
+            part_a = jnp.stack([mine_a, other_a], axis=1).reshape(D, 2 * D)
+            part_b = jnp.stack([mine_b, other_b], axis=1).reshape(D, 2 * D + 128)
+            owned = [
+                scatter(from_pairs(jnp.concatenate([part_a[:, D:], part_b[:, : 2 * D]], axis=1))),
+                scatter(part_a[:, :D]),
+                scatter(unpack_rows(grads[:, wide:])),
                 scatter(grads[:, :wide].reshape(FF, D)),
-                scatter(grads_first[:, 3 * D : 3 * D + cols]),
-            )
-            owned = tuple(g.astype(f32) for g in owned)
+                scatter(part_b[:, 2 * D : 2 * D + cols]),
+            ]
+            owned = [g.astype(f32) for g in owned]
             squares = lax.psum(sum(jnp.sum(g * g) for g in owned), AXES)
+            owned[4] = owned[4].T
         norm = jnp.sqrt(squares)
         factor = jnp.minimum(1.0, CLIP_LIMIT / (norm + 1e-06))
         taken = step[0].astype(f32)
@@ -667,12 +710,13 @@
             (weight_proj, first_proj, second_proj, 2.0 / math.sqrt(D // 48), 0.04),
             (weight_fc1, first_fc1, second_fc1, rate_in, 0.04),
             (weight_fc2, first_fc2, second_fc2, 2.0 / math.sqrt(FF), 0.04),
-            (vectors, first_vectors, second_vectors, 1.0, 0.0),
+            (vectors.T, first_vectors.T, second_vectors.T, 1.0, 0.0),
         )
         new = [
             adam_update(w, factor * g, m, v, rate, decay, fix_one, fix_two)
             for g, (w, m, v, rate, decay) in zip(owned, states)
         ]
+        new[4] = tuple(v.T for v in new[4])
         shape = (rows_dev, row, D)
         outs = [result.reshape(shape), grad_inputs.reshape(shape), norm.reshape(1)]
         outs += [w for w, _, _ in new]

time: 390 us -> 371 us (0.951)
  waiting for transfers between devices: 82.4 us -> 69.6 us
  starting transfers between devices: 21.1 us -> 32.5 us
  other arithmetic: 15.8 us -> 7.96 us
  local copies, waits for them, and re-layouts: 8.68 us -> 1.85 us
    ppermute x14 -> x24, starting transfers between devices: 18.1 us -> 29.4 us  [swap(): return lax.ppermute(value, axis, [(i, i ^ flip) for i in range(size)])]
    reduce_scatter x1, waiting for transfers between devices: 8.34 us -> 0.04 us  [local(): rest_owned = lax.psum_scatter(grads, AXES, scatter_dimension=0, tiled=False)]
    ppermute x14 -> x24, waiting for transfers between devices: 68 us -> 63.2 us  [swap(): return lax.ppermute(value, axis, [(i, i ^ flip) for i in range(size)])]
    unnamed x59 -> x36, local copies, waits for them, and re-layouts: 6.1 us -> 1.85 us
    pallas_call x7 -> x11, Pallas kernels: 97.3 us -> 94.5 us  [the longest x1 52.8 us: mlp_block(): pl.pallas_call(mlp_kernel, grid=(rows // BM,), in_specs=[tile(D), pl.Bloc...]
  transfers between devices with their start and end apart: 17 -> 27, of which waited for: 13 -> 14; matrix products, arithmetic and copies ran while one was open for 3% -> 0% of each run, Pallas kernels for 42% -> 44%
where the time goes in v4:
time: 371 us
  Pallas kernels  242 us (65%)
  waiting for transfers between devices  69.6 us (19%)
  starting transfers between devices  32.5 us (9%)
  between operations  16.4 us (4%)
  other arithmetic  7.96 us (2%)
    pallas_call x1, Pallas kernels, attn_bwd(): pl.pallas_call(bwd_kernel, grid=(6,), in_specs=[pl.BlockSpec(memory_space...  73.5 us
    ppermute x24, waiting for transfers between devices, swap(): return lax.ppermute(value, axis, [(i, i ^ flip) for i in range(size)])  63.2 us
    pallas_call x1, Pallas kernels, mlp_block(): pl.pallas_call(mlp_kernel, grid=(rows // BM,), in_specs=[tile(D), pl.Bloc...  52.8 us
    pallas_call x1, Pallas kernels, attn_fwd(): pl.pallas_call(fwd_kernel, grid=(6,), in_specs=[pl.BlockSpec(memory_space...  44.8 us
    ppermute x24, starting transfers between devices, swap(): return lax.ppermute(value, axis, [(i, i ^ flip) for i in range(size)])  29.4 us
    pallas_call x2, Pallas kernels, split_grad(): pl.pallas_call(split_kernel, grid=(2,), in_specs=[pl.BlockSpec(memory_spa...  13.3 us
    pallas_call x1, Pallas kernels, input_grad(): pl.pallas_call(input_kernel, grid=(rows // BM,), in_specs=[tile(D), tile(...  12.8 us
    pallas_call x1, Pallas kernels, qkv_forward(): pl.pallas_call(qkv_kernel, grid=(rows // BM,), in_specs=[pl.BlockSpec(mem...  12.3 us
  transfers between devices with their start and end apart: 27, of which 14 were waited for; matrix products, arithmetic and copies ran while one was open for 0% of the time, Pallas kernels for 44%

profile of v4, /device:TPU:0, one launch (start us, length us, event | category | flops | bytes accessed | tf_op | source)
XLA Modules:
  0.0 370.7 jit_solution(16003648246120097126)
XLA Ops:
  9.3 3.1 collective-permute-start
  17.0 7.5 %collective-permute-done.1 = bf16[24,2432]{1,0:T(8,128)(2,1)S(1)} collective-permute-done((bf16[24,2432]{1,0:T(8,128)(2,1)}, bf16[24,2432]{1,0:T(8,128)(2,1)S(1)}, u32[]{:S(2)}, u32[]{:S(2)}) %collective-permute-start.1) | collective-permute-done | bytes 116768 | tf_op jit(solution)/shard_map/ppermute | solution.py:564
  29.0 10.1 %collective-permute-done.4.refs_1_ = bf16[4,24,2432]{2,1,0:T(8,128)(2,1)S(1)} collective-permute-done((bf16[4,24,2432]{2,1,0:T(8,128)(2,1)S(1)}, bf16[4,24,2432]{2,1,0:T(8,128)(2,1)S(1)}, u32[]{:S(2)}, u32[]{:S(2)}) %collective-permute-start.4) | collective-permute-done | bytes 466976 | tf_op jit(solution)/shard_map/ppermute | solution.py:564
  39.7 5.1 %norm_input.1 = (f32[1536,768]{1,0:T(8,128)}, f32[1536,128]{1,0:T(8,128)}) custom-call(bf16[1536,768]{1,0:T(8,128)(2,1)} %bitcast.49), custom_call_target="tpu_custom_call" | custom-call | flops 1000 | bytes 1000 | tf_op jit(solution)/shard_map/norm_input/pallas_call | solution.py:253
  44.8 8.9 %collective-permute-done.3.refs_3_ = bf16[4,24,2432]{2,1,0:T(8,128)(2,1)S(1)} collective-permute-done((bf16[4,24,2432]{2,1,0:T(8,128)(2,1)S(1)}, bf16[4,24,2432]{2,1,0:T(8,128)(2,1)S(1)}, u32[]{:S(2)}, u32[]{:S(2)}) %collective-permute-start.3) | collective-permute-done | bytes 466976 | tf_op jit(solution)/shard_map/ppermute | solution.py:564
  55.8 12.3 %qkv_forward.1 = (bf16[1536,1536]{1,0:T(8,128)(2,1)}, bf16[1536,2304]{1,0:T(8,128)(2,1)}, f32[16,768]{1,0:T(8,128)}, bf16[4,4,2,24,2432]{4,3,2,1,0:T(8,128)(2,1)}) custom-call(s32[3]{0:T(128)} %pad_add_fusion.place_ref, f32[1536,768]{1,0:T(8,128)} %get-tuple-element.92.n_ref, bf16[4,24,2432]{2,1,0:T(8,128)(2,1)} %copy-done.5, ...), custom_call_target="tpu_custom_call" | custom-call | flops 5435817984 | bytes 18874368 | tf_op jit(solution)/shard_map/qkv_forward/pallas_call | solution.py:317
  68.1 44.8 %attn_fwd.1 = (bf16[1536,1536]{1,0:T(8,128)(2,1)}, f32[6,8,1536]{2,1,0:T(8,128)}) custom-call(s32[1,6]{1,0:T(1,128)} %len_ref.3, bf16[1536,2304]{1,0:T(8,128)(2,1)} %get-tuple-element.100.qkv_ref, bf16[1536,1536]{1,0:T(8,128)(2,1)} %get-tuple-element.101.left_ref), custom_call_target="tpu_custom_call", output_to_operand_aliasing={{0}: (2, {})} | custom-call | flops 7247757312 | bytes 10485760 | tf_op jit(solution)/shard_map/attn_fwd/pallas_call | solution.py:143
  112.9 52.8 %mlp_block.1 = (bf16[1536,768]{1,0:T(8,128)(2,1)}, bf16[1536,768]{1,0:T(8,128)(2,1)}, bf16[1536,768]{1,0:T(8,128)(2,1)}, bf16[1536,3072]{1,0:T(8,128)(2,1)}, bf1...) custom-call(bf16[1536,768]{1,0:T(8,128)(2,1)} %bitcast.50, ...), custom_call_target="tpu_custom_call" | custom-call | flops 32614907904 | bytes 50331648 | tf_op jit(solution)/shard_map/mlp_block/pallas_call | solution.py:399
  165.7 11.7 %fc2_grad.1.old_ref = bf16[32,192,768]{2,1,0:T(8,128)(2,1)} custom-call(bf16[1536,3072]{1,0:T(8,128)(2,1)} %get-tuple-element.152.a_ref, bf16[1536,768]{1,0:T(8,128)(2,1)} %get-tuple-element.153.b_ref), custom_call_target="tpu_custom_call" | custom-call | flops 7247757312 | bytes 16777216 | tf_op jit(solution)/shard_map/fc2_grad/pallas_call | solution.py:415
  177.4 11.7 %fc1_grad.1 = bf16[32,192,768]{2,1,0:T(8,128)(2,1)} custom-call(bf16[1536,768]{1,0:T(8,128)(2,1)} %get-tuple-element.150.a_ref, bf16[1536,3072]{1,0:T(8,128)(2,1)} %get-tuple-element.151.b_ref, bf16[32,192,768]{2,1,0:T(8,128)(2,1)} %fc2_grad.1.old_ref), custom_call_target="tpu_custom_call", output_to_operand_aliasing={{}: (2, {})} | custom-call | flops 7247757312 | bytes 20971520 | tf_op jit(solution)/shard_map/fc1_grad/pallas_call | solution.py:430
  189.1 73.5 %attn_bwd.1.right_ref.d_ref = bf16[1536,3072]{1,0:T(8,128)(2,1)} custom-call(s32[1,6]{1,0:T(1,128)} %len_ref.3, bf16[1536,2304]{1,0:T(8,128)(2,1)} %get-tuple-element.100.qkv_ref, bf16[1536,1536]{1,0:T(8,128)(2,1)} %get-tuple-element.102.o_ref.left_ref, bf16[1536,768]{1,0:T(8,128)(2,1)} %get-tuple-element.107.do_ref, ...), custom_call_target="tpu_custom_call", output_to_operand_aliasing={{}: (5, {})} | custom-call | flops 18119393280 | bytes 20971520 | tf_op jit(solution)/shard_map/attn_bwd/pallas_call | solution.py:208
  262.6 6.6 %split_grad.2 = (bf16[16,24,1536]{2,1,0:T(8,128)(2,1)S(1)}, bf16[16,24,1536]{2,1,0:T(8,128)(2,1)S(1)}) custom-call(s32[1]{0:T(128)} %bitcast.3.core_ref, bf16[1536,1536]{1,0:T(8,128)(2,1)} %get-tuple-element.102.o_ref.left_ref, bf16[1536,3072]{1,0:T(8,128)(2,1)} %attn_bwd.1.right_ref.d_ref), custom_call_target="tpu_custom_call" | custom-call | flops 1000 | bytes 1000 | tf_op jit(solution)/shard_map/split_grad/pallas_call | solution.py:460
  269.4 2.7 collective-permute-done.10
  276.4 12.8 %input_grad.1 = (bf16[1536,768]{1,0:T(8,128)(2,1)}, f32[16,768]{1,0:T(8,128)}) custom-call(f32[1536,768]{1,0:T(8,128)} %get-tuple-element.92.n_ref, f32[1536,128]{1,0:T(8,128)} %get-tuple-element.106.r_ref, bf16[1536,3072]{1,0:T(8,128)(2,1)} %attn_bwd.1.right_ref.d_ref, f32[1536,768]{1,0:T(8,128)} %get-tuple-element.110.dx1_ref, ...), custom_call_target="tpu_custom_call" | custom-call | flops 1000 | bytes 1000 | tf_op jit(solution)/shard_map/input_grad/pallas_call | solution.py:489
  293.4 2.7 collective-permute-start.15
  298.3 6.7 %split_grad.3 = (bf16[16,24,1664]{2,1,0:T(8,128)(2,1)S(1)}, bf16[16,24,1664]{2,1,0:T(8,128)(2,1)S(1)}) custom-call(s32[1]{0:T(128)} %bitcast.3.core_ref, bf16[1536,1536]{1,0:T(8,128)(2,1)} %get-tuple-element.102.o_ref.left_ref, bf16[1536,3072]{1,0:T(8,128)(2,1)} %attn_bwd.1.right_ref.d_ref, f32[16,768]{1,0:T(8,128)S(1)} %copy-done.1), custom_call_target="tpu_custom_call" | custom-call | flops 1000 | bytes 1000 | tf_op jit(solution)/shard_map/split_grad/pallas_call | solution.py:460
  305.1 2.7 collective-permute-done.16.refs_3_
  307.8 3.0 collective-permute-done.17
  314.6 6.9 %collective-permute-done.18.refs_1_ = bf16[4,24,1664]{2,1,0:T(8,128)(2,1)S(1)} collective-permute-done((bf16[4,24,1664]{2,1,0:T(8,128)(2,1)S(1)}, bf16[4,24,1664]{2,1,0:T(8,128)(2,1)S(1)}, u32[]{:S(2)}, u32[]{:S(2)}) %collective-permute-start.18) | collective-permute-done | bytes 319520 | tf_op jit(solution)/shard_map/ppermute | solution.py:564
  321.5 8.6 %collective-permute-done.19.refs_2_ = bf16[4,24,1664]{2,1,0:T(8,128)(2,1)S(1)} collective-permute-done((bf16[4,24,1664]{2,1,0:T(8,128)(2,1)S(1)}, bf16[4,24,1664]{2,1,0:T(8,128)(2,1)S(1)}, u32[]{:S(2)}, u32[]{:S(2)}) %collective-permute-start.19) | collective-permute-done | bytes 319520 | tf_op jit(solution)/shard_map/ppermute | solution.py:564
  330.3 3.8 %collective-permute-start.21 = (bf16[24,1664]{1,0:T(8,128)(2,1)S(1)}, bf16[24,1664]{1,0:T(8,128)(2,1)S(1)}, u32[]{:S(2)}, u32[]{:S(2)}) collective-permute-start(bf16[24,1664]{1,0:T(8,128)(2,1)S(1)} %get-tuple-element.147), channel_id=1, source_target_pairs={{0,2},{1,3},{2,0},{3,1},{4,6},{5,7},{6,4},{7,5},{8,10},{9,11},{10,... | collective-permute-start | bytes 239624 | tf_op jit(solution)/shard_map/ppermute | solution.py:564
  337.5 6.5 %collective-permute-done.22.refs_6_ = bf16[24,1664]{1,0:T(8,128)(2,1)S(1)} collective-permute-done((bf16[24,1664]{1,0:T(8,128)(2,1)S(1)}, bf16[24,1664]{1,0:T(8,128)(2,1)S(1)}, u32[]{:S(2)}, u32[]{:S(2)}) %collective-permute-start.22) | collective-permute-done | bytes 79904 | tf_op jit(solution)/shard_map/ppermute | solution.py:564
  346.1 3.0 all-to-all-start
  349.9 6.3 %all-to-all-done = f32[32,1,128]{2,1,0:T(1,128)S(1)} async-done(((f32[32,1,128]{2,1,0:T(1,128)}), f32[32,1,128]{2,1,0:T(1,128)S(1)}, u32[]{:S(2)}, u32[]{:S(2)}) %all-to-all-start) | async-done | bytes 16416 | tf_op jit(solution)/shard_map/all_to_all | solution.py:686
  (92 shorter events, 40.5 us)
Async XLA Ops:
  7.2 105.7 %all-gather.3.cloned.1.call-start = ((), (), s32[]{:S(2)}) async-start(), calls=%async_computation.3 | async-start | bytes 10948608 | tf_op jit(solution)/shard_map/all_gather | solution.py:632
  9.3 334.8 %reduce-scatter.2.cloned.1.call-start = ((), (), s32[]{:S(2)}) async-start(), calls=%async_computation.2 | async-start | bytes 9732096 | tf_op jit(solution)/shard_map/reduce_scatter | solution.py:660
  9.3 7.7 %collective-permute-start = (bf16[24,2432]{1,0:T(8,128)(2,1)}, bf16[24,2432]{1,0:T(8,128)(2,1)S(1)}, u32[]{:S(2)}, u32[]{:S(2)}) collective-permute-start(bf16[24,2432]{1,0:T(8,128)(2,1)} %get-tuple-element.89), channel_id=1, source_target_pairs={{0,2},{1,3},{2,0},{3,1},{4,6},{5,7},{6,4},{7,5},{8,10},{9,11},{10,... | collective-permute-start | bytes 350216 | tf_op jit(solution)/shard_map/ppermute | solution.py:564
  12.4 12.1 %collective-permute-start.1 = (bf16[24,2432]{1,0:T(8,128)(2,1)}, bf16[24,2432]{1,0:T(8,128)(2,1)S(1)}, u32[]{:S(2)}, u32[]{:S(2)}) collective-permute-start(bf16[24,2432]{1,0:T(8,128)(2,1)} %get-tuple-element.89), channel_id=1, source_target_pairs={{0,4},{1,5},{2,6},{3,7},{4,0},{5,1},{6,2},{7,3},{8,12},{9,13},{10,... | collective-permute-start | bytes 350216 | tf_op jit(solution)/shard_map/ppermute | solution.py:564
  15.0 9.5 %collective-permute-start.2 = (bf16[24,2432]{1,0:T(8,128)(2,1)}, bf16[24,2432]{1,0:T(8,128)(2,1)S(1)}, u32[]{:S(2)}, u32[]{:S(2)}) collective-permute-start(bf16[24,2432]{1,0:T(8,128)(2,1)} %get-tuple-element.89), channel_id=1, source_target_pairs={{0,6},{1,7},{2,4},{3,5},{4,2},{5,3},{6,0},{7,1},{8,14},{9,15},{10,... | collective-permute-start | bytes 350216 | tf_op jit(solution)/shard_map/ppermute | solution.py:564
  25.5 13.7 %collective-permute-start.4 = (bf16[4,24,2432]{2,1,0:T(8,128)(2,1)S(1)}, bf16[4,24,2432]{2,1,0:T(8,128)(2,1)S(1)}, u32[]{:S(2)}, u32[]{:S(2)}) collective-permute-start(bf16[4,24,2432]{2,1,0:T(8,128)(2,1)S(1)} %pad_maximum_fusion.refs_0_), channel_id=1, source_target_pairs={{0,8},{8,0},{16,24},{24,16},{1,9},{9,1},{17,25},{25,17},{2,10},{10... | collective-permute-start | bytes 1400840 | tf_op jit(solution)/shard_map/ppermute | solution.py:564
  27.0 12.1 %collective-permute-start.5 = (bf16[4,24,2432]{2,1,0:T(8,128)(2,1)S(1)}, bf16[4,24,2432]{2,1,0:T(8,128)(2,1)S(1)}, u32[]{:S(2)}, u32[]{:S(2)}) collective-permute-start(bf16[4,24,2432]{2,1,0:T(8,128)(2,1)S(1)} %pad_maximum_fusion.refs_0_), channel_id=1, source_target_pairs={{0,16},{8,24},{16,0},{24,8},{1,17},{9,25},{17,1},{25,9},{2,18},{10... | collective-permute-start | bytes 1400840 | tf_op jit(solution)/shard_map/ppermute | solution.py:564
  28.6 25.1 %collective-permute-start.3 = (bf16[4,24,2432]{2,1,0:T(8,128)(2,1)S(1)}, bf16[4,24,2432]{2,1,0:T(8,128)(2,1)S(1)}, u32[]{:S(2)}, u32[]{:S(2)}) collective-permute-start(bf16[4,24,2432]{2,1,0:T(8,128)(2,1)S(1)} %pad_maximum_fusion.refs_0_), channel_id=1, source_target_pairs={{0,24},{8,16},{16,8},{24,0},{1,25},{9,17},{17,9},{25,1},{2,26},{10... | collective-permute-start | bytes 1400840 | tf_op jit(solution)/shard_map/ppermute | solution.py:564
  29.0 24.7 %collective-permute-start.6 = (bf16[4,24,2432]{2,1,0:T(8,128)(2,1)S(1)}, bf16[4,24,2432]{2,1,0:T(8,128)(2,1)}, u32[]{:S(2)}, u32[]{:S(2)}) collective-permute-start(bf16[4,24,2432]{2,1,0:T(8,128)(2,1)S(1)} %pad_maximum_fusion.refs_0_), channel_id=1, source_target_pairs={{0,1},{1,0},{2,3},{3,2},{4,5},{5,4},{6,7},{7,6},{8,9},{9,8},{10,11... | collective-permute-start | bytes 1400840 | tf_op jit(solution)/shard_map/ppermute | solution.py:564
  39.2 14.5 %collective-permute-start.7 = (bf16[4,24,2432]{2,1,0:T(8,128)(2,1)S(1)}, bf16[4,24,2432]{2,1,0:T(8,128)(2,1)}, u32[]{:S(2)}, u32[]{:S(2)}) collective-permute-start(bf16[4,24,2432]{2,1,0:T(8,128)(2,1)S(1)} %collective-permute-done.4.refs_1_), channel_id=1, source_target_pairs={{0,1},{1,0},{2,3},{3,2},{4,5},{5,4},{6,7},{7,6},{8,9},{9,8},{10,11... | collective-permute-start | bytes 1400840 | tf_op jit(solution)/shard_map/ppermute | solution.py:564
  39.2 14.5 %collective-permute-start.8 = (bf16[4,24,2432]{2,1,0:T(8,128)(2,1)S(1)}, bf16[4,24,2432]{2,1,0:T(8,128)(2,1)}, u32[]{:S(2)}, u32[]{:S(2)}) collective-permute-start(bf16[4,24,2432]{2,1,0:T(8,128)(2,1)S(1)} %collective-permute-done.5.refs_2_), channel_id=1, source_target_pairs={{0,1},{1,0},{2,3},{3,2},{4,5},{5,4},{6,7},{7,6},{8,9},{9,8},{10,11... | collective-permute-start | bytes 1400840 | tf_op jit(solution)/shard_map/ppermute | solution.py:564
  272.9 16.3 %collective-permute-start.11 = (bf16[4,24,1536]{2,1,0:T(8,128)(2,1)}, bf16[4,24,1536]{2,1,0:T(8,128)(2,1)S(1)}, u32[]{:S(2)}, u32[]{:S(2)}) collective-permute-start(bf16[4,24,1536]{2,1,0:T(8,128)(2,1)} %get-tuple-element.122), channel_id=1, source_target_pairs={{0,8},{8,0},{16,24},{24,16},{1,9},{9,1},{17,25},{25,17},{2,10},{10... | collective-permute-start | bytes 884744 | tf_op jit(solution)/shard_map/ppermute | solution.py:564
  274.4 14.8 %collective-permute-start.12 = (bf16[4,24,1536]{2,1,0:T(8,128)(2,1)S(1)}, bf16[4,24,1536]{2,1,0:T(8,128)(2,1)S(1)}, u32[]{:S(2)}, u32[]{:S(2)}) collective-permute-start(bf16[4,24,1536]{2,1,0:T(8,128)(2,1)S(1)} %get-tuple-element.123), channel_id=1, source_target_pairs={{0,16},{8,24},{16,0},{24,8},{1,17},{9,25},{17,1},{25,9},{2,18},{10... | collective-permute-start | bytes 884744 | tf_op jit(solution)/shard_map/ppermute | solution.py:564
  274.9 16.4 %collective-permute-start.13 = (bf16[4,24,1536]{2,1,0:T(8,128)(2,1)S(1)}, bf16[4,24,1536]{2,1,0:T(8,128)(2,1)S(1)}, u32[]{:S(2)}, u32[]{:S(2)}) collective-permute-start(bf16[4,24,1536]{2,1,0:T(8,128)(2,1)S(1)} %get-tuple-element.124), channel_id=1, source_target_pairs={{0,24},{8,16},{16,8},{24,0},{1,25},{9,17},{17,9},{25,1},{2,26},{10... | collective-permute-start | bytes 884744 | tf_op jit(solution)/shard_map/ppermute | solution.py:564
  291.4 13.6 %collective-permute-start.14 = (bf16[24,1536]{1,0:T(8,128)(2,1)S(1)}, bf16[24,1536]{1,0:T(8,128)(2,1)S(1)}, u32[]{:S(2)}, u32[]{:S(2)}) collective-permute-start(bf16[24,1536]{1,0:T(8,128)(2,1)S(1)} %get-tuple-element.131), channel_id=1, source_target_pairs={{0,2},{1,3},{2,0},{3,1},{4,6},{5,7},{6,4},{7,5},{8,10},{9,11},{10,... | collective-permute-start | bytes 221192 | tf_op jit(solution)/shard_map/ppermute | solution.py:564
  293.4 11.7 %collective-permute-start.15 = (bf16[24,1536]{1,0:T(8,128)(2,1)S(1)}, bf16[24,1536]{1,0:T(8,128)(2,1)S(1)}, u32[]{:S(2)}, u32[]{:S(2)}) collective-permute-start(bf16[24,1536]{1,0:T(8,128)(2,1)S(1)} %get-tuple-element.132), channel_id=1, source_target_pairs={{0,4},{1,5},{2,6},{3,7},{4,0},{5,1},{6,2},{7,3},{8,12},{9,13},{10,... | collective-permute-start | bytes 221192 | tf_op jit(solution)/shard_map/ppermute | solution.py:564
  296.1 11.6 %collective-permute-start.16 = (bf16[24,1536]{1,0:T(8,128)(2,1)S(1)}, bf16[24,1536]{1,0:T(8,128)(2,1)S(1)}, u32[]{:S(2)}, u32[]{:S(2)}) collective-permute-start(bf16[24,1536]{1,0:T(8,128)(2,1)S(1)} %get-tuple-element.133), channel_id=1, source_target_pairs={{0,6},{1,7},{2,4},{3,5},{4,2},{5,3},{6,0},{7,1},{8,14},{9,15},{10,... | collective-permute-start | bytes 221192 | tf_op jit(solution)/shard_map/ppermute | solution.py:564
  311.1 10.4 %collective-permute-start.18 = (bf16[4,24,1664]{2,1,0:T(8,128)(2,1)S(1)}, bf16[4,24,1664]{2,1,0:T(8,128)(2,1)S(1)}, u32[]{:S(2)}, u32[]{:S(2)}) collective-permute-start(bf16[4,24,1664]{2,1,0:T(8,128)(2,1)S(1)} %get-tuple-element.143), channel_id=1, source_target_pairs={{0,8},{8,0},{16,24},{24,16},{1,9},{9,1},{17,25},{25,17},{2,10},{10... | collective-permute-start | bytes 958472 | tf_op jit(solution)/shard_map/ppermute | solution.py:564
  312.4 17.7 %collective-permute-start.19 = (bf16[4,24,1664]{2,1,0:T(8,128)(2,1)S(1)}, bf16[4,24,1664]{2,1,0:T(8,128)(2,1)S(1)}, u32[]{:S(2)}, u32[]{:S(2)}) collective-permute-start(bf16[4,24,1664]{2,1,0:T(8,128)(2,1)S(1)} %get-tuple-element.144), channel_id=1, source_target_pairs={{0,16},{8,24},{16,0},{24,8},{1,17},{9,25},{17,1},{25,9},{2,18},{10... | collective-permute-start | bytes 958472 | tf_op jit(solution)/shard_map/ppermute | solution.py:564
  313.2 17.0 %collective-permute-start.20 = (bf16[4,24,1664]{2,1,0:T(8,128)(2,1)S(1)}, bf16[4,24,1664]{2,1,0:T(8,128)(2,1)S(1)}, u32[]{:S(2)}, u32[]{:S(2)}) collective-permute-start(bf16[4,24,1664]{2,1,0:T(8,128)(2,1)S(1)} %get-tuple-element.145), channel_id=1, source_target_pairs={{0,24},{8,16},{16,8},{24,0},{1,25},{9,17},{17,9},{25,1},{2,26},{10... | collective-permute-start | bytes 958472 | tf_op jit(solution)/shard_map/ppermute | solution.py:564
  330.3 7.2 %collective-permute-start.21 = (bf16[24,1664]{1,0:T(8,128)(2,1)S(1)}, bf16[24,1664]{1,0:T(8,128)(2,1)S(1)}, u32[]{:S(2)}, u32[]{:S(2)}) collective-permute-start(bf16[24,1664]{1,0:T(8,128)(2,1)S(1)} %get-tuple-element.147), channel_id=1, source_target_pairs={{0,2},{1,3},{2,0},{3,1},{4,6},{5,7},{6,4},{7,5},{8,10},{9,11},{10,... | collective-permute-start | bytes 239624 | tf_op jit(solution)/shard_map/ppermute | solution.py:564
  334.1 9.9 %collective-permute-start.22 = (bf16[24,1664]{1,0:T(8,128)(2,1)S(1)}, bf16[24,1664]{1,0:T(8,128)(2,1)S(1)}, u32[]{:S(2)}, u32[]{:S(2)}) collective-permute-start(bf16[24,1664]{1,0:T(8,128)(2,1)S(1)} %get-tuple-element.148), channel_id=1, source_target_pairs={{0,4},{1,5},{2,6},{3,7},{4,0},{5,1},{6,2},{7,3},{8,12},{9,13},{10,... | collective-permute-start | bytes 239624 | tf_op jit(solution)/shard_map/ppermute | solution.py:564
  335.3 8.8 %collective-permute-start.23 = (bf16[24,1664]{1,0:T(8,128)(2,1)S(1)}, bf16[24,1664]{1,0:T(8,128)(2,1)S(1)}, u32[]{:S(2)}, u32[]{:S(2)}) collective-permute-start(bf16[24,1664]{1,0:T(8,128)(2,1)S(1)} %get-tuple-element.149), channel_id=1, source_target_pairs={{0,6},{1,7},{2,4},{3,5},{4,2},{5,3},{6,0},{7,1},{8,14},{9,15},{10,... | collective-permute-start | bytes 239624 | tf_op jit(solution)/shard_map/ppermute | solution.py:564
  346.1 10.1 %all-to-all-start = ((f32[32,1,128]{2,1,0:T(1,128)}), f32[32,1,128]{2,1,0:T(1,128)S(1)}, u32[]{:S(2)}, u32[]{:S(2)}) async-start(f32[32,1,128]{2,1,0:T(1,128)} %bitcast.19), calls=%async_computation.1 | async-start | bytes 32768 | tf_op jit(solution)/shard_map/all_to_all | solution.py:686
  (21 other events, 688.3 us)
Sparse Core Ops, SparseCore 0:
  11.0 95.4 all-gather.2
  189.3 154.7 reduce-scatter.1

commit v5 on v4

--- a/solution.py
+++ b/solution.py
@@ -326,14 +326,17 @@
 CH=768
 
 
-def mlp_kernel(x_ref,o_ref,dy_ref,vec_ref,w2_ref,wa_ref,wb_ref,wc_ref,wd_ref,wp_ref,
+def mlp_kernel(x_ref,o_ref,dy_ref,vec_ref,rest_ref,wp_ref,
                out_ref,h_ref,dm_ref,z_ref,du_ref,dx_ref,da_ref,do_ref,sum_ref,
-               a_s,x1_s,n2_s,mo_s,dh_s,ua,ub,ga,gb,w1_s):
+               a_s,x1_s,n2_s,mo_s,dh_s,ua,ub,ga,gb,w1_s,w2_s,sems):
     step=pl.program_id(0)
+    r=wp_ref.shape[1]
+    copies=[pltpu.make_async_copy(rest_ref.at[:,0:4*r],w2_s,sems.at[4])]
+    copies+=[pltpu.make_async_copy(rest_ref.at[:,(4+b)*r:(5+b)*r],w1_s.at[b],sems.at[b]) for b in range(4)]
     @pl.when(step==0)
     def _():
-        for b,ref in enumerate((wa_ref,wb_ref,wc_ref,wd_ref)):
-            w1_s[b]=ref[...].reshape(D,D)
+        for copy in copies:
+            copy.start()
         sum_ref[...]=jnp.zeros_like(sum_ref)
     row=lambda i: vec_ref[i:i+1,:]
     def add(i,v):
@@ -353,9 +356,13 @@
     mo_s[...]=jnp.zeros_like(mo_s)
     dh_s[...]=jnp.zeros_like(dh_s)
     def w2(c):
-        return w2_ref[pl.ds(8*c,8)].reshape(D,D)
+        return w2_s[pl.ds(8*c,8)].reshape(D,D)
+    @pl.when(step==0)
+    def _():
+        for copy in copies:
+            copy.wait()
     def up(c,u,g):
-        u[...]=nn(h_ref[...],w1_s[c])
+        u[...]=nn(h_ref[...],w1_s[c].reshape(D,D))
         g[...]=nt(dm_ref[...],w2(c))
     def down(c,u,g):
         cols=pl.ds(pl.multiple_of(c*CH,CH),CH)
@@ -368,7 +375,7 @@
         du_ref[:,cols]=du
         sum_ref[pl.ds(8+c,1),:]+=jnp.sum(du.astype(f32),axis=0,keepdims=True)
         mo_s[...]+=nn(z,w2(c))
-        dh_s[...]+=nt(du,w1_s[c])
+        dh_s[...]+=nt(du,w1_s[c].reshape(D,D))
     def body(i,carry):
         up(2*i,ua,ga)
         up(2*i+1,ub,gb)
@@ -397,12 +404,12 @@
     n,r=packed.shape[0],D//packed.shape[0]
     sd=jax.ShapeDtypeStruct
     return pl.pallas_call(mlp_kernel,grid=(rows//BM,),
-        in_specs=[tile(D),pl.BlockSpec((BM,D),lambda i:(i,1)),tile(D),once((16,D)),once((n,4*r,D))]+[once((n,r,D),lambda i,b=b:(0,b,0)) for b in range(4,9)],
+        in_specs=[tile(D),pl.BlockSpec((BM,D),lambda i:(i,1)),tile(D),once((16,D)),pl.BlockSpec(memory_space=pl.ANY),once((n,r,D),lambda i:(0,8,0))],
         out_specs=[tile(D),tile(D),tile(D),tile(FF),tile(FF),tile(D),pl.BlockSpec((BM,D),lambda i:(i,3)),tile(D),pl.BlockSpec((16,D),lambda i:(0,0))],
         out_shape=[sd((rows,D),bf),sd((rows,D),bf),sd((rows,D),bf),sd((rows,FF),bf),sd((rows,FF),bf),sd((rows,D),f32),sd((rows,4*D),bf),sd((rows,D),bf),sd((16,D),f32)],
-        scratch_shapes=[pltpu.VMEM((BM,D),f32)]*5+[pltpu.VMEM((BM,CH),f32)]*4+[pltpu.VMEM((4,D,D),bf)],
+        scratch_shapes=[pltpu.VMEM((BM,D),f32)]*5+[pltpu.VMEM((BM,CH),f32)]*4+[pltpu.VMEM((4,n,r,D),bf),pltpu.VMEM((n,4*r,D),bf),pltpu.SemaphoreType.DMA((5,))],
         compiler_params=params(),name="mlp_block",
-        cost_estimate=pl.CostEstimate(flops=2*rows*D*(2*D+4*FF),bytes_accessed=48<<20,transcendentals=0))(x,o,dy,vec,*[packed]*6)
+        cost_estimate=pl.CostEstimate(flops=2*rows*D*(2*D+4*FF),bytes_accessed=48<<20,transcendentals=0))(x,o,dy,vec,packed,packed)
 
 
 def outer_kernel(a_ref,b_ref,g_ref):
@@ -535,19 +542,41 @@
     near=pl.BlockSpec(memory_space=pltpu.VMEM)
     r=rest.shape[0]//8
     shapes=[(r,3*D),(r,D),(r,FF),(4*r,D),(128,r),(PACK,128)]
-    return pl.pallas_call(finish_kernel,
+    return pl.pallas_call(finish_kernel,grid=(1,),
         in_specs=[near]*9,
-        out_specs=[near]*6,
+        out_specs=[pl.BlockSpec(v,lambda i:(0,0)) for v in shapes[:5]]+[near],
         out_shape=[jax.ShapeDtypeStruct(v,f32) for v in shapes],
-        compiler_params=pltpu.CompilerParams(vmem_limit_bytes=24<<20),name="finish_sum",
+        compiler_params=pltpu.CompilerParams(vmem_limit_bytes=58<<20),name="finish_sum",
         cost_estimate=pl.CostEstimate(flops=1000,bytes_accessed=1000,transcendentals=0))(*first,*second,rest)
 
 
-def adam_update(weight, grad, first, second, rate, decay, fix_one, fix_two):
-    first = BETA_ONE * first + (1.0 - BETA_ONE) * grad
-    second = BETA_TWO * second + (1.0 - BETA_TWO) * grad * grad
-    stride = first / fix_one / (jnp.sqrt(second / fix_two) + ADAM_EPS)
-    return (weight - rate * (stride + decay * weight), first, second)
+RATES=((2.0/math.sqrt(D),0.04),(2.0/math.sqrt(D//48),0.04),(2.0/math.sqrt(D),0.04),(2.0/math.sqrt(FF),0.04),(1.0,0.0))
+
+
+def adam_kernel(fix_ref,square_ref,*refs):
+    grads,states,outs=refs[:5],refs[5:20],refs[20:]
+    norm=jnp.sqrt(jnp.sum(square_ref[...],axis=0,keepdims=True)[:,0:1])
+    outs[0][...]=norm
+    factor=jnp.minimum(1.0,CLIP_LIMIT/(norm+1e-06))
+    for k,(rate,decay) in enumerate(RATES):
+        weight,first,second=(ref[...] for ref in states[3*k:3*k+3])
+        grad=factor*grads[k][0:weight.shape[0],:]
+        first=BETA_ONE*first+(1.0-BETA_ONE)*grad
+        second=BETA_TWO*second+(1.0-BETA_TWO)*grad*grad
+        stride=first/fix_ref[0]/(jnp.sqrt(second/fix_ref[1])+ADAM_EPS)
+        outs[3*k+1][...]=weight-rate*(stride+decay*weight)
+        outs[3*k+2][...]=first
+        outs[3*k+3][...]=second
+
+
+def adam_all(fix,squares,grads,states):
+    whole=lambda v: pl.BlockSpec(v,lambda i:(0,0))
+    shapes=[(1,1)]+[v.shape for v in states]
+    return pl.pallas_call(adam_kernel,grid=(1,),
+        in_specs=[pl.BlockSpec(memory_space=pltpu.SMEM)]+[whole(v.shape) for v in (squares,*grads,*states)],
+        out_specs=[whole(v) for v in shapes],
+        out_shape=[jax.ShapeDtypeStruct(v,f32) for v in shapes],
+        compiler_params=params(),name="adam_all")(fix,squares,*grads,*states)
 
 
 def pack_rows(full):
@@ -682,8 +711,7 @@
             *owned_a, other_b = lax.optimization_barrier((*owned_a, other_b))
             owned_b = third_stage(second_stage(me_z, first_stage(me_dp, mine_b, other_b)))
             *owned, squares = finish_sum(owned_a, owned_b, rest_owned)
-            owned[4] = owned[4][:cols]
-            squares = jnp.sum(lax.all_to_all(squares, AXES, 0, 0, tiled=True), axis=0)[0]
+            squares = lax.all_to_all(squares, AXES, 0, 0, tiled=True)
         else:
             mine_b, other_b = split_grad(core, left, right, sums)
             wide = FF // PACK
@@ -697,31 +725,18 @@
                 scatter(part_b[:, 2 * D : 2 * D + cols]),
             ]
             owned = [g.astype(f32) for g in owned]
-            squares = lax.psum(sum(jnp.sum(g * g) for g in owned), AXES)
+            squares = jnp.full((1, 128), lax.psum(sum(jnp.sum(g * g) for g in owned), AXES))
             owned[4] = owned[4].T
-        norm = jnp.sqrt(squares)
-        factor = jnp.minimum(1.0, CLIP_LIMIT / (norm + 1e-06))
         taken = step[0].astype(f32)
-        fix_one = 1.0 - jnp.power(BETA_ONE, taken)
-        fix_two = 1.0 - jnp.power(BETA_TWO, taken)
-        rate_in = 2.0 / math.sqrt(D)
-        states = (
-            (weight_qkv, first_qkv, second_qkv, rate_in, 0.04),
-            (weight_proj, first_proj, second_proj, 2.0 / math.sqrt(D // 48), 0.04),
-            (weight_fc1, first_fc1, second_fc1, rate_in, 0.04),
-            (weight_fc2, first_fc2, second_fc2, 2.0 / math.sqrt(FF), 0.04),
-            (vectors.T, first_vectors.T, second_vectors.T, 1.0, 0.0),
-        )
-        new = [
-            adam_update(w, factor * g, m, v, rate, decay, fix_one, fix_two)
-            for g, (w, m, v, rate, decay) in zip(owned, states)
-        ]
-        new[4] = tuple(v.T for v in new[4])
+        fix = jnp.stack([1.0 - jnp.power(BETA_ONE, taken), 1.0 - jnp.power(BETA_TWO, taken)])
+        states = (weight_qkv, first_qkv, second_qkv, weight_proj, first_proj, second_proj)
+        states += (weight_fc1, first_fc1, second_fc1, weight_fc2, first_fc2, second_fc2)
+        norm, *new = adam_all(fix, squares, owned, states + (vectors.T, first_vectors.T, second_vectors.T))
+        new[12:] = [v.T for v in new[12:]]
         shape = (rows_dev, row, D)
-        outs = [result.reshape(shape), grad_inputs.reshape(shape), norm.reshape(1)]
-        outs += [w for w, _, _ in new]
-        for _, m, v in new:
-            outs += [m, v]
+        outs = [result.reshape(shape), grad_inputs.reshape(shape), norm.reshape(1)] + new[0::3]
+        for k in range(5):
+            outs += new[3 * k + 1 : 3 * k + 3]
         return tuple(outs)
 
     return local

time: 371 us -> 368 us (level)
  other arithmetic: 7.96 us -> 2.16 us
  Pallas kernels: 242 us -> 246 us
    sub x4 -> x0, other arithmetic: 5.72 us -> none  [adam_update(): return (weight - rate * (stride + decay * weight), first, second)]
    pallas_call x1 -> x2, Pallas kernels: 1.04 us -> 6.24 us  [the longest x1 3.92 us: adam_all(): pl.pallas_call(adam_kernel, grid=(1,), in_specs=[pl.BlockSpec(memory_spac...]
  transfers between devices with their start and end apart: 27 -> 27, of which waited for: 14 -> 13; matrix products, arithmetic and copies ran while one was open for 0% -> 1% of each run, Pallas kernels for 44% -> 44%
where the time goes in v5:
time: 368 us; the launch traced here: 367 us
  Pallas kernels  246 us (67%)
  waiting for transfers between devices  68.5 us (19%)
  starting transfers between devices  32.5 us (9%)
  between operations  15.1 us (4%)
    pallas_call x1, Pallas kernels, attn_bwd(): pl.pallas_call(bwd_kernel, grid=(6,), in_specs=[pl.BlockSpec(memory_space...  73.5 us
    ppermute x24, waiting for transfers between devices, swap(): return lax.ppermute(value, axis, [(i, i ^ flip) for i in range(size)])  62 us
    pallas_call x1, Pallas kernels, mlp_block(): pl.pallas_call(mlp_kernel, grid=(rows // BM,), in_specs=[tile(D), pl.Bloc...  50.6 us
    pallas_call x1, Pallas kernels, attn_fwd(): pl.pallas_call(fwd_kernel, grid=(6,), in_specs=[pl.BlockSpec(memory_space...  44.8 us
    ppermute x24, starting transfers between devices, swap(): return lax.ppermute(value, axis, [(i, i ^ flip) for i in range(size)])  28.9 us
    pallas_call x2, Pallas kernels, split_grad(): pl.pallas_call(split_kernel, grid=(2,), in_specs=[pl.BlockSpec(memory_spa...  13.3 us
    pallas_call x1, Pallas kernels, input_grad(): pl.pallas_call(input_kernel, grid=(rows // BM,), in_specs=[tile(D), tile(...  12.9 us
    pallas_call x1, Pallas kernels, qkv_forward(): pl.pallas_call(qkv_kernel, grid=(rows // BM,), in_specs=[pl.BlockSpec(mem...  12.3 us
  transfers between devices with their start and end apart: 27, of which 13 were waited for; matrix products, arithmetic and copies ran while one was open for 1% of the time, Pallas kernels for 44%

profile of v5, /device:TPU:0, one launch (start us, length us, event | category | flops | bytes accessed | tf_op | source)
XLA Modules:
  0.0 367.0 jit_solution(5542200250934019681)
XLA Ops:
  9.3 3.1 collective-permute-start
  17.0 7.5 %collective-permute-done.1 = bf16[24,2432]{1,0:T(8,128)(2,1)S(1)} collective-permute-done((bf16[24,2432]{1,0:T(8,128)(2,1)}, bf16[24,2432]{1,0:T(8,128)(2,1)S(1)}, u32[]{:S(2)}, u32[]{:S(2)}) %collective-permute-start.1) | collective-permute-done | bytes 116768 | tf_op jit(solution)/shard_map/ppermute | solution.py:593
  29.0 10.1 %collective-permute-done.4.refs_1_ = bf16[4,24,2432]{2,1,0:T(8,128)(2,1)S(1)} collective-permute-done((bf16[4,24,2432]{2,1,0:T(8,128)(2,1)S(1)}, bf16[4,24,2432]{2,1,0:T(8,128)(2,1)S(1)}, u32[]{:S(2)}, u32[]{:S(2)}) %collective-permute-start.4) | collective-permute-done | bytes 466976 | tf_op jit(solution)/shard_map/ppermute | solution.py:593
  39.7 5.1 %norm_input.1 = (f32[1536,768]{1,0:T(8,128)}, f32[1536,128]{1,0:T(8,128)}) custom-call(bf16[1536,768]{1,0:T(8,128)(2,1)} %bitcast.32), custom_call_target="tpu_custom_call" | custom-call | flops 1000 | bytes 1000 | tf_op jit(solution)/shard_map/norm_input/pallas_call | solution.py:253
  44.8 8.9 %collective-permute-done.3.refs_3_ = bf16[4,24,2432]{2,1,0:T(8,128)(2,1)S(1)} collective-permute-done((bf16[4,24,2432]{2,1,0:T(8,128)(2,1)S(1)}, bf16[4,24,2432]{2,1,0:T(8,128)(2,1)S(1)}, u32[]{:S(2)}, u32[]{:S(2)}) %collective-permute-start.3) | collective-permute-done | bytes 466976 | tf_op jit(solution)/shard_map/ppermute | solution.py:593
  55.8 12.3 %qkv_forward.1 = (bf16[1536,1536]{1,0:T(8,128)(2,1)}, bf16[1536,2304]{1,0:T(8,128)(2,1)}, f32[16,768]{1,0:T(8,128)}, bf16[4,4,2,24,2432]{4,3,2,1,0:T(8,128)(2,1)}) custom-call(s32[3]{0:T(128)} %pad_add_fusion.place_ref, f32[1536,768]{1,0:T(8,128)} %get-tuple-element.108.n_ref, bf16[4,24,2432]{2,1,0:T(8,128)(2,1)} %copy-done.3, ...), custom_call_target="tpu_custom_call" | custom-call | flops 5435817984 | bytes 18874368 | tf_op jit(solution)/shard_map/qkv_forward/pallas_call | solution.py:317
  68.1 44.8 %attn_fwd.1 = (bf16[1536,1536]{1,0:T(8,128)(2,1)}, f32[6,8,1536]{2,1,0:T(8,128)}) custom-call(s32[1,6]{1,0:T(1,128)} %len_ref.3, bf16[1536,2304]{1,0:T(8,128)(2,1)} %get-tuple-element.116.qkv_ref, bf16[1536,1536]{1,0:T(8,128)(2,1)} %get-tuple-element.117.left_ref), custom_call_target="tpu_custom_call", output_to_operand_aliasing={{0}: (2, {})} | custom-call | flops 7247757312 | bytes 10485760 | tf_op jit(solution)/shard_map/attn_fwd/pallas_call | solution.py:143
  112.9 50.6 %mlp_block.1 = (bf16[1536,768]{1,0:T(8,128)(2,1)}, bf16[1536,768]{1,0:T(8,128)(2,1)}, bf16[1536,768]{1,0:T(8,128)(2,1)}, bf16[1536,3072]{1,0:T(8,128)(2,1)}, bf1...) custom-call(bf16[1536,768]{1,0:T(8,128)(2,1)} %bitcast.33, ...), custom_call_target="tpu_custom_call" | custom-call | flops 32614907904 | bytes 50331648 | tf_op jit(solution)/shard_map/mlp_block/pallas_call | solution.py:406
  163.5 11.7 %fc2_grad.1.old_ref = bf16[32,192,768]{2,1,0:T(8,128)(2,1)} custom-call(bf16[1536,3072]{1,0:T(8,128)(2,1)} %get-tuple-element.168.a_ref, bf16[1536,768]{1,0:T(8,128)(2,1)} %get-tuple-element.169.b_ref), custom_call_target="tpu_custom_call" | custom-call | flops 7247757312 | bytes 16777216 | tf_op jit(solution)/shard_map/fc2_grad/pallas_call | solution.py:422
  175.2 11.7 %fc1_grad.1 = bf16[32,192,768]{2,1,0:T(8,128)(2,1)} custom-call(bf16[1536,768]{1,0:T(8,128)(2,1)} %get-tuple-element.166.a_ref, bf16[1536,3072]{1,0:T(8,128)(2,1)} %get-tuple-element.167.b_ref, bf16[32,192,768]{2,1,0:T(8,128)(2,1)} %fc2_grad.1.old_ref), custom_call_target="tpu_custom_call", output_to_operand_aliasing={{}: (2, {})} | custom-call | flops 7247757312 | bytes 20971520 | tf_op jit(solution)/shard_map/fc1_grad/pallas_call | solution.py:437
  186.9 73.5 %attn_bwd.1.right_ref.d_ref = bf16[1536,3072]{1,0:T(8,128)(2,1)} custom-call(s32[1,6]{1,0:T(1,128)} %len_ref.3, bf16[1536,2304]{1,0:T(8,128)(2,1)} %get-tuple-element.116.qkv_ref, bf16[1536,1536]{1,0:T(8,128)(2,1)} %get-tuple-element.118.o_ref.left_ref, bf16[1536,768]{1,0:T(8,128)(2,1)} %get-tuple-element.123.do_ref, ...), custom_call_target="tpu_custom_call", output_to_operand_aliasing={{}: (5, {})} | custom-call | flops 18119393280 | bytes 20971520 | tf_op jit(solution)/shard_map/attn_bwd/pallas_call | solution.py:208
  260.5 6.6 %split_grad.2 = (bf16[16,24,1536]{2,1,0:T(8,128)(2,1)S(1)}, bf16[16,24,1536]{2,1,0:T(8,128)(2,1)S(1)}) custom-call(s32[1]{0:T(128)} %bitcast.3.core_ref, bf16[1536,1536]{1,0:T(8,128)(2,1)} %get-tuple-element.118.o_ref.left_ref, bf16[1536,3072]{1,0:T(8,128)(2,1)} %attn_bwd.1.right_ref.d_ref), custom_call_target="tpu_custom_call" | custom-call | flops 1000 | bytes 1000 | tf_op jit(solution)/shard_map/split_grad/pallas_call | solution.py:467
  267.2 2.7 collective-permute-done.10
  274.3 12.9 %input_grad.1 = (bf16[1536,768]{1,0:T(8,128)(2,1)}, f32[16,768]{1,0:T(8,128)}) custom-call(f32[1536,768]{1,0:T(8,128)} %get-tuple-element.108.n_ref, f32[1536,128]{1,0:T(8,128)} %get-tuple-element.122.r_ref, bf16[1536,3072]{1,0:T(8,128)(2,1)} %attn_bwd.1.right_ref.d_ref, f32[1536,768]{1,0:T(8,128)} %get-tuple-element.126.dx1_ref, ...), custom_call_target="tpu_custom_call" | custom-call | flops 1000 | bytes 1000 | tf_op jit(solution)/shard_map/input_grad/pallas_call | solution.py:496
  296.7 6.7 %split_grad.3 = (bf16[16,24,1664]{2,1,0:T(8,128)(2,1)S(1)}, bf16[16,24,1664]{2,1,0:T(8,128)(2,1)S(1)}) custom-call(s32[1]{0:T(128)} %bitcast.3.core_ref, bf16[1536,1536]{1,0:T(8,128)(2,1)} %get-tuple-element.118.o_ref.left_ref, bf16[1536,3072]{1,0:T(8,128)(2,1)} %attn_bwd.1.right_ref.d_ref, f32[16,768]{1,0:T(8,128)S(1)} %copy-done.2), custom_call_target="tpu_custom_call" | custom-call | flops 1000 | bytes 1000 | tf_op jit(solution)/shard_map/split_grad/pallas_call | solution.py:467
  303.4 2.8 collective-permute-done.16.refs_3_
  306.2 3.0 collective-permute-done.17
  313.0 7.5 %collective-permute-done.18.refs_1_ = bf16[4,24,1664]{2,1,0:T(8,128)(2,1)S(1)} collective-permute-done((bf16[4,24,1664]{2,1,0:T(8,128)(2,1)S(1)}, bf16[4,24,1664]{2,1,0:T(8,128)(2,1)S(1)}, u32[]{:S(2)}, u32[]{:S(2)}) %collective-permute-start.18) | collective-permute-done | bytes 319520 | tf_op jit(solution)/shard_map/ppermute | solution.py:593
  320.5 8.6 %collective-permute-done.19.refs_2_ = bf16[4,24,1664]{2,1,0:T(8,128)(2,1)S(1)} collective-permute-done((bf16[4,24,1664]{2,1,0:T(8,128)(2,1)S(1)}, bf16[4,24,1664]{2,1,0:T(8,128)(2,1)S(1)}, u32[]{:S(2)}, u32[]{:S(2)}) %collective-permute-start.19) | collective-permute-done | bytes 319520 | tf_op jit(solution)/shard_map/ppermute | solution.py:593
  329.9 3.0 collective-permute-start.21
  336.5 5.5 %collective-permute-done.22.refs_6_ = bf16[24,1664]{1,0:T(8,128)(2,1)S(1)} collective-permute-done((bf16[24,1664]{1,0:T(8,128)(2,1)S(1)}, bf16[24,1664]{1,0:T(8,128)(2,1)S(1)}, u32[]{:S(2)}, u32[]{:S(2)}) %collective-permute-start.22) | collective-permute-done | bytes 79904 | tf_op jit(solution)/shard_map/ppermute | solution.py:593
  345.0 3.6 all-to-all-start
  349.2 6.5 %all-to-all-done = f32[32,1,128]{2,1,0:T(1,128)S(1)} async-done(((f32[32,1,128]{2,1,0:T(1,128)}), f32[32,1,128]{2,1,0:T(1,128)S(1)}, u32[]{:S(2)}, u32[]{:S(2)}) %all-to-all-start) | async-done | bytes 16416 | tf_op jit(solution)/shard_map/all_to_all | solution.py:714
  356.3 3.9 %adam_all.1 = (f32[1,1]{1,0:T(1,128)}, f32[24,2304]{1,0:T(8,128)}, f32[24,2304]{1,0:T(8,128)}, f32[24,2304]{1,0:T(8,128)}, f32[24,768]{1,0:T(8,128)}, /*index=5*...) custom-call(f32[2]{0:T(128)} %pad_maximum_fusion.1.fix_ref, ...), custom_call_target="tpu_custom_call" | custom-call | tf_op jit(solution)/shard_map/adam_all/pallas_call | solution.py:575
  (80 shorter events, 39.3 us)
Async XLA Ops:
  7.2 105.7 %all-gather.3.cloned.1.call-start = ((), (), s32[]{:S(2)}) async-start(), calls=%async_computation.3 | async-start | bytes 10948608 | tf_op jit(solution)/shard_map/all_gather | solution.py:661
  9.3 332.8 %reduce-scatter.2.cloned.1.call-start = ((), (), s32[]{:S(2)}) async-start(), calls=%async_computation.2 | async-start | bytes 9732096 | tf_op jit(solution)/shard_map/reduce_scatter | solution.py:689
  9.3 7.7 %collective-permute-start = (bf16[24,2432]{1,0:T(8,128)(2,1)}, bf16[24,2432]{1,0:T(8,128)(2,1)S(1)}, u32[]{:S(2)}, u32[]{:S(2)}) collective-permute-start(bf16[24,2432]{1,0:T(8,128)(2,1)} %get-tuple-element.105), channel_id=1, source_target_pairs={{0,2},{1,3},{2,0},{3,1},{4,6},{5,7},{6,4},{7,5},{8,10},{9,11},{10,... | collective-permute-start | bytes 350216 | tf_op jit(solution)/shard_map/ppermute | solution.py:593
  12.4 12.1 %collective-permute-start.1 = (bf16[24,2432]{1,0:T(8,128)(2,1)}, bf16[24,2432]{1,0:T(8,128)(2,1)S(1)}, u32[]{:S(2)}, u32[]{:S(2)}) collective-permute-start(bf16[24,2432]{1,0:T(8,128)(2,1)} %get-tuple-element.105), channel_id=1, source_target_pairs={{0,4},{1,5},{2,6},{3,7},{4,0},{5,1},{6,2},{7,3},{8,12},{9,13},{10,... | collective-permute-start | bytes 350216 | tf_op jit(solution)/shard_map/ppermute | solution.py:593
  15.0 9.5 %collective-permute-start.2 = (bf16[24,2432]{1,0:T(8,128)(2,1)}, bf16[24,2432]{1,0:T(8,128)(2,1)S(1)}, u32[]{:S(2)}, u32[]{:S(2)}) collective-permute-start(bf16[24,2432]{1,0:T(8,128)(2,1)} %get-tuple-element.105), channel_id=1, source_target_pairs={{0,6},{1,7},{2,4},{3,5},{4,2},{5,3},{6,0},{7,1},{8,14},{9,15},{10,... | collective-permute-start | bytes 350216 | tf_op jit(solution)/shard_map/ppermute | solution.py:593
  25.5 13.7 %collective-permute-start.4 = (bf16[4,24,2432]{2,1,0:T(8,128)(2,1)S(1)}, bf16[4,24,2432]{2,1,0:T(8,128)(2,1)S(1)}, u32[]{:S(2)}, u32[]{:S(2)}) collective-permute-start(bf16[4,24,2432]{2,1,0:T(8,128)(2,1)S(1)} %pad_maximum_fusion.refs_0_), channel_id=1, source_target_pairs={{0,8},{8,0},{16,24},{24,16},{1,9},{9,1},{17,25},{25,17},{2,10},{10... | collective-permute-start | bytes 1400840 | tf_op jit(solution)/shard_map/ppermute | solution.py:593
  27.0 12.1 %collective-permute-start.5 = (bf16[4,24,2432]{2,1,0:T(8,128)(2,1)S(1)}, bf16[4,24,2432]{2,1,0:T(8,128)(2,1)S(1)}, u32[]{:S(2)}, u32[]{:S(2)}) collective-permute-start(bf16[4,24,2432]{2,1,0:T(8,128)(2,1)S(1)} %pad_maximum_fusion.refs_0_), channel_id=1, source_target_pairs={{0,16},{8,24},{16,0},{24,8},{1,17},{9,25},{17,1},{25,9},{2,18},{10... | collective-permute-start | bytes 1400840 | tf_op jit(solution)/shard_map/ppermute | solution.py:593
  28.6 25.1 %collective-permute-start.3 = (bf16[4,24,2432]{2,1,0:T(8,128)(2,1)S(1)}, bf16[4,24,2432]{2,1,0:T(8,128)(2,1)S(1)}, u32[]{:S(2)}, u32[]{:S(2)}) collective-permute-start(bf16[4,24,2432]{2,1,0:T(8,128)(2,1)S(1)} %pad_maximum_fusion.refs_0_), channel_id=1, source_target_pairs={{0,24},{8,16},{16,8},{24,0},{1,25},{9,17},{17,9},{25,1},{2,26},{10... | collective-permute-start | bytes 1400840 | tf_op jit(solution)/shard_map/ppermute | solution.py:593
  29.0 24.7 %collective-permute-start.6 = (bf16[4,24,2432]{2,1,0:T(8,128)(2,1)S(1)}, bf16[4,24,2432]{2,1,0:T(8,128)(2,1)}, u32[]{:S(2)}, u32[]{:S(2)}) collective-permute-start(bf16[4,24,2432]{2,1,0:T(8,128)(2,1)S(1)} %pad_maximum_fusion.refs_0_), channel_id=1, source_target_pairs={{0,1},{1,0},{2,3},{3,2},{4,5},{5,4},{6,7},{7,6},{8,9},{9,8},{10,11... | collective-permute-start | bytes 1400840 | tf_op jit(solution)/shard_map/ppermute | solution.py:593
  39.2 14.5 %collective-permute-start.7 = (bf16[4,24,2432]{2,1,0:T(8,128)(2,1)S(1)}, bf16[4,24,2432]{2,1,0:T(8,128)(2,1)}, u32[]{:S(2)}, u32[]{:S(2)}) collective-permute-start(bf16[4,24,2432]{2,1,0:T(8,128)(2,1)S(1)} %collective-permute-done.4.refs_1_), channel_id=1, source_target_pairs={{0,1},{1,0},{2,3},{3,2},{4,5},{5,4},{6,7},{7,6},{8,9},{9,8},{10,11... | collective-permute-start | bytes 1400840 | tf_op jit(solution)/shard_map/ppermute | solution.py:593
  39.2 14.5 %collective-permute-start.8 = (bf16[4,24,2432]{2,1,0:T(8,128)(2,1)S(1)}, bf16[4,24,2432]{2,1,0:T(8,128)(2,1)}, u32[]{:S(2)}, u32[]{:S(2)}) collective-permute-start(bf16[4,24,2432]{2,1,0:T(8,128)(2,1)S(1)} %collective-permute-done.5.refs_2_), channel_id=1, source_target_pairs={{0,1},{1,0},{2,3},{3,2},{4,5},{5,4},{6,7},{7,6},{8,9},{9,8},{10,11... | collective-permute-start | bytes 1400840 | tf_op jit(solution)/shard_map/ppermute | solution.py:593
  270.8 16.4 %collective-permute-start.11 = (bf16[4,24,1536]{2,1,0:T(8,128)(2,1)}, bf16[4,24,1536]{2,1,0:T(8,128)(2,1)S(1)}, u32[]{:S(2)}, u32[]{:S(2)}) collective-permute-start(bf16[4,24,1536]{2,1,0:T(8,128)(2,1)} %get-tuple-element.138), channel_id=1, source_target_pairs={{0,8},{8,0},{16,24},{24,16},{1,9},{9,1},{17,25},{25,17},{2,10},{10... | collective-permute-start | bytes 884744 | tf_op jit(solution)/shard_map/ppermute | solution.py:593
  272.2 14.9 %collective-permute-start.12 = (bf16[4,24,1536]{2,1,0:T(8,128)(2,1)S(1)}, bf16[4,24,1536]{2,1,0:T(8,128)(2,1)S(1)}, u32[]{:S(2)}, u32[]{:S(2)}) collective-permute-start(bf16[4,24,1536]{2,1,0:T(8,128)(2,1)S(1)} %get-tuple-element.139), channel_id=1, source_target_pairs={{0,16},{8,24},{16,0},{24,8},{1,17},{9,25},{17,1},{25,9},{2,18},{10... | collective-permute-start | bytes 884744 | tf_op jit(solution)/shard_map/ppermute | solution.py:593
  272.7 16.3 %collective-permute-start.13 = (bf16[4,24,1536]{2,1,0:T(8,128)(2,1)S(1)}, bf16[4,24,1536]{2,1,0:T(8,128)(2,1)S(1)}, u32[]{:S(2)}, u32[]{:S(2)}) collective-permute-start(bf16[4,24,1536]{2,1,0:T(8,128)(2,1)S(1)} %get-tuple-element.140), channel_id=1, source_target_pairs={{0,24},{8,16},{16,8},{24,0},{1,25},{9,17},{17,9},{25,1},{2,26},{10... | collective-permute-start | bytes 884744 | tf_op jit(solution)/shard_map/ppermute | solution.py:593
  289.8 13.5 %collective-permute-start.14 = (bf16[24,1536]{1,0:T(8,128)(2,1)S(1)}, bf16[24,1536]{1,0:T(8,128)(2,1)S(1)}, u32[]{:S(2)}, u32[]{:S(2)}) collective-permute-start(bf16[24,1536]{1,0:T(8,128)(2,1)S(1)} %get-tuple-element.147), channel_id=1, source_target_pairs={{0,2},{1,3},{2,0},{3,1},{4,6},{5,7},{6,4},{7,5},{8,10},{9,11},{10,... | collective-permute-start | bytes 221192 | tf_op jit(solution)/shard_map/ppermute | solution.py:593
  291.8 11.5 %collective-permute-start.15 = (bf16[24,1536]{1,0:T(8,128)(2,1)S(1)}, bf16[24,1536]{1,0:T(8,128)(2,1)S(1)}, u32[]{:S(2)}, u32[]{:S(2)}) collective-permute-start(bf16[24,1536]{1,0:T(8,128)(2,1)S(1)} %get-tuple-element.148), channel_id=1, source_target_pairs={{0,4},{1,5},{2,6},{3,7},{4,0},{5,1},{6,2},{7,3},{8,12},{9,13},{10,... | collective-permute-start | bytes 221192 | tf_op jit(solution)/shard_map/ppermute | solution.py:593
  294.4 11.8 %collective-permute-start.16 = (bf16[24,1536]{1,0:T(8,128)(2,1)S(1)}, bf16[24,1536]{1,0:T(8,128)(2,1)S(1)}, u32[]{:S(2)}, u32[]{:S(2)}) collective-permute-start(bf16[24,1536]{1,0:T(8,128)(2,1)S(1)} %get-tuple-element.149), channel_id=1, source_target_pairs={{0,6},{1,7},{2,4},{3,5},{4,2},{5,3},{6,0},{7,1},{8,14},{9,15},{10,... | collective-permute-start | bytes 221192 | tf_op jit(solution)/shard_map/ppermute | solution.py:593
  309.5 11.0 %collective-permute-start.18 = (bf16[4,24,1664]{2,1,0:T(8,128)(2,1)S(1)}, bf16[4,24,1664]{2,1,0:T(8,128)(2,1)S(1)}, u32[]{:S(2)}, u32[]{:S(2)}) collective-permute-start(bf16[4,24,1664]{2,1,0:T(8,128)(2,1)S(1)} %get-tuple-element.159), channel_id=1, source_target_pairs={{0,8},{8,0},{16,24},{24,16},{1,9},{9,1},{17,25},{25,17},{2,10},{10... | collective-permute-start | bytes 958472 | tf_op jit(solution)/shard_map/ppermute | solution.py:593
  310.9 18.2 %collective-permute-start.19 = (bf16[4,24,1664]{2,1,0:T(8,128)(2,1)S(1)}, bf16[4,24,1664]{2,1,0:T(8,128)(2,1)S(1)}, u32[]{:S(2)}, u32[]{:S(2)}) collective-permute-start(bf16[4,24,1664]{2,1,0:T(8,128)(2,1)S(1)} %get-tuple-element.160), channel_id=1, source_target_pairs={{0,16},{8,24},{16,0},{24,8},{1,17},{9,25},{17,1},{25,9},{2,18},{10... | collective-permute-start | bytes 958472 | tf_op jit(solution)/shard_map/ppermute | solution.py:593
  311.6 17.6 %collective-permute-start.20 = (bf16[4,24,1664]{2,1,0:T(8,128)(2,1)S(1)}, bf16[4,24,1664]{2,1,0:T(8,128)(2,1)S(1)}, u32[]{:S(2)}, u32[]{:S(2)}) collective-permute-start(bf16[4,24,1664]{2,1,0:T(8,128)(2,1)S(1)} %get-tuple-element.161), channel_id=1, source_target_pairs={{0,24},{8,16},{16,8},{24,0},{1,25},{9,17},{17,9},{25,1},{2,26},{10... | collective-permute-start | bytes 958472 | tf_op jit(solution)/shard_map/ppermute | solution.py:593
  329.9 6.6 %collective-permute-start.21 = (bf16[24,1664]{1,0:T(8,128)(2,1)S(1)}, bf16[24,1664]{1,0:T(8,128)(2,1)S(1)}, u32[]{:S(2)}, u32[]{:S(2)}) collective-permute-start(bf16[24,1664]{1,0:T(8,128)(2,1)S(1)} %get-tuple-element.163), channel_id=1, source_target_pairs={{0,2},{1,3},{2,0},{3,1},{4,6},{5,7},{6,4},{7,5},{8,10},{9,11},{10,... | collective-permute-start | bytes 239624 | tf_op jit(solution)/shard_map/ppermute | solution.py:593
  333.0 9.1 %collective-permute-start.22 = (bf16[24,1664]{1,0:T(8,128)(2,1)S(1)}, bf16[24,1664]{1,0:T(8,128)(2,1)S(1)}, u32[]{:S(2)}, u32[]{:S(2)}) collective-permute-start(bf16[24,1664]{1,0:T(8,128)(2,1)S(1)} %get-tuple-element.164), channel_id=1, source_target_pairs={{0,4},{1,5},{2,6},{3,7},{4,0},{5,1},{6,2},{7,3},{8,12},{9,13},{10,... | collective-permute-start | bytes 239624 | tf_op jit(solution)/shard_map/ppermute | solution.py:593
  334.3 7.8 %collective-permute-start.23 = (bf16[24,1664]{1,0:T(8,128)(2,1)S(1)}, bf16[24,1664]{1,0:T(8,128)(2,1)S(1)}, u32[]{:S(2)}, u32[]{:S(2)}) collective-permute-start(bf16[24,1664]{1,0:T(8,128)(2,1)S(1)} %get-tuple-element.165), channel_id=1, source_target_pairs={{0,6},{1,7},{2,4},{3,5},{4,2},{5,3},{6,0},{7,1},{8,14},{9,15},{10,... | collective-permute-start | bytes 239624 | tf_op jit(solution)/shard_map/ppermute | solution.py:593
  345.0 10.6 %all-to-all-start = ((f32[32,1,128]{2,1,0:T(1,128)}), f32[32,1,128]{2,1,0:T(1,128)S(1)}, u32[]{:S(2)}, u32[]{:S(2)}) async-start(f32[32,1,128]{2,1,0:T(1,128)} %bitcast.42), calls=%async_computation.1 | async-start | bytes 32768 | tf_op jit(solution)/shard_map/all_to_all | solution.py:714
  (17 other events, 196.3 us)
Sparse Core Ops, SparseCore 0:
  11.0 95.4 all-gather.2
  187.0 150.8 reduce-scatter.1

commit v6 on v5

--- a/solution.py
+++ b/solution.py
@@ -412,34 +412,40 @@
         cost_estimate=pl.CostEstimate(flops=2*rows*D*(2*D+4*FF),bytes_accessed=48<<20,transcendentals=0))(x,o,dy,vec,packed,packed)
 
 
-def outer_kernel(a_ref,b_ref,g_ref):
-    g_ref[...]=tn(a_ref[...],b_ref[...]).reshape(g_ref.shape).astype(bf)
-
-
-def fc2_grad(z,dm,n,extra):
+def fc_kernel(z_ref,dm_ref,h_ref,du_ref,g_ref,down,up,sems):
+    i=pl.program_id(0)
+    per,r=down.shape[2],up.shape[2]
+    n=down.shape[1]
+    def down_copy(k):
+        return pltpu.make_async_copy(down.at[k],g_ref.at[pl.ds(pl.multiple_of(k*n,n),n),0:per],sems.at[k])
+    def up_copy(k):
+        return pltpu.make_async_copy(up.at[k],g_ref.at[:,pl.ds(pl.multiple_of(per+k*r,r),r)],sems.at[4+k])
+    @pl.when(i<4)
+    def _():
+        down[i]=tn(z_ref[...],dm_ref[...]).reshape(down.shape[1:]).astype(bf)
+        down_copy(i).start()
+    @pl.when(i>=4)
+    def _():
+        up[i-4]=tn(h_ref[...],du_ref[...]).reshape(up.shape[1:]).astype(bf)
+        up_copy(i-4).start()
+    @pl.when(i==7)
+    def _():
+        for k in range(4):
+            down_copy(k).wait()
+            up_copy(k).wait()
+
+
+def fc_grads(z,dm,h,du):
     rows=z.shape[0]
-    per=FF//n
-    return pl.pallas_call(outer_kernel,grid=(FF//D,),
-        in_specs=[pl.BlockSpec((rows,D),lambda i:(0,i)),once((rows,D))],
-        out_specs=pl.BlockSpec((n*D//FF,per,D),lambda i:(i,0,0)),
-        out_shape=jax.ShapeDtypeStruct((n,per+extra,D),bf),
-        compiler_params=params(),name="fc2_grad",
-        cost_estimate=pl.CostEstimate(flops=2*rows*D*FF,bytes_accessed=16<<20,transcendentals=0))(z,dm)
-
-
-def fc1_kernel(a_ref,b_ref,old_ref,g_ref):
-    outer_kernel(a_ref,b_ref,g_ref)
-
-
-def fc1_grad(h,du,packed):
-    rows=h.shape[0]
-    n=packed.shape[0]; r=D//n
-    return pl.pallas_call(fc1_kernel,grid=(FF//D,),
-        in_specs=[once((rows,D)),pl.BlockSpec((rows,D),lambda i:(0,i)),pl.BlockSpec(memory_space=pl.ANY)],
-        out_specs=pl.BlockSpec((n,r,D),lambda i:(0,FF//D+i,0)),
-        out_shape=jax.ShapeDtypeStruct(packed.shape,bf),input_output_aliases={2:0},
-        compiler_params=params(),name="fc1_grad",
-        cost_estimate=pl.CostEstimate(flops=2*rows*D*FF,bytes_accessed=20<<20,transcendentals=0))(h,du,packed)
+    per,r=FF//PACK,D//PACK
+    return pl.pallas_call(fc_kernel,grid=(8,),
+        in_specs=[pl.BlockSpec((rows,D),lambda i:(0,jnp.minimum(i,3))),once((rows,D)),once((rows,D)),
+            pl.BlockSpec((rows,D),lambda i:(0,jnp.maximum(i-4,0)))],
+        out_specs=pl.BlockSpec(memory_space=pl.ANY),
+        out_shape=jax.ShapeDtypeStruct((PACK,2*per,D),bf),
+        scratch_shapes=[pltpu.VMEM((4,PACK//4,per,D),bf),pltpu.VMEM((4,PACK,r,D),bf),pltpu.SemaphoreType.DMA((8,))],
+        compiler_params=params(),name="fc_grads",
+        cost_estimate=pl.CostEstimate(flops=4*rows*D*FF,bytes_accessed=36<<20,transcendentals=0))(z,dm,h,du)
 
 
 def split_kernel(core_ref,left_ref,right_ref,*refs):
@@ -683,8 +689,7 @@
         result, normed_two, grad_down, active, grad_inner, grad_middle, right, grad_mixed, sums = mlp_block(
             inputs, left, cotangent.reshape(count, D), vec, rest
         )
-        grads = fc2_grad(active, grad_down, PACK, FF // PACK)
-        grads = fc1_grad(normed_two, grad_inner, grads)
+        grads = fc_grads(active, grad_down, normed_two, grad_inner)
         if fast:
             rest_owned = lax.psum_scatter(grads, AXES, scatter_dimension=0, tiled=False)
         right = jnp.concatenate(

time: 368 us -> 366 us (level)
    pallas_call x2 -> x1, Pallas kernels: 23.4 us -> 21.5 us  [fc_grads(): pl.pallas_call(fc_kernel, grid=(8,), in_specs=[pl.BlockSpec((rows, D), la...]
  transfers between devices with their start and end apart: 27 -> 27, of which waited for: 13 -> 13; matrix products, arithmetic and copies ran while one was open for 1% -> 1% of each run, Pallas kernels for 44% -> 45%
where the time goes in v6:
time: 366 us; the launch traced here: 365 us
  Pallas kernels  244 us (67%)
  waiting for transfers between devices  68.5 us (19%)
  starting transfers between devices  32.5 us (9%)
  between operations  15.1 us (4%)
    pallas_call x1, Pallas kernels, attn_bwd(): pl.pallas_call(bwd_kernel, grid=(6,), in_specs=[pl.BlockSpec(memory_space...  73.5 us
    ppermute x24, waiting for transfers between devices, swap(): return lax.ppermute(value, axis, [(i, i ^ flip) for i in range(size)])  62 us
    pallas_call x1, Pallas kernels, mlp_block(): pl.pallas_call(mlp_kernel, grid=(rows // BM,), in_specs=[tile(D), pl.Bloc...  50.6 us
    pallas_call x1, Pallas kernels, attn_fwd(): pl.pallas_call(fwd_kernel, grid=(6,), in_specs=[pl.BlockSpec(memory_space...  44.8 us
    ppermute x24, starting transfers between devices, swap(): return lax.ppermute(value, axis, [(i, i ^ flip) for i in range(size)])  28.9 us
    pallas_call x1, Pallas kernels, fc_grads(): pl.pallas_call(fc_kernel, grid=(8,), in_specs=[pl.BlockSpec((rows, D), la...  21.5 us
    pallas_call x2, Pallas kernels, split_grad(): pl.pallas_call(split_kernel, grid=(2,), in_specs=[pl.BlockSpec(memory_spa...  13.3 us
    pallas_call x1, Pallas kernels, input_grad(): pl.pallas_call(input_kernel, grid=(rows // BM,), in_specs=[tile(D), tile(...  12.9 us
  transfers between devices with their start and end apart: 27, of which 13 were waited for; matrix products, arithmetic and copies ran while one was open for 1% of the time, Pallas kernels for 45%

profile of v6, /device:TPU:0, one launch (start us, length us, event | category | flops | bytes accessed | tf_op | source)
XLA Modules:
  0.0 365.2 jit_solution(10337002383559198163)
XLA Ops:
  9.3 3.1 collective-permute-start
  12.4 2.6 collective-permute-start.1
  17.0 7.5 %collective-permute-done.1 = bf16[24,2432]{1,0:T(8,128)(2,1)S(1)} collective-permute-done((bf16[24,2432]{1,0:T(8,128)(2,1)}, bf16[24,2432]{1,0:T(8,128)(2,1)S(1)}, u32[]{:S(2)}, u32[]{:S(2)}) %collective-permute-start.1) | collective-permute-done | bytes 116768 | tf_op jit(solution)/shard_map/ppermute | solution.py:599
  29.0 10.1 %collective-permute-done.4.refs_1_ = bf16[4,24,2432]{2,1,0:T(8,128)(2,1)S(1)} collective-permute-done((bf16[4,24,2432]{2,1,0:T(8,128)(2,1)S(1)}, bf16[4,24,2432]{2,1,0:T(8,128)(2,1)S(1)}, u32[]{:S(2)}, u32[]{:S(2)}) %collective-permute-start.4) | collective-permute-done | bytes 466976 | tf_op jit(solution)/shard_map/ppermute | solution.py:599
  39.7 5.1 %norm_input.1 = (f32[1536,768]{1,0:T(8,128)}, f32[1536,128]{1,0:T(8,128)}) custom-call(bf16[1536,768]{1,0:T(8,128)(2,1)} %bitcast.32), custom_call_target="tpu_custom_call" | custom-call | flops 1000 | bytes 1000 | tf_op jit(solution)/shard_map/norm_input/pallas_call | solution.py:253
  44.8 8.9 %collective-permute-done.3.refs_3_ = bf16[4,24,2432]{2,1,0:T(8,128)(2,1)S(1)} collective-permute-done((bf16[4,24,2432]{2,1,0:T(8,128)(2,1)S(1)}, bf16[4,24,2432]{2,1,0:T(8,128)(2,1)S(1)}, u32[]{:S(2)}, u32[]{:S(2)}) %collective-permute-start.3) | collective-permute-done | bytes 466976 | tf_op jit(solution)/shard_map/ppermute | solution.py:599
  55.8 12.3 %qkv_forward.1 = (bf16[1536,1536]{1,0:T(8,128)(2,1)}, bf16[1536,2304]{1,0:T(8,128)(2,1)}, f32[16,768]{1,0:T(8,128)}, bf16[4,4,2,24,2432]{4,3,2,1,0:T(8,128)(2,1)}) custom-call(s32[3]{0:T(128)} %pad_add_fusion.place_ref, f32[1536,768]{1,0:T(8,128)} %get-tuple-element.108.n_ref, bf16[4,24,2432]{2,1,0:T(8,128)(2,1)} %copy-done.3, ...), custom_call_target="tpu_custom_call" | custom-call | flops 5435817984 | bytes 18874368 | tf_op jit(solution)/shard_map/qkv_forward/pallas_call | solution.py:317
  68.1 44.8 %attn_fwd.1 = (bf16[1536,1536]{1,0:T(8,128)(2,1)}, f32[6,8,1536]{2,1,0:T(8,128)}) custom-call(s32[1,6]{1,0:T(1,128)} %len_ref.3, bf16[1536,2304]{1,0:T(8,128)(2,1)} %get-tuple-element.116.qkv_ref, bf16[1536,1536]{1,0:T(8,128)(2,1)} %get-tuple-element.117.left_ref), custom_call_target="tpu_custom_call", output_to_operand_aliasing={{0}: (2, {})} | custom-call | flops 7247757312 | bytes 10485760 | tf_op jit(solution)/shard_map/attn_fwd/pallas_call | solution.py:143
  112.9 50.6 %mlp_block.1 = (bf16[1536,768]{1,0:T(8,128)(2,1)}, bf16[1536,768]{1,0:T(8,128)(2,1)}, bf16[1536,768]{1,0:T(8,128)(2,1)}, bf16[1536,3072]{1,0:T(8,128)(2,1)}, bf1...) custom-call(bf16[1536,768]{1,0:T(8,128)(2,1)} %bitcast.33, ...), custom_call_target="tpu_custom_call" | custom-call | flops 32614907904 | bytes 50331648 | tf_op jit(solution)/shard_map/mlp_block/pallas_call | solution.py:406
  163.5 21.5 %fc_grads.1 = bf16[32,192,768]{2,1,0:T(8,128)(2,1)} custom-call(bf16[1536,3072]{1,0:T(8,128)(2,1)} %get-tuple-element.166.z_ref, bf16[1536,768]{1,0:T(8,128)(2,1)} %get-tuple-element.167.dm_ref, bf16[1536,768]{1,0:T(8,128)(2,1)} %get-tuple-element.168.h_ref, bf16[1536,3072]{1,0:T(8,128)(2,1)} %get-tuple-element.169.du_ref), custom_call_target="tpu_custom_call" | custom-call | flops 14495514624 | bytes 37748736 | tf_op jit(solution)/shard_map/fc_grads/pallas_call | solution.py:441
  185.1 73.5 %attn_bwd.1.right_ref.d_ref = bf16[1536,3072]{1,0:T(8,128)(2,1)} custom-call(s32[1,6]{1,0:T(1,128)} %len_ref.3, bf16[1536,2304]{1,0:T(8,128)(2,1)} %get-tuple-element.116.qkv_ref, bf16[1536,1536]{1,0:T(8,128)(2,1)} %get-tuple-element.118.o_ref.left_ref, bf16[1536,768]{1,0:T(8,128)(2,1)} %get-tuple-element.123.do_ref, ...), custom_call_target="tpu_custom_call", output_to_operand_aliasing={{}: (5, {})} | custom-call | flops 18119393280 | bytes 20971520 | tf_op jit(solution)/shard_map/attn_bwd/pallas_call | solution.py:208
  258.6 6.6 %split_grad.2 = (bf16[16,24,1536]{2,1,0:T(8,128)(2,1)S(1)}, bf16[16,24,1536]{2,1,0:T(8,128)(2,1)S(1)}) custom-call(s32[1]{0:T(128)} %bitcast.3.core_ref, bf16[1536,1536]{1,0:T(8,128)(2,1)} %get-tuple-element.118.o_ref.left_ref, bf16[1536,3072]{1,0:T(8,128)(2,1)} %attn_bwd.1.right_ref.d_ref), custom_call_target="tpu_custom_call" | custom-call | flops 1000 | bytes 1000 | tf_op jit(solution)/shard_map/split_grad/pallas_call | solution.py:473
  265.4 2.7 collective-permute-done.10
  272.4 12.9 %input_grad.1 = (bf16[1536,768]{1,0:T(8,128)(2,1)}, f32[16,768]{1,0:T(8,128)}) custom-call(f32[1536,768]{1,0:T(8,128)} %get-tuple-element.108.n_ref, f32[1536,128]{1,0:T(8,128)} %get-tuple-element.122.r_ref, bf16[1536,3072]{1,0:T(8,128)(2,1)} %attn_bwd.1.right_ref.d_ref, f32[1536,768]{1,0:T(8,128)} %get-tuple-element.126.dx1_ref, ...), custom_call_target="tpu_custom_call" | custom-call | flops 1000 | bytes 1000 | tf_op jit(solution)/shard_map/input_grad/pallas_call | solution.py:502
  294.8 6.7 %split_grad.3 = (bf16[16,24,1664]{2,1,0:T(8,128)(2,1)S(1)}, bf16[16,24,1664]{2,1,0:T(8,128)(2,1)S(1)}) custom-call(s32[1]{0:T(128)} %bitcast.3.core_ref, bf16[1536,1536]{1,0:T(8,128)(2,1)} %get-tuple-element.118.o_ref.left_ref, bf16[1536,3072]{1,0:T(8,128)(2,1)} %attn_bwd.1.right_ref.d_ref, f32[16,768]{1,0:T(8,128)S(1)} %copy-done.2), custom_call_target="tpu_custom_call" | custom-call | flops 1000 | bytes 1000 | tf_op jit(solution)/shard_map/split_grad/pallas_call | solution.py:473
  301.6 2.8 collective-permute-done.16.refs_3_
  304.3 3.0 collective-permute-done.17
  311.2 7.5 %collective-permute-done.18.refs_1_ = bf16[4,24,1664]{2,1,0:T(8,128)(2,1)S(1)} collective-permute-done((bf16[4,24,1664]{2,1,0:T(8,128)(2,1)S(1)}, bf16[4,24,1664]{2,1,0:T(8,128)(2,1)S(1)}, u32[]{:S(2)}, u32[]{:S(2)}) %collective-permute-start.18) | collective-permute-done | bytes 319520 | tf_op jit(solution)/shard_map/ppermute | solution.py:599
  318.7 8.6 %collective-permute-done.19.refs_2_ = bf16[4,24,1664]{2,1,0:T(8,128)(2,1)S(1)} collective-permute-done((bf16[4,24,1664]{2,1,0:T(8,128)(2,1)S(1)}, bf16[4,24,1664]{2,1,0:T(8,128)(2,1)S(1)}, u32[]{:S(2)}, u32[]{:S(2)}) %collective-permute-start.19) | collective-permute-done | bytes 319520 | tf_op jit(solution)/shard_map/ppermute | solution.py:599
  328.1 3.1 collective-permute-start.21
  334.7 5.5 %collective-permute-done.22.refs_6_ = bf16[24,1664]{1,0:T(8,128)(2,1)S(1)} collective-permute-done((bf16[24,1664]{1,0:T(8,128)(2,1)S(1)}, bf16[24,1664]{1,0:T(8,128)(2,1)S(1)}, u32[]{:S(2)}, u32[]{:S(2)}) %collective-permute-start.22) | collective-permute-done | bytes 79904 | tf_op jit(solution)/shard_map/ppermute | solution.py:599
  343.2 3.6 all-to-all-start
  347.3 6.5 %all-to-all-done = f32[32,1,128]{2,1,0:T(1,128)S(1)} async-done(((f32[32,1,128]{2,1,0:T(1,128)}), f32[32,1,128]{2,1,0:T(1,128)S(1)}, u32[]{:S(2)}, u32[]{:S(2)}) %all-to-all-start) | async-done | bytes 16416 | tf_op jit(solution)/shard_map/all_to_all | solution.py:719
  354.4 3.9 %adam_all.1 = (f32[1,1]{1,0:T(1,128)}, f32[24,2304]{1,0:T(8,128)}, f32[24,2304]{1,0:T(8,128)}, f32[24,2304]{1,0:T(8,128)}, f32[24,768]{1,0:T(8,128)}, /*index=5*...) custom-call(f32[2]{0:T(128)} %pad_maximum_fusion.1.fix_ref, ...), custom_call_target="tpu_custom_call" | custom-call | tf_op jit(solution)/shard_map/adam_all/pallas_call | solution.py:581
  (79 shorter events, 36.7 us)
Async XLA Ops:
  7.2 105.7 %all-gather.3.cloned.1.call-start = ((), (), s32[]{:S(2)}) async-start(), calls=%async_computation.3 | async-start | bytes 10948608 | tf_op jit(solution)/shard_map/all_gather | solution.py:667
  9.3 331.0 %reduce-scatter.2.cloned.1.call-start = ((), (), s32[]{:S(2)}) async-start(), calls=%async_computation.2 | async-start | bytes 9732096 | tf_op jit(solution)/shard_map/reduce_scatter | solution.py:694
  9.3 7.7 %collective-permute-start = (bf16[24,2432]{1,0:T(8,128)(2,1)}, bf16[24,2432]{1,0:T(8,128)(2,1)S(1)}, u32[]{:S(2)}, u32[]{:S(2)}) collective-permute-start(bf16[24,2432]{1,0:T(8,128)(2,1)} %get-tuple-element.105), channel_id=1, source_target_pairs={{0,2},{1,3},{2,0},{3,1},{4,6},{5,7},{6,4},{7,5},{8,10},{9,11},{10,... | collective-permute-start | bytes 350216 | tf_op jit(solution)/shard_map/ppermute | solution.py:599
  12.4 12.1 %collective-permute-start.1 = (bf16[24,2432]{1,0:T(8,128)(2,1)}, bf16[24,2432]{1,0:T(8,128)(2,1)S(1)}, u32[]{:S(2)}, u32[]{:S(2)}) collective-permute-start(bf16[24,2432]{1,0:T(8,128)(2,1)} %get-tuple-element.105), channel_id=1, source_target_pairs={{0,4},{1,5},{2,6},{3,7},{4,0},{5,1},{6,2},{7,3},{8,12},{9,13},{10,... | collective-permute-start | bytes 350216 | tf_op jit(solution)/shard_map/ppermute | solution.py:599
  15.0 9.5 %collective-permute-start.2 = (bf16[24,2432]{1,0:T(8,128)(2,1)}, bf16[24,2432]{1,0:T(8,128)(2,1)S(1)}, u32[]{:S(2)}, u32[]{:S(2)}) collective-permute-start(bf16[24,2432]{1,0:T(8,128)(2,1)} %get-tuple-element.105), channel_id=1, source_target_pairs={{0,6},{1,7},{2,4},{3,5},{4,2},{5,3},{6,0},{7,1},{8,14},{9,15},{10,... | collective-permute-start | bytes 350216 | tf_op jit(solution)/shard_map/ppermute | solution.py:599
  25.5 13.7 %collective-permute-start.4 = (bf16[4,24,2432]{2,1,0:T(8,128)(2,1)S(1)}, bf16[4,24,2432]{2,1,0:T(8,128)(2,1)S(1)}, u32[]{:S(2)}, u32[]{:S(2)}) collective-permute-start(bf16[4,24,2432]{2,1,0:T(8,128)(2,1)S(1)} %pad_maximum_fusion.refs_0_), channel_id=1, source_target_pairs={{0,8},{8,0},{16,24},{24,16},{1,9},{9,1},{17,25},{25,17},{2,10},{10... | collective-permute-start | bytes 1400840 | tf_op jit(solution)/shard_map/ppermute | solution.py:599
  27.0 12.1 %collective-permute-start.5 = (bf16[4,24,2432]{2,1,0:T(8,128)(2,1)S(1)}, bf16[4,24,2432]{2,1,0:T(8,128)(2,1)S(1)}, u32[]{:S(2)}, u32[]{:S(2)}) collective-permute-start(bf16[4,24,2432]{2,1,0:T(8,128)(2,1)S(1)} %pad_maximum_fusion.refs_0_), channel_id=1, source_target_pairs={{0,16},{8,24},{16,0},{24,8},{1,17},{9,25},{17,1},{25,9},{2,18},{10... | collective-permute-start | bytes 1400840 | tf_op jit(solution)/shard_map/ppermute | solution.py:599
  28.6 25.1 %collective-permute-start.3 = (bf16[4,24,2432]{2,1,0:T(8,128)(2,1)S(1)}, bf16[4,24,2432]{2,1,0:T(8,128)(2,1)S(1)}, u32[]{:S(2)}, u32[]{:S(2)}) collective-permute-start(bf16[4,24,2432]{2,1,0:T(8,128)(2,1)S(1)} %pad_maximum_fusion.refs_0_), channel_id=1, source_target_pairs={{0,24},{8,16},{16,8},{24,0},{1,25},{9,17},{17,9},{25,1},{2,26},{10... | collective-permute-start | bytes 1400840 | tf_op jit(solution)/shard_map/ppermute | solution.py:599
  29.0 24.7 %collective-permute-start.6 = (bf16[4,24,2432]{2,1,0:T(8,128)(2,1)S(1)}, bf16[4,24,2432]{2,1,0:T(8,128)(2,1)}, u32[]{:S(2)}, u32[]{:S(2)}) collective-permute-start(bf16[4,24,2432]{2,1,0:T(8,128)(2,1)S(1)} %pad_maximum_fusion.refs_0_), channel_id=1, source_target_pairs={{0,1},{1,0},{2,3},{3,2},{4,5},{5,4},{6,7},{7,6},{8,9},{9,8},{10,11... | collective-permute-start | bytes 1400840 | tf_op jit(solution)/shard_map/ppermute | solution.py:599
  39.2 14.5 %collective-permute-start.7 = (bf16[4,24,2432]{2,1,0:T(8,128)(2,1)S(1)}, bf16[4,24,2432]{2,1,0:T(8,128)(2,1)}, u32[]{:S(2)}, u32[]{:S(2)}) collective-permute-start(bf16[4,24,2432]{2,1,0:T(8,128)(2,1)S(1)} %collective-permute-done.4.refs_1_), channel_id=1, source_target_pairs={{0,1},{1,0},{2,3},{3,2},{4,5},{5,4},{6,7},{7,6},{8,9},{9,8},{10,11... | collective-permute-start | bytes 1400840 | tf_op jit(solution)/shard_map/ppermute | solution.py:599
  39.2 14.5 %collective-permute-start.8 = (bf16[4,24,2432]{2,1,0:T(8,128)(2,1)S(1)}, bf16[4,24,2432]{2,1,0:T(8,128)(2,1)}, u32[]{:S(2)}, u32[]{:S(2)}) collective-permute-start(bf16[4,24,2432]{2,1,0:T(8,128)(2,1)S(1)} %collective-permute-done.5.refs_2_), channel_id=1, source_target_pairs={{0,1},{1,0},{2,3},{3,2},{4,5},{5,4},{6,7},{7,6},{8,9},{9,8},{10,11... | collective-permute-start | bytes 1400840 | tf_op jit(solution)/shard_map/ppermute | solution.py:599
  268.9 16.4 %collective-permute-start.11 = (bf16[4,24,1536]{2,1,0:T(8,128)(2,1)}, bf16[4,24,1536]{2,1,0:T(8,128)(2,1)S(1)}, u32[]{:S(2)}, u32[]{:S(2)}) collective-permute-start(bf16[4,24,1536]{2,1,0:T(8,128)(2,1)} %get-tuple-element.138), channel_id=1, source_target_pairs={{0,8},{8,0},{16,24},{24,16},{1,9},{9,1},{17,25},{25,17},{2,10},{10... | collective-permute-start | bytes 884744 | tf_op jit(solution)/shard_map/ppermute | solution.py:599
  270.4 14.9 %collective-permute-start.12 = (bf16[4,24,1536]{2,1,0:T(8,128)(2,1)S(1)}, bf16[4,24,1536]{2,1,0:T(8,128)(2,1)S(1)}, u32[]{:S(2)}, u32[]{:S(2)}) collective-permute-start(bf16[4,24,1536]{2,1,0:T(8,128)(2,1)S(1)} %get-tuple-element.139), channel_id=1, source_target_pairs={{0,16},{8,24},{16,0},{24,8},{1,17},{9,25},{17,1},{25,9},{2,18},{10... | collective-permute-start | bytes 884744 | tf_op jit(solution)/shard_map/ppermute | solution.py:599
  270.9 16.3 %collective-permute-start.13 = (bf16[4,24,1536]{2,1,0:T(8,128)(2,1)S(1)}, bf16[4,24,1536]{2,1,0:T(8,128)(2,1)S(1)}, u32[]{:S(2)}, u32[]{:S(2)}) collective-permute-start(bf16[4,24,1536]{2,1,0:T(8,128)(2,1)S(1)} %get-tuple-element.140), channel_id=1, source_target_pairs={{0,24},{8,16},{16,8},{24,0},{1,25},{9,17},{17,9},{25,1},{2,26},{10... | collective-permute-start | bytes 884744 | tf_op jit(solution)/shard_map/ppermute | solution.py:599
  288.0 13.5 %collective-permute-start.14 = (bf16[24,1536]{1,0:T(8,128)(2,1)S(1)}, bf16[24,1536]{1,0:T(8,128)(2,1)S(1)}, u32[]{:S(2)}, u32[]{:S(2)}) collective-permute-start(bf16[24,1536]{1,0:T(8,128)(2,1)S(1)} %get-tuple-element.147), channel_id=1, source_target_pairs={{0,2},{1,3},{2,0},{3,1},{4,6},{5,7},{6,4},{7,5},{8,10},{9,11},{10,... | collective-permute-start | bytes 221192 | tf_op jit(solution)/shard_map/ppermute | solution.py:599
  290.0 11.5 %collective-permute-start.15 = (bf16[24,1536]{1,0:T(8,128)(2,1)S(1)}, bf16[24,1536]{1,0:T(8,128)(2,1)S(1)}, u32[]{:S(2)}, u32[]{:S(2)}) collective-permute-start(bf16[24,1536]{1,0:T(8,128)(2,1)S(1)} %get-tuple-element.148), channel_id=1, source_target_pairs={{0,4},{1,5},{2,6},{3,7},{4,0},{5,1},{6,2},{7,3},{8,12},{9,13},{10,... | collective-permute-start | bytes 221192 | tf_op jit(solution)/shard_map/ppermute | solution.py:599
  292.6 11.8 %collective-permute-start.16 = (bf16[24,1536]{1,0:T(8,128)(2,1)S(1)}, bf16[24,1536]{1,0:T(8,128)(2,1)S(1)}, u32[]{:S(2)}, u32[]{:S(2)}) collective-permute-start(bf16[24,1536]{1,0:T(8,128)(2,1)S(1)} %get-tuple-element.149), channel_id=1, source_target_pairs={{0,6},{1,7},{2,4},{3,5},{4,2},{5,3},{6,0},{7,1},{8,14},{9,15},{10,... | collective-permute-start | bytes 221192 | tf_op jit(solution)/shard_map/ppermute | solution.py:599
  307.6 11.0 %collective-permute-start.18 = (bf16[4,24,1664]{2,1,0:T(8,128)(2,1)S(1)}, bf16[4,24,1664]{2,1,0:T(8,128)(2,1)S(1)}, u32[]{:S(2)}, u32[]{:S(2)}) collective-permute-start(bf16[4,24,1664]{2,1,0:T(8,128)(2,1)S(1)} %get-tuple-element.159), channel_id=1, source_target_pairs={{0,8},{8,0},{16,24},{24,16},{1,9},{9,1},{17,25},{25,17},{2,10},{10... | collective-permute-start | bytes 958472 | tf_op jit(solution)/shard_map/ppermute | solution.py:599
  309.0 18.2 %collective-permute-start.19 = (bf16[4,24,1664]{2,1,0:T(8,128)(2,1)S(1)}, bf16[4,24,1664]{2,1,0:T(8,128)(2,1)S(1)}, u32[]{:S(2)}, u32[]{:S(2)}) collective-permute-start(bf16[4,24,1664]{2,1,0:T(8,128)(2,1)S(1)} %get-tuple-element.160), channel_id=1, source_target_pairs={{0,16},{8,24},{16,0},{24,8},{1,17},{9,25},{17,1},{25,9},{2,18},{10... | collective-permute-start | bytes 958472 | tf_op jit(solution)/shard_map/ppermute | solution.py:599
  309.7 17.6 %collective-permute-start.20 = (bf16[4,24,1664]{2,1,0:T(8,128)(2,1)S(1)}, bf16[4,24,1664]{2,1,0:T(8,128)(2,1)S(1)}, u32[]{:S(2)}, u32[]{:S(2)}) collective-permute-start(bf16[4,24,1664]{2,1,0:T(8,128)(2,1)S(1)} %get-tuple-element.161), channel_id=1, source_target_pairs={{0,24},{8,16},{16,8},{24,0},{1,25},{9,17},{17,9},{25,1},{2,26},{10... | collective-permute-start | bytes 958472 | tf_op jit(solution)/shard_map/ppermute | solution.py:599
  328.1 6.6 %collective-permute-start.21 = (bf16[24,1664]{1,0:T(8,128)(2,1)S(1)}, bf16[24,1664]{1,0:T(8,128)(2,1)S(1)}, u32[]{:S(2)}, u32[]{:S(2)}) collective-permute-start(bf16[24,1664]{1,0:T(8,128)(2,1)S(1)} %get-tuple-element.163), channel_id=1, source_target_pairs={{0,2},{1,3},{2,0},{3,1},{4,6},{5,7},{6,4},{7,5},{8,10},{9,11},{10,... | collective-permute-start | bytes 239624 | tf_op jit(solution)/shard_map/ppermute | solution.py:599
  331.1 9.1 %collective-permute-start.22 = (bf16[24,1664]{1,0:T(8,128)(2,1)S(1)}, bf16[24,1664]{1,0:T(8,128)(2,1)S(1)}, u32[]{:S(2)}, u32[]{:S(2)}) collective-permute-start(bf16[24,1664]{1,0:T(8,128)(2,1)S(1)} %get-tuple-element.164), channel_id=1, source_target_pairs={{0,4},{1,5},{2,6},{3,7},{4,0},{5,1},{6,2},{7,3},{8,12},{9,13},{10,... | collective-permute-start | bytes 239624 | tf_op jit(solution)/shard_map/ppermute | solution.py:599
  332.5 7.8 %collective-permute-start.23 = (bf16[24,1664]{1,0:T(8,128)(2,1)S(1)}, bf16[24,1664]{1,0:T(8,128)(2,1)S(1)}, u32[]{:S(2)}, u32[]{:S(2)}) collective-permute-start(bf16[24,1664]{1,0:T(8,128)(2,1)S(1)} %get-tuple-element.165), channel_id=1, source_target_pairs={{0,6},{1,7},{2,4},{3,5},{4,2},{5,3},{6,0},{7,1},{8,14},{9,15},{10,... | collective-permute-start | bytes 239624 | tf_op jit(solution)/shard_map/ppermute | solution.py:599
  343.2 10.6 %all-to-all-start = ((f32[32,1,128]{2,1,0:T(1,128)}), f32[32,1,128]{2,1,0:T(1,128)S(1)}, u32[]{:S(2)}, u32[]{:S(2)}) async-start(f32[32,1,128]{2,1,0:T(1,128)} %bitcast.42), calls=%async_computation.1 | async-start | bytes 32768 | tf_op jit(solution)/shard_map/all_to_all | solution.py:719
  (17 other events, 196.3 us)
Sparse Core Ops, SparseCore 0:
  11.0 95.4 all-gather.2
  185.2 150.8 reduce-scatter.1

commit v7 on v6

--- a/solution.py
+++ b/solution.py
@@ -278,9 +278,9 @@
     shapes=[(r,WIDE),(9*r,D)]
     whole=lambda s: pl.BlockSpec(s,lambda i:(0,)*len(s))
     return pl.pallas_call(pack_kernel,grid=(1,),
-        in_specs=[whole(v.shape) for v in ins],out_specs=[whole(v) for v in shapes],
+        in_specs=[whole(v.shape) for v in ins],out_specs=[pl.BlockSpec(memory_space=pltpu.VMEM),whole(shapes[1])],
         out_shape=[jax.ShapeDtypeStruct(v,bf) for v in shapes],
-        compiler_params=params(),name="pack_shards")(*ins)
+        compiler_params=pltpu.CompilerParams(vmem_limit_bytes=48<<20),name="pack_shards")(*ins)
 
 
 def qkv_kernel(place_ref,n_ref,*refs):

time: 366 us -> 371 us (1.014)
  local copies, waits for them, and re-layouts: 3.28 us -> 7.68 us
    unnamed x28 -> x38, local copies, waits for them, and re-layouts: 3.28 us -> 7.68 us
  transfers between devices with their start and end apart: 27 -> 27, of which waited for: 13 -> 16; matrix products, arithmetic and copies ran while one was open for 1% -> 0% of each run, Pallas kernels for 45% -> 44%
where the time goes in v7:
time: 371 us; the launch traced here: 370 us
  Pallas kernels  242 us (65%)
  waiting for transfers between devices  69.9 us (19%)
  starting transfers between devices  34.2 us (9%)
  between operations  15 us (4%)
  local copies, waits for them, and re-layouts  7.68 us (2%)
    pallas_call x1, Pallas kernels, attn_bwd(): pl.pallas_call(bwd_kernel, grid=(6,), in_specs=[pl.BlockSpec(memory_space...  73.5 us
    ppermute x24, waiting for transfers between devices, swap(): return lax.ppermute(value, axis, [(i, i ^ flip) for i in range(size)])  63.4 us
    pallas_call x1, Pallas kernels, mlp_block(): pl.pallas_call(mlp_kernel, grid=(rows // BM,), in_specs=[tile(D), pl.Bloc...  50.6 us
    pallas_call x1, Pallas kernels, attn_fwd(): pl.pallas_call(fwd_kernel, grid=(6,), in_specs=[pl.BlockSpec(memory_space...  44.8 us
    ppermute x24, starting transfers between devices, swap(): return lax.ppermute(value, axis, [(i, i ^ flip) for i in range(size)])  30.4 us
    pallas_call x1, Pallas kernels, fc_grads(): pl.pallas_call(fc_kernel, grid=(8,), in_specs=[pl.BlockSpec((rows, D), la...  21.6 us
    pallas_call x2, Pallas kernels, split_grad(): pl.pallas_call(split_kernel, grid=(2,), in_specs=[pl.BlockSpec(memory_spa...  13.3 us
    pallas_call x1, Pallas kernels, input_grad(): pl.pallas_call(input_kernel, grid=(rows // BM,), in_specs=[tile(D), tile(...  12.7 us
  transfers between devices with their start and end apart: 27, of which 16 were waited for; matrix products, arithmetic and copies ran while one was open for 0% of the time, Pallas kernels for 44%

profile of v7, /device:TPU:0, one launch (start us, length us, event | category | flops | bytes accessed | tf_op | source)
XLA Modules:
  0.0 370.4 jit_solution(10238958989295262140)
XLA Ops:
  12.5 3.1 collective-permute-start
  15.6 2.6 collective-permute-start.1
  20.1 7.4 %collective-permute-done.1 = bf16[24,2432]{1,0:T(8,128)(2,1)S(1)} collective-permute-done((bf16[24,2432]{1,0:T(8,128)(2,1)S(1)}, bf16[24,2432]{1,0:T(8,128)(2,1)S(1)}, u32[]{:S(2)}, u32[]{:S(2)}) %collective-permute-start.1) | collective-permute-done | bytes 116768 | tf_op jit(solution)/shard_map/ppermute | solution.py:599
  31.1 10.1 %collective-permute-done.4.refs_1_ = bf16[4,24,2432]{2,1,0:T(8,128)(2,1)S(1)} collective-permute-done((bf16[4,24,2432]{2,1,0:T(8,128)(2,1)S(1)}, bf16[4,24,2432]{2,1,0:T(8,128)(2,1)S(1)}, u32[]{:S(2)}, u32[]{:S(2)}) %collective-permute-start.4) | collective-permute-done | bytes 466976 | tf_op jit(solution)/shard_map/ppermute | solution.py:599
  41.8 5.1 %norm_input.1 = (f32[1536,768]{1,0:T(8,128)}, f32[1536,128]{1,0:T(8,128)}) custom-call(bf16[1536,768]{1,0:T(8,128)(2,1)} %bitcast.35), custom_call_target="tpu_custom_call" | custom-call | flops 1000 | bytes 1000 | tf_op jit(solution)/shard_map/norm_input/pallas_call | solution.py:253
  46.9 8.9 %collective-permute-done.3.refs_3_ = bf16[4,24,2432]{2,1,0:T(8,128)(2,1)S(1)} collective-permute-done((bf16[4,24,2432]{2,1,0:T(8,128)(2,1)S(1)}, bf16[4,24,2432]{2,1,0:T(8,128)(2,1)S(1)}, u32[]{:S(2)}, u32[]{:S(2)}) %collective-permute-start.3) | collective-permute-done | bytes 466976 | tf_op jit(solution)/shard_map/ppermute | solution.py:599
  57.8 12.3 %qkv_forward.1 = (bf16[1536,1536]{1,0:T(8,128)(2,1)}, bf16[1536,2304]{1,0:T(8,128)(2,1)}, f32[16,768]{1,0:T(8,128)}, bf16[4,4,2,24,2432]{4,3,2,1,0:T(8,128)(2,1)}) custom-call(s32[3]{0:T(128)} %pad_add_fusion.place_ref, f32[1536,768]{1,0:T(8,128)} %get-tuple-element.108.n_ref, bf16[4,24,2432]{2,1,0:T(8,128)(2,1)} %copy-done.8, ...), custom_call_target="tpu_custom_call" | custom-call | flops 5435817984 | bytes 18874368 | tf_op jit(solution)/shard_map/qkv_forward/pallas_call | solution.py:317
  70.1 44.8 %attn_fwd.1 = (bf16[1536,1536]{1,0:T(8,128)(2,1)}, f32[6,8,1536]{2,1,0:T(8,128)}) custom-call(s32[1,6]{1,0:T(1,128)} %len_ref.3, bf16[1536,2304]{1,0:T(8,128)(2,1)} %get-tuple-element.116.qkv_ref, bf16[1536,1536]{1,0:T(8,128)(2,1)} %get-tuple-element.117.left_ref), custom_call_target="tpu_custom_call", output_to_operand_aliasing={{0}: (2, {})} | custom-call | flops 7247757312 | bytes 10485760 | tf_op jit(solution)/shard_map/attn_fwd/pallas_call | solution.py:143
  114.9 50.6 %mlp_block.1 = (bf16[1536,768]{1,0:T(8,128)(2,1)}, bf16[1536,768]{1,0:T(8,128)(2,1)}, bf16[1536,768]{1,0:T(8,128)(2,1)}, bf16[1536,3072]{1,0:T(8,128)(2,1)}, bf1...) custom-call(bf16[1536,768]{1,0:T(8,128)(2,1)} %bitcast.36, ...), custom_call_target="tpu_custom_call" | custom-call | flops 32614907904 | bytes 50331648 | tf_op jit(solution)/shard_map/mlp_block/pallas_call | solution.py:406
  165.5 21.6 %fc_grads.1 = bf16[32,192,768]{2,1,0:T(8,128)(2,1)} custom-call(bf16[1536,3072]{1,0:T(8,128)(2,1)} %get-tuple-element.166.z_ref, bf16[1536,768]{1,0:T(8,128)(2,1)} %get-tuple-element.167.dm_ref, bf16[1536,768]{1,0:T(8,128)(2,1)} %get-tuple-element.168.h_ref, bf16[1536,3072]{1,0:T(8,128)(2,1)} %get-tuple-element.169.du_ref), custom_call_target="tpu_custom_call" | custom-call | flops 14495514624 | bytes 37748736 | tf_op jit(solution)/shard_map/fc_grads/pallas_call | solution.py:441
  187.1 73.5 %attn_bwd.1.right_ref.d_ref = bf16[1536,3072]{1,0:T(8,128)(2,1)} custom-call(s32[1,6]{1,0:T(1,128)} %len_ref.3, bf16[1536,2304]{1,0:T(8,128)(2,1)} %get-tuple-element.116.qkv_ref, bf16[1536,1536]{1,0:T(8,128)(2,1)} %get-tuple-element.118.o_ref.left_ref, bf16[1536,768]{1,0:T(8,128)(2,1)} %get-tuple-element.123.do_ref, ...), custom_call_target="tpu_custom_call", output_to_operand_aliasing={{}: (5, {})} | custom-call | flops 18119393280 | bytes 20971520 | tf_op jit(solution)/shard_map/attn_bwd/pallas_call | solution.py:208
  260.6 6.6 %split_grad.2 = (bf16[16,24,1536]{2,1,0:T(8,128)(2,1)S(1)}, bf16[16,24,1536]{2,1,0:T(8,128)(2,1)S(1)}) custom-call(s32[1]{0:T(128)} %bitcast.3.core_ref, bf16[1536,1536]{1,0:T(8,128)(2,1)} %get-tuple-element.118.o_ref.left_ref, bf16[1536,3072]{1,0:T(8,128)(2,1)} %attn_bwd.1.right_ref.d_ref), custom_call_target="tpu_custom_call" | custom-call | flops 1000 | bytes 1000 | tf_op jit(solution)/shard_map/split_grad/pallas_call | solution.py:473
  267.4 2.8 collective-permute-done.10
  274.4 12.7 %input_grad.1 = (bf16[1536,768]{1,0:T(8,128)(2,1)}, f32[16,768]{1,0:T(8,128)}) custom-call(f32[1536,768]{1,0:T(8,128)} %get-tuple-element.108.n_ref, f32[1536,128]{1,0:T(8,128)} %get-tuple-element.122.r_ref, bf16[1536,3072]{1,0:T(8,128)(2,1)} %attn_bwd.1.right_ref.d_ref, f32[1536,768]{1,0:T(8,128)} %get-tuple-element.126.dx1_ref, ...), custom_call_target="tpu_custom_call" | custom-call | flops 1000 | bytes 1000 | tf_op jit(solution)/shard_map/input_grad/pallas_call | solution.py:502
  287.1 4.5 %collective-permute-done.13.refs_3_ = bf16[4,24,1536]{2,1,0:T(8,128)(2,1)S(1)} collective-permute-done((bf16[4,24,1536]{2,1,0:T(8,128)(2,1)S(1)}, bf16[4,24,1536]{2,1,0:T(8,128)(2,1)S(1)}, u32[]{:S(2)}, u32[]{:S(2)}) %collective-permute-start.13) | collective-permute-done | bytes 294944 | tf_op jit(solution)/shard_map/ppermute | solution.py:599
  299.1 6.7 %split_grad.3 = (bf16[16,24,1664]{2,1,0:T(8,128)(2,1)S(1)}, bf16[16,24,1664]{2,1,0:T(8,128)(2,1)S(1)}) custom-call(s32[1]{0:T(128)} %bitcast.3.core_ref, bf16[1536,1536]{1,0:T(8,128)(2,1)} %get-tuple-element.118.o_ref.left_ref, bf16[1536,3072]{1,0:T(8,128)(2,1)} %attn_bwd.1.right_ref.d_ref, f32[16,768]{1,0:T(8,128)S(1)} %copy-done.6), custom_call_target="tpu_custom_call" | custom-call | flops 1000 | bytes 1000 | tf_op jit(solution)/shard_map/split_grad/pallas_call | solution.py:473
  308.4 3.0 collective-permute-done.17
  315.3 6.9 %collective-permute-done.18.refs_1_ = bf16[4,24,1664]{2,1,0:T(8,128)(2,1)S(1)} collective-permute-done((bf16[4,24,1664]{2,1,0:T(8,128)(2,1)S(1)}, bf16[4,24,1664]{2,1,0:T(8,128)(2,1)S(1)}, u32[]{:S(2)}, u32[]{:S(2)}) %collective-permute-start.18) | collective-permute-done | bytes 319520 | tf_op jit(solution)/shard_map/ppermute | solution.py:599
  322.2 8.6 %collective-permute-done.19.refs_2_ = bf16[4,24,1664]{2,1,0:T(8,128)(2,1)S(1)} collective-permute-done((bf16[4,24,1664]{2,1,0:T(8,128)(2,1)S(1)}, bf16[4,24,1664]{2,1,0:T(8,128)(2,1)S(1)}, u32[]{:S(2)}, u32[]{:S(2)}) %collective-permute-start.19) | collective-permute-done | bytes 319520 | tf_op jit(solution)/shard_map/ppermute | solution.py:599
  331.5 5.3 %collective-permute-start.21 = (bf16[24,1664]{1,0:T(8,128)(2,1)S(1)}, bf16[24,1664]{1,0:T(8,128)(2,1)S(1)}, u32[]{:S(2)}, u32[]{:S(2)}) collective-permute-start(bf16[24,1664]{1,0:T(8,128)(2,1)S(1)} %get-tuple-element.163), channel_id=1, source_target_pairs={{0,2},{1,3},{2,0},{3,1},{4,6},{5,7},{6,4},{7,5},{8,10},{9,11},{10,... | collective-permute-start | bytes 239624 | tf_op jit(solution)/shard_map/ppermute | solution.py:599
  342.4 2.9 collective-permute-done.22.refs_6_
  348.3 3.6 all-to-all-start
  352.6 6.4 %all-to-all-done = f32[32,1,128]{2,1,0:T(1,128)S(1)} async-done(((f32[32,1,128]{2,1,0:T(1,128)}), f32[32,1,128]{2,1,0:T(1,128)S(1)}, u32[]{:S(2)}, u32[]{:S(2)}) %all-to-all-start) | async-done | bytes 16416 | tf_op jit(solution)/shard_map/all_to_all | solution.py:719
  359.6 3.9 %adam_all.1 = (f32[1,1]{1,0:T(1,128)}, f32[24,2304]{1,0:T(8,128)}, f32[24,2304]{1,0:T(8,128)}, f32[24,2304]{1,0:T(8,128)}, f32[24,768]{1,0:T(8,128)}, /*index=5*...) custom-call(f32[2]{0:T(128)} %pad_maximum_fusion.1.fix_ref, ...), custom_call_target="tpu_custom_call" | custom-call | tf_op jit(solution)/shard_map/adam_all/pallas_call | solution.py:581
  (89 shorter events, 41.5 us)
Async XLA Ops:
  7.2 107.7 %all-gather.3.cloned.1.call-start = ((), (), s32[]{:S(2)}) async-start(), calls=%async_computation.3 | async-start | bytes 10948608 | tf_op jit(solution)/shard_map/all_gather | solution.py:667
  12.5 332.9 %reduce-scatter.2.cloned.1.call-start = ((), (), s32[]{:S(2)}) async-start(), calls=%async_computation.2 | async-start | bytes 9732096 | tf_op jit(solution)/shard_map/reduce_scatter | solution.py:694
  12.5 7.5 %collective-permute-start = (bf16[24,2432]{1,0:T(8,128)(2,1)S(1)}, bf16[24,2432]{1,0:T(8,128)(2,1)S(1)}, u32[]{:S(2)}, u32[]{:S(2)}) collective-permute-start(bf16[24,2432]{1,0:T(8,128)(2,1)S(1)} %get-tuple-element.105), channel_id=1, source_target_pairs={{0,2},{1,3},{2,0},{3,1},{4,6},{5,7},{6,4},{7,5},{8,10},{9,11},{10,... | collective-permute-start | bytes 350216 | tf_op jit(solution)/shard_map/ppermute | solution.py:599
  15.6 11.9 %collective-permute-start.1 = (bf16[24,2432]{1,0:T(8,128)(2,1)S(1)}, bf16[24,2432]{1,0:T(8,128)(2,1)S(1)}, u32[]{:S(2)}, u32[]{:S(2)}) collective-permute-start(bf16[24,2432]{1,0:T(8,128)(2,1)S(1)} %get-tuple-element.105), channel_id=1, source_target_pairs={{0,4},{1,5},{2,6},{3,7},{4,0},{5,1},{6,2},{7,3},{8,12},{9,13},{10,... | collective-permute-start | bytes 350216 | tf_op jit(solution)/shard_map/ppermute | solution.py:599
  18.2 9.3 %collective-permute-start.2 = (bf16[24,2432]{1,0:T(8,128)(2,1)S(1)}, bf16[24,2432]{1,0:T(8,128)(2,1)S(1)}, u32[]{:S(2)}, u32[]{:S(2)}) collective-permute-start(bf16[24,2432]{1,0:T(8,128)(2,1)S(1)} %get-tuple-element.105), channel_id=1, source_target_pairs={{0,6},{1,7},{2,4},{3,5},{4,2},{5,3},{6,0},{7,1},{8,14},{9,15},{10,... | collective-permute-start | bytes 350216 | tf_op jit(solution)/shard_map/ppermute | solution.py:599
  27.6 13.7 %collective-permute-start.4 = (bf16[4,24,2432]{2,1,0:T(8,128)(2,1)S(1)}, bf16[4,24,2432]{2,1,0:T(8,128)(2,1)S(1)}, u32[]{:S(2)}, u32[]{:S(2)}) collective-permute-start(bf16[4,24,2432]{2,1,0:T(8,128)(2,1)S(1)} %pad_maximum_fusion.refs_0_), channel_id=1, source_target_pairs={{0,8},{8,0},{16,24},{24,16},{1,9},{9,1},{17,25},{25,17},{2,10},{10... | collective-permute-start | bytes 1400840 | tf_op jit(solution)/shard_map/ppermute | solution.py:599
  29.1 12.2 %collective-permute-start.5 = (bf16[4,24,2432]{2,1,0:T(8,128)(2,1)S(1)}, bf16[4,24,2432]{2,1,0:T(8,128)(2,1)S(1)}, u32[]{:S(2)}, u32[]{:S(2)}) collective-permute-start(bf16[4,24,2432]{2,1,0:T(8,128)(2,1)S(1)} %pad_maximum_fusion.refs_0_), channel_id=1, source_target_pairs={{0,16},{8,24},{16,0},{24,8},{1,17},{9,25},{17,1},{25,9},{2,18},{10... | collective-permute-start | bytes 1400840 | tf_op jit(solution)/shard_map/ppermute | solution.py:599
  30.7 25.1 %collective-permute-start.3 = (bf16[4,24,2432]{2,1,0:T(8,128)(2,1)S(1)}, bf16[4,24,2432]{2,1,0:T(8,128)(2,1)S(1)}, u32[]{:S(2)}, u32[]{:S(2)}) collective-permute-start(bf16[4,24,2432]{2,1,0:T(8,128)(2,1)S(1)} %pad_maximum_fusion.refs_0_), channel_id=1, source_target_pairs={{0,24},{8,16},{16,8},{24,0},{1,25},{9,17},{17,9},{25,1},{2,26},{10... | collective-permute-start | bytes 1400840 | tf_op jit(solution)/shard_map/ppermute | solution.py:599
  31.1 24.6 %collective-permute-start.6 = (bf16[4,24,2432]{2,1,0:T(8,128)(2,1)S(1)}, bf16[4,24,2432]{2,1,0:T(8,128)(2,1)}, u32[]{:S(2)}, u32[]{:S(2)}) collective-permute-start(bf16[4,24,2432]{2,1,0:T(8,128)(2,1)S(1)} %pad_maximum_fusion.refs_0_), channel_id=1, source_target_pairs={{0,1},{1,0},{2,3},{3,2},{4,5},{5,4},{6,7},{7,6},{8,9},{9,8},{10,11... | collective-permute-start | bytes 1400840 | tf_op jit(solution)/shard_map/ppermute | solution.py:599
  41.3 14.5 %collective-permute-start.7 = (bf16[4,24,2432]{2,1,0:T(8,128)(2,1)S(1)}, bf16[4,24,2432]{2,1,0:T(8,128)(2,1)}, u32[]{:S(2)}, u32[]{:S(2)}) collective-permute-start(bf16[4,24,2432]{2,1,0:T(8,128)(2,1)S(1)} %collective-permute-done.4.refs_1_), channel_id=1, source_target_pairs={{0,1},{1,0},{2,3},{3,2},{4,5},{5,4},{6,7},{7,6},{8,9},{9,8},{10,11... | collective-permute-start | bytes 1400840 | tf_op jit(solution)/shard_map/ppermute | solution.py:599
  41.3 14.4 %collective-permute-start.8 = (bf16[4,24,2432]{2,1,0:T(8,128)(2,1)S(1)}, bf16[4,24,2432]{2,1,0:T(8,128)(2,1)}, u32[]{:S(2)}, u32[]{:S(2)}) collective-permute-start(bf16[4,24,2432]{2,1,0:T(8,128)(2,1)S(1)} %collective-permute-done.5.refs_2_), channel_id=1, source_target_pairs={{0,1},{1,0},{2,3},{3,2},{4,5},{5,4},{6,7},{7,6},{8,9},{9,8},{10,11... | collective-permute-start | bytes 1400840 | tf_op jit(solution)/shard_map/ppermute | solution.py:599
  270.9 16.2 %collective-permute-start.11 = (bf16[4,24,1536]{2,1,0:T(8,128)(2,1)}, bf16[4,24,1536]{2,1,0:T(8,128)(2,1)S(1)}, u32[]{:S(2)}, u32[]{:S(2)}) collective-permute-start(bf16[4,24,1536]{2,1,0:T(8,128)(2,1)} %get-tuple-element.138), channel_id=1, source_target_pairs={{0,8},{8,0},{16,24},{24,16},{1,9},{9,1},{17,25},{25,17},{2,10},{10... | collective-permute-start | bytes 884744 | tf_op jit(solution)/shard_map/ppermute | solution.py:599
  272.5 14.7 %collective-permute-start.12 = (bf16[4,24,1536]{2,1,0:T(8,128)(2,1)S(1)}, bf16[4,24,1536]{2,1,0:T(8,128)(2,1)S(1)}, u32[]{:S(2)}, u32[]{:S(2)}) collective-permute-start(bf16[4,24,1536]{2,1,0:T(8,128)(2,1)S(1)} %get-tuple-element.139), channel_id=1, source_target_pairs={{0,16},{8,24},{16,0},{24,8},{1,17},{9,25},{17,1},{25,9},{2,18},{10... | collective-permute-start | bytes 884744 | tf_op jit(solution)/shard_map/ppermute | solution.py:599
  272.9 18.8 %collective-permute-start.13 = (bf16[4,24,1536]{2,1,0:T(8,128)(2,1)S(1)}, bf16[4,24,1536]{2,1,0:T(8,128)(2,1)S(1)}, u32[]{:S(2)}, u32[]{:S(2)}) collective-permute-start(bf16[4,24,1536]{2,1,0:T(8,128)(2,1)S(1)} %get-tuple-element.140), channel_id=1, source_target_pairs={{0,24},{8,16},{16,8},{24,0},{1,25},{9,17},{17,9},{25,1},{2,26},{10... | collective-permute-start | bytes 884744 | tf_op jit(solution)/shard_map/ppermute | solution.py:599
  292.5 13.3 %collective-permute-start.14 = (bf16[24,1536]{1,0:T(8,128)(2,1)S(1)}, bf16[24,1536]{1,0:T(8,128)(2,1)S(1)}, u32[]{:S(2)}, u32[]{:S(2)}) collective-permute-start(bf16[24,1536]{1,0:T(8,128)(2,1)S(1)} %get-tuple-element.147), channel_id=1, source_target_pairs={{0,2},{1,3},{2,0},{3,1},{4,6},{5,7},{6,4},{7,5},{8,10},{9,11},{10,... | collective-permute-start | bytes 221192 | tf_op jit(solution)/shard_map/ppermute | solution.py:599
  294.8 12.4 %collective-permute-start.15 = (bf16[24,1536]{1,0:T(8,128)(2,1)S(1)}, bf16[24,1536]{1,0:T(8,128)(2,1)S(1)}, u32[]{:S(2)}, u32[]{:S(2)}) collective-permute-start(bf16[24,1536]{1,0:T(8,128)(2,1)S(1)} %get-tuple-element.148), channel_id=1, source_target_pairs={{0,4},{1,5},{2,6},{3,7},{4,0},{5,1},{6,2},{7,3},{8,12},{9,13},{10,... | collective-permute-start | bytes 221192 | tf_op jit(solution)/shard_map/ppermute | solution.py:599
  296.8 11.6 %collective-permute-start.16 = (bf16[24,1536]{1,0:T(8,128)(2,1)S(1)}, bf16[24,1536]{1,0:T(8,128)(2,1)S(1)}, u32[]{:S(2)}, u32[]{:S(2)}) collective-permute-start(bf16[24,1536]{1,0:T(8,128)(2,1)S(1)} %get-tuple-element.149), channel_id=1, source_target_pairs={{0,6},{1,7},{2,4},{3,5},{4,2},{5,3},{6,0},{7,1},{8,14},{9,15},{10,... | collective-permute-start | bytes 221192 | tf_op jit(solution)/shard_map/ppermute | solution.py:599
  311.7 10.4 %collective-permute-start.18 = (bf16[4,24,1664]{2,1,0:T(8,128)(2,1)S(1)}, bf16[4,24,1664]{2,1,0:T(8,128)(2,1)S(1)}, u32[]{:S(2)}, u32[]{:S(2)}) collective-permute-start(bf16[4,24,1664]{2,1,0:T(8,128)(2,1)S(1)} %get-tuple-element.159), channel_id=1, source_target_pairs={{0,8},{8,0},{16,24},{24,16},{1,9},{9,1},{17,25},{25,17},{2,10},{10... | collective-permute-start | bytes 958472 | tf_op jit(solution)/shard_map/ppermute | solution.py:599
  312.9 17.8 %collective-permute-start.19 = (bf16[4,24,1664]{2,1,0:T(8,128)(2,1)S(1)}, bf16[4,24,1664]{2,1,0:T(8,128)(2,1)S(1)}, u32[]{:S(2)}, u32[]{:S(2)}) collective-permute-start(bf16[4,24,1664]{2,1,0:T(8,128)(2,1)S(1)} %get-tuple-element.160), channel_id=1, source_target_pairs={{0,16},{8,24},{16,0},{24,8},{1,17},{9,25},{17,1},{25,9},{2,18},{10... | collective-permute-start | bytes 958472 | tf_op jit(solution)/shard_map/ppermute | solution.py:599
  313.2 17.5 %collective-permute-start.20 = (bf16[4,24,1664]{2,1,0:T(8,128)(2,1)S(1)}, bf16[4,24,1664]{2,1,0:T(8,128)(2,1)S(1)}, u32[]{:S(2)}, u32[]{:S(2)}) collective-permute-start(bf16[4,24,1664]{2,1,0:T(8,128)(2,1)S(1)} %get-tuple-element.161), channel_id=1, source_target_pairs={{0,24},{8,16},{16,8},{24,0},{1,25},{9,17},{17,9},{25,1},{2,26},{10... | collective-permute-start | bytes 958472 | tf_op jit(solution)/shard_map/ppermute | solution.py:599
  331.5 10.9 %collective-permute-start.21 = (bf16[24,1664]{1,0:T(8,128)(2,1)S(1)}, bf16[24,1664]{1,0:T(8,128)(2,1)S(1)}, u32[]{:S(2)}, u32[]{:S(2)}) collective-permute-start(bf16[24,1664]{1,0:T(8,128)(2,1)S(1)} %get-tuple-element.163), channel_id=1, source_target_pairs={{0,2},{1,3},{2,0},{3,1},{4,6},{5,7},{6,4},{7,5},{8,10},{9,11},{10,... | collective-permute-start | bytes 239624 | tf_op jit(solution)/shard_map/ppermute | solution.py:599
  336.8 8.5 %collective-permute-start.22 = (bf16[24,1664]{1,0:T(8,128)(2,1)S(1)}, bf16[24,1664]{1,0:T(8,128)(2,1)S(1)}, u32[]{:S(2)}, u32[]{:S(2)}) collective-permute-start(bf16[24,1664]{1,0:T(8,128)(2,1)S(1)} %get-tuple-element.164), channel_id=1, source_target_pairs={{0,4},{1,5},{2,6},{3,7},{4,0},{5,1},{6,2},{7,3},{8,12},{9,13},{10,... | collective-permute-start | bytes 239624 | tf_op jit(solution)/shard_map/ppermute | solution.py:599
  337.6 7.7 %collective-permute-start.23 = (bf16[24,1664]{1,0:T(8,128)(2,1)S(1)}, bf16[24,1664]{1,0:T(8,128)(2,1)S(1)}, u32[]{:S(2)}, u32[]{:S(2)}) collective-permute-start(bf16[24,1664]{1,0:T(8,128)(2,1)S(1)} %get-tuple-element.165), channel_id=1, source_target_pairs={{0,6},{1,7},{2,4},{3,5},{4,2},{5,3},{6,0},{7,1},{8,14},{9,15},{10,... | collective-permute-start | bytes 239624 | tf_op jit(solution)/shard_map/ppermute | solution.py:599
  348.3 10.7 %all-to-all-start = ((f32[32,1,128]{2,1,0:T(1,128)}), f32[32,1,128]{2,1,0:T(1,128)S(1)}, u32[]{:S(2)}, u32[]{:S(2)}) async-start(f32[32,1,128]{2,1,0:T(1,128)} %bitcast.42), calls=%async_computation.1 | async-start | bytes 32768 | tf_op jit(solution)/shard_map/all_to_all | solution.py:719
  (22 other events, 199.3 us)
Sparse Core Ops, SparseCore 0:
  12.6 96.5 all-gather.2
  187.3 158.0 reduce-scatter.1
